TPU v7x, 32 devices: a whole 2x2x4 slice. The times are simulated.
32 devices in a mesh: dp: 32 (over z, y, x, core).
Axes of the slice: x: 2, y: 2, z: 4, core: 2. Of those that a mesh axis runs over, the one named last changes fastest.
Arguments:
- tokens: bfloat16 [8192, 1024], P('dp'), may hold values from -6 to 6
- cotangent: bfloat16 [8192, 1024], P('dp'), may hold values from -6 to 6
- destination: int32 [8192], replicated, may hold values from 0 to 8191, as said below
- lengths: int32 [32, 4], P('dp'), may hold values from 1 to 192, 256 in all within a row
- norm_gains: bfloat16 [2, 2, 1024], P(None, None, 'dp'), may hold values from 0.5 to 1.5
- in_proj: bfloat16 [2, 1024, 3352], P(None, 'dp'), may hold values from -0.1875 to 0.1875
- conv_weight: bfloat16 [2, 4, 1792], P(None, None, 'dp'), may hold values from -3 to 3
- ssm_gain: bfloat16 [2, 1536], P(None, 'dp'), may hold values from 0.5 to 1.5
- mixer_out: bfloat16 [2, 1536, 1024], P(None, 'dp'), may hold values from -0.15625 to 0.15625
- qkv_proj: bfloat16 [2, 1024, 768], P(None, 'dp'), may hold values from -0.1875 to 0.1875
- attn_out: bfloat16 [2, 512, 1024], P(None, 'dp'), may hold values from -1 to 1
- gate_up: bfloat16 [2, 1024, 4096], P(None, 'dp'), may hold values from -0.1875 to 0.1875
- down_proj: bfloat16 [2, 2048, 1024], P(None, 'dp'), may hold values from -0.125 to 0.125
- a_log: float32 [2, 24], replicated, may hold values from 0 to 2.5
- d_skip: float32 [2, 24], replicated, may hold values from 0.5 to 1.5
- dt_bias: float32 [2, 24], replicated, may hold values from -6 to -2
Outputs:
- out_tokens: bfloat16 [8192, 1024], P('dp')
- in_grad: float32 [8192, 1024], P('dp')
- grad_norm_gains: float32 [2, 2, 1024], P(None, None, 'dp')
- grad_in_proj: float32 [2, 1024, 3352], P(None, 'dp')
- grad_conv_weight: float32 [2, 4, 1792], P(None, None, 'dp')
- grad_ssm_gain: float32 [2, 1536], P(None, 'dp')
- grad_mixer_out: float32 [2, 1536, 1024], P(None, 'dp')
- grad_qkv_proj: float32 [2, 1024, 768], P(None, 'dp')
- grad_attn_out: float32 [2, 512, 1024], P(None, 'dp')
- grad_gate_up: float32 [2, 1024, 4096], P(None, 'dp')
- grad_down_proj: float32 [2, 2048, 1024], P(None, 'dp')
- grad_a_log: float32 [2, 24], replicated
- grad_d_skip: float32 [2, 24], replicated
- grad_dt_bias: float32 [2, 24], replicated
Inputs may be any that keep to these rules, and one draw needn't show every extreme that they name: `destination`: A permutation of the dealt rows; the 256 rows that arrive on each device are dealt in equal numbers to every device. Each device's 4 lengths add up to 256, and the longest of them is exactly 192.
All inputs are finite; a program needn't handle non-finite values.
Results may differ from a plain program's by a relative error of at most 0.023.
Values may be sent and summed in bfloat16 or wider, within the bound.
A program may use at most 320 MiB of HBM per device.

v0:
```python
import jax
import jax.numpy as jnp
from jax import lax
from jax.sharding import PartitionSpec as P

FF = 2048
HEADS = 24
HDIM = 64
STATE = 128
QH = 8
KVH = 2
HD = 64
LAYERS = 2
SCAN_BLOCK = 128
INNER = 1536
CONVCH = 1792


EPSILON = 1e-05
ROPE_BASE = 100000000000.0
SCORE_SCALE = 0.125
HIGHEST = lax.Precision.HIGHEST
PLAIN = lax.Precision.DEFAULT


def lower_value(v):
    return lax.optimization_barrier(v.astype(jnp.bfloat16)).astype(jnp.float32)


def passing_value(v):
    return v


def rounder_keep(v):
    return (lower_value(v), None)


def rounder_pass(kept, grad):
    return (grad,)


def plain_keep(v):
    return (v, None)


def plain_lower(kept, grad):
    return (lower_value(grad),)


def make_rounders():
    value_round = jax.custom_vjp(lower_value)
    value_round.defvjp(rounder_keep, rounder_pass)
    grad_round = jax.custom_vjp(passing_value)
    grad_round.defvjp(plain_keep, plain_lower)
    return (value_round, grad_round)


def project(left, right, precise):
    return jnp.dot(left, right, preferred_element_type=jnp.float32, precision=precise)


def rms_norm(values, gain):
    return values * lax.rsqrt(jnp.mean(values * values, axis=-1, keepdims=True) + EPSILON) * gain


def doc_layout(doc_lengths, rows_count):
    rows_index = jnp.arange(rows_count, dtype=jnp.int32)
    doc_ends = jnp.cumsum(doc_lengths, dtype=jnp.int32)
    segment = jnp.sum(
        (rows_index[:, None] >= doc_ends[None, :]).astype(jnp.int32), axis=1, dtype=jnp.int32
    )
    doc_starts = doc_ends - doc_lengths
    member = (
        segment[:, None] == jnp.arange(doc_lengths.shape[0], dtype=jnp.int32)[None, :]
    ).astype(jnp.int32)
    position = rows_index - jnp.sum(member * doc_starts[None, :], axis=1, dtype=jnp.int32)
    return (segment, position)


def causal_conv(channels, kernel, position):
    taps = kernel.shape[0]
    summed = channels * kernel[taps - 1]
    for offset in range(1, taps):
        shifted = jnp.pad(channels, ((offset, 0), (0, 0)))[: channels.shape[0]]
        valid = (position >= offset).astype(channels.dtype)
        summed = summed + shifted * kernel[taps - 1 - offset] * valid[:, None]
    return summed


def rotate(values, position):
    half_dim = values.shape[-1] // 2
    inverse = ROPE_BASE ** (-(jnp.arange(half_dim, dtype=jnp.float32) * 2.0 / values.shape[-1]))
    angles = position.astype(jnp.float32)[:, None] * inverse[None, :]
    target = (values.shape[0],) + (1,) * (values.ndim - 2) + (half_dim,)
    cosine = jnp.cos(angles).reshape(target)
    sine = jnp.sin(angles).reshape(target)
    front = values[..., :half_dim]
    rear = values[..., half_dim:]
    return jnp.concatenate([front * cosine - rear * sine, rear * cosine + front * sine], axis=-1)


def block_step(carry, inputs):
    state, last_segment = carry
    x_part, b_part, c_part, dt_part, decay_log, seg_part = inputs
    cumul = jnp.cumsum(decay_log, axis=0)
    block_len = seg_part.shape[0]
    rows_index = jnp.arange(block_len, dtype=jnp.int32)
    inside = (seg_part[:, None] == seg_part[None, :]) & (rows_index[:, None] >= rows_index[None, :])
    gaps = cumul[:, None, :] - cumul[None, :, :]
    decay = jnp.exp(jnp.minimum(gaps, 0.0)) * inside[:, :, None].astype(cumul.dtype)
    affinity = project(c_part, b_part.T, HIGHEST)
    scaled = x_part * dt_part[:, :, None]
    within = jnp.einsum("ijh,jhp->ihp", decay * affinity[:, :, None], scaled, precision=HIGHEST)
    enters = (seg_part == last_segment).astype(cumul.dtype)
    from_state = jnp.einsum("in,hpn->ihp", c_part, state, precision=HIGHEST)
    carried = from_state * (jnp.exp(cumul) * enters[:, None])[:, :, None]
    final_segment = seg_part[block_len - 1]
    same_final = (seg_part == final_segment).astype(cumul.dtype)
    toward = jnp.exp(cumul[block_len - 1][None, :] - cumul) * same_final[:, None]
    fresh = jnp.einsum("jh,jhp,jn->hpn", toward, scaled, b_part, precision=HIGHEST)
    retain = jnp.exp(cumul[block_len - 1]) * (final_segment == last_segment).astype(cumul.dtype)
    new_state = state * retain[:, None, None] + fresh
    return ((new_state, final_segment), within + carried)


def state_space(x_heads, b_all, c_all, dt_all, rates, segment):
    rows_count = x_heads.shape[0]
    blocks = rows_count // SCAN_BLOCK

    def split_rows(values):
        return values.reshape((blocks, SCAN_BLOCK) + values.shape[1:])

    start = (jnp.zeros((HEADS, HDIM, STATE), jnp.float32), jnp.array(-1, dtype=jnp.int32))
    decay_log = dt_all * rates[None, :]
    inputs = (
        split_rows(x_heads),
        split_rows(b_all),
        split_rows(c_all),
        split_rows(dt_all),
        split_rows(decay_log),
        split_rows(segment),
    )
    _, outputs = lax.scan(jax.checkpoint(block_step), start, inputs)
    return outputs.reshape(rows_count, HEADS, HDIM)


def attention(normed, w_qkv, w_attn, segment, position, precise, rounders):
    value_round, grad_round = rounders
    rows_count = normed.shape[0]
    packed = grad_round(project(normed, w_qkv, precise))
    queries = packed[:, : QH * HD].reshape(rows_count, KVH, QH // KVH, HD)
    key_heads = packed[:, QH * HD : (QH + KVH) * HD].reshape(rows_count, KVH, HD)
    value_heads = value_round(packed[:, (QH + KVH) * HD :].reshape(rows_count, KVH, HD))
    queries = value_round(rotate(queries, position))
    key_heads = value_round(rotate(key_heads, position))
    raw_scores = jnp.einsum("skgd,tkd->kgst", queries, key_heads, precision=precise)
    scores = grad_round(raw_scores) * SCORE_SCALE
    rows_index = jnp.arange(rows_count, dtype=jnp.int32)
    allowed = (segment[:, None] == segment[None, :]) & (rows_index[:, None] >= rows_index[None, :])
    scores = jnp.where(allowed[None, None, :, :], scores, -1e30)
    largest = jnp.max(scores, axis=-1, keepdims=True)
    expo = jnp.exp(scores - largest)
    probs = value_round(expo / jnp.sum(expo, axis=-1, keepdims=True))
    context = jnp.einsum("kgst,tkd->skgd", probs, value_heads, precision=precise)
    context = value_round(grad_round(context.reshape(rows_count, QH * HD)))
    return grad_round(project(context, w_attn, precise))


def hybrid_layer(hidden, segment, position, weights, head_params, precise, rounders):
    value_round, grad_round = rounders
    gains, w_in, kernel, gain_inner, w_mix, w_qkv, w_attn, w_gate_up, w_down = weights
    log_rates, skip_coef, step_bias = head_params
    rows_count = hidden.shape[0]
    normed = value_round(rms_norm(hidden, gains[0]))
    inner = grad_round(project(normed, w_in, precise))
    gate_z = inner[:, :INNER]
    conv_in = inner[:, INNER : INNER + CONVCH]
    step_raw = inner[:, INNER + CONVCH :]
    conv_out = jax.nn.silu(causal_conv(conv_in, kernel, position))
    x_heads = conv_out[:, :INNER].reshape(rows_count, HEADS, HDIM)
    b_all = conv_out[:, INNER : INNER + STATE]
    c_all = conv_out[:, INNER + STATE :]
    dt_all = jax.nn.softplus(step_raw + step_bias[None, :])
    rates = -jnp.exp(log_rates)
    scanned = (
        state_space(x_heads, b_all, c_all, dt_all, rates, segment)
        + skip_coef[None, :, None] * x_heads
    )
    gated = scanned.reshape(rows_count, INNER) * jax.nn.silu(gate_z)
    mixed = value_round(rms_norm(gated, gain_inner))
    mamba_branch = grad_round(project(mixed, w_mix, precise))
    attn_branch = attention(normed, w_qkv, w_attn, segment, position, precise, rounders)
    middle = hidden + mamba_branch + attn_branch
    normed_two = value_round(rms_norm(middle, gains[1]))
    gate_values = grad_round(project(normed_two, w_gate_up, precise))
    activated = value_round(jax.nn.silu(gate_values[:, :FF]) * gate_values[:, FF:])
    return middle + grad_round(project(activated, w_down, precise))


def shards(
    tokens,
    cotangent,
    destination,
    lengths,
    norm_gains,
    in_proj,
    conv_weight,
    ssm_gain,
    mixer_out,
    qkv_proj,
    attn_out,
    gate_up,
    down_proj,
    a_log,
    d_skip,
    dt_bias,
):
    rounders = make_rounders()
    devices = lax.axis_size("dp")
    myself = lax.axis_index("dp")
    rows_here = tokens.shape[0]
    share = rows_here // devices
    model_width = tokens.shape[1]
    slabs = destination.reshape(devices, rows_here)
    local_rows = jnp.arange(rows_here, dtype=jnp.int32)
    own_slab = lax.dynamic_slice_in_dim(slabs, myself, 1, 0)[0]
    order = jnp.argsort(own_slab // rows_here * rows_here + local_rows)
    outgoing_rows = tokens[order].reshape(devices, share, model_width)
    outgoing_cot = cotangent[order].reshape(devices, share, model_width)
    arrived = (
        lax.all_to_all(outgoing_rows, "dp", split_axis=0, concat_axis=0, tiled=True),
        lax.all_to_all(outgoing_cot, "dp", split_axis=0, concat_axis=0, tiled=True),
    )
    ranking = jnp.where(
        slabs // rows_here == myself, local_rows[None, :], rows_here + local_rows[None, :]
    )
    chosen = jnp.argsort(ranking, axis=1)[:, :share]
    places = (jnp.take_along_axis(slabs, chosen, axis=1) % rows_here).reshape(-1)
    hidden = (
        jnp.zeros((rows_here, model_width), jnp.float32)
        .at[places]
        .set(arrived[0].reshape(-1, model_width).astype(jnp.float32))
    )
    upstream = (
        jnp.zeros((rows_here, model_width), jnp.float32)
        .at[places]
        .set(arrived[1].reshape(-1, model_width).astype(jnp.float32))
    )
    segment, position = doc_layout(lengths[0], rows_here)

    def gather_layer(layer_idx):
        pieces = (
            lax.all_gather(norm_gains[layer_idx], "dp", axis=1, tiled=True),
            lax.all_gather(in_proj[layer_idx], "dp", axis=0, tiled=True),
            lax.all_gather(conv_weight[layer_idx], "dp", axis=1, tiled=True),
            lax.all_gather(ssm_gain[layer_idx], "dp", axis=0, tiled=True),
            lax.all_gather(mixer_out[layer_idx], "dp", axis=0, tiled=True),
            lax.all_gather(qkv_proj[layer_idx], "dp", axis=0, tiled=True),
            lax.all_gather(attn_out[layer_idx], "dp", axis=0, tiled=True),
            lax.all_gather(gate_up[layer_idx], "dp", axis=0, tiled=True),
            lax.all_gather(down_proj[layer_idx], "dp", axis=0, tiled=True),
        )
        return tuple((piece.astype(jnp.float32) for piece in pieces))

    def gather_layer_again(layer_idx):
        pieces = (
            lax.all_gather(norm_gains[layer_idx], "dp", axis=1, tiled=True),
            lax.all_gather(in_proj[layer_idx], "dp", axis=0, tiled=True),
            lax.all_gather(conv_weight[layer_idx], "dp", axis=1, tiled=True),
            lax.all_gather(ssm_gain[layer_idx], "dp", axis=0, tiled=True),
            lax.all_gather(mixer_out[layer_idx], "dp", axis=0, tiled=True),
            lax.all_gather(qkv_proj[layer_idx], "dp", axis=0, tiled=True),
            lax.all_gather(attn_out[layer_idx], "dp", axis=0, tiled=True),
            lax.all_gather(gate_up[layer_idx], "dp", axis=0, tiled=True),
            lax.all_gather(down_proj[layer_idx], "dp", axis=0, tiled=True),
        )
        return tuple((piece.astype(jnp.float32) for piece in pieces))

    def heads_of(layer_idx):
        return (a_log[layer_idx], d_skip[layer_idx], dt_bias[layer_idx])

    def layer_step(layer_input, weights, head_params):
        return hybrid_layer(layer_input, segment, position, weights, head_params, PLAIN, rounders)

    inputs_kept = []
    for layer_idx in range(LAYERS):
        weights = gather_layer(layer_idx)
        inputs_kept.append(hidden)
        hidden = layer_step(hidden, weights, heads_of(layer_idx))
    leaving = hidden.astype(jnp.bfloat16)[places].reshape(devices, share, model_width)
    returned = lax.all_to_all(leaving, "dp", split_axis=0, concat_axis=0, tiled=True)
    out_tokens = (
        jnp.zeros((rows_here, model_width), jnp.bfloat16)
        .at[order]
        .set(returned.reshape(-1, model_width))
    )
    flowing = upstream
    owned_parts = [None] * LAYERS
    head_parts = [None] * LAYERS
    for layer_idx in reversed(range(LAYERS)):
        weights = gather_layer_again(layer_idx)
        _, puller = jax.vjp(layer_step, inputs_kept[layer_idx], weights, heads_of(layer_idx))
        flowing, weight_terms, head_terms = puller(flowing)
        owned_parts[layer_idx] = (
            lax.psum_scatter(weight_terms[0], "dp", scatter_dimension=1, tiled=True),
            lax.psum_scatter(weight_terms[1], "dp", scatter_dimension=0, tiled=True),
            lax.psum_scatter(weight_terms[2], "dp", scatter_dimension=1, tiled=True),
            lax.psum_scatter(weight_terms[3], "dp", scatter_dimension=0, tiled=True),
            lax.psum_scatter(weight_terms[4], "dp", scatter_dimension=0, tiled=True),
            lax.psum_scatter(weight_terms[5], "dp", scatter_dimension=0, tiled=True),
            lax.psum_scatter(weight_terms[6], "dp", scatter_dimension=0, tiled=True),
            lax.psum_scatter(weight_terms[7], "dp", scatter_dimension=0, tiled=True),
            lax.psum_scatter(weight_terms[8], "dp", scatter_dimension=0, tiled=True),
        )
        head_parts[layer_idx] = head_terms
    stacked = tuple(
        (
            jnp.stack([owned_parts[layer_idx][member] for layer_idx in range(LAYERS)])
            for member in range(9)
        )
    )
    head_local = tuple(
        (
            jnp.stack([head_parts[layer_idx][member] for layer_idx in range(LAYERS)])
            for member in range(3)
        )
    )
    head_total = lax.psum((head_local[0], head_local[1], head_local[2]), "dp")
    sending_back = flowing[places].reshape(devices, share, model_width)
    grads_home = lax.all_to_all(
        sending_back.astype(jnp.bfloat16), "dp", split_axis=0, concat_axis=0, tiled=True
    ).astype(sending_back.dtype)
    in_grad = (
        jnp.zeros((rows_here, model_width), jnp.float32)
        .at[order]
        .set(grads_home.reshape(-1, model_width))
    )
    return (
        out_tokens,
        in_grad,
        stacked[0],
        stacked[1],
        stacked[2],
        stacked[3],
        stacked[4],
        stacked[5],
        stacked[6],
        stacked[7],
        stacked[8],
        head_total[0],
        head_total[1],
        head_total[2],
    )


def solution(mesh):
    placed = (
        P("dp", None),
        P("dp", None),
        P(),
        P("dp", None),
        P(None, None, "dp"),
        P(None, "dp", None),
        P(None, None, "dp"),
        P(None, "dp"),
        P(None, "dp", None),
        P(None, "dp", None),
        P(None, "dp", None),
        P(None, "dp", None),
        P(None, "dp", None),
        P(),
        P(),
        P(),
    )
    return jax.shard_map(
        shards,
        mesh=mesh,
        in_specs=placed,
        out_specs=(
            P("dp", None),
            P("dp", None),
            P(None, None, "dp"),
            P(None, "dp", None),
            P(None, None, "dp"),
            P(None, "dp"),
            P(None, "dp", None),
            P(None, "dp", None),
            P(None, "dp", None),
            P(None, "dp", None),
            P(None, "dp", None),
            P(),
            P(),
            P(),
        ),
        check_vma=False,
    )
```

profile of v0, /device:TPU:0, one launch (start us, length us, event | category | flops | bytes accessed | tf_op | source)
XLA Modules:
  0.0 3358.5 jit_solution(10042987860029685411)
XLA Ops:
  37.5 43.4 %all-gather = bf16[1,2,1024]{1,0,2:T(2,128)(2,1)S(1)} all-gather(bf16[1,2,32]{1,0,2:T(2,128)(2,1)S(1)} %copy.570), channel_id=2, replica_groups=mesh['dp'=32] {'dp'}, dimensions={2}, use_global_device_ids=true | all-gather | bytes 4224 | tf_op jit(solution)/shard_map/all_gather | solution.py:253
  87.7 39.9 %all-gather.2 = bf16[1,4,1792]{1,0,2:T(2,128)(2,1)S(1)} all-gather(bf16[1,4,56]{1,0,2:T(2,128)(2,1)S(1)} %copy.571), channel_id=4, replica_groups=mesh['dp'=32] {'dp'}, dimensions={2}, use_global_device_ids=true | all-gather | bytes 14784 | tf_op jit(solution)/shard_map/all_gather | solution.py:255
  128.6 38.3 %slice_reduce_fusion.7 = (f32[1792]{0:T(1024)}, f32[1792]{0:T(1024)S(1)}, f32[1792]{0:T(1024)S(1)}, f32[1792]{0:T(1024)}) fusion(f32[1,4,1792]{1,0,2:T(1,128)S(1)} %convert_element_type.571), kind=kLoop, calls=%fused_computation.606 | loop fusion | bytes 57344 | tf_op jit(solution)/shard_map/slice | solution.py:82
  168.4 40.1 %all-reduce.65 = (bf16[1536]{0:T(1024)(128)(2,1)S(1)}, bf16[1536]{0:T(1024)(128)(2,1)S(1)}) all-reduce(bf16[1536]{0:T(1024)(128)(2,1)S(1)} %dynamic-update-slice, bf16[1536]{0:T(1024)(128)(2,1)S(1)} %dynamic-update-slice.1), channel_id=5, replica_groups=mesh['dp'=32] {'dp'}, use_global_device_ids=true, to_apply=%add.58 | all-reduce | flops 3072 | bytes 12288
  208.6 42.1 %all-gather.9 = bf16[1,2,1024]{1,0,2:T(2,128)(2,1)S(1)} all-gather(bf16[1,2,32]{1,0,2:T(2,128)(2,1)S(1)} %copy.572), channel_id=11, replica_groups=mesh['dp'=32] {'dp'}, dimensions={2}, use_global_device_ids=true | all-gather | bytes 4224 | tf_op jit(solution)/shard_map/all_gather | solution.py:253
  252.2 40.4 %all-gather.11 = bf16[1,4,1792]{1,0,2:T(2,128)(2,1)S(1)} all-gather(bf16[1,4,56]{1,0,2:T(2,128)(2,1)S(1)} %copy.573), channel_id=13, replica_groups=mesh['dp'=32] {'dp'}, dimensions={2}, use_global_device_ids=true | all-gather | bytes 14784 | tf_op jit(solution)/shard_map/all_gather | solution.py:255
  303.7 38.3 %slice_reduce_fusion.3 = (f32[1792]{0:T(1024)}, f32[1792]{0:T(1024)}, f32[1792]{0:T(1024)}, f32[1792]{0:T(1024)}) fusion(f32[1,4,1792]{1,0,2:T(1,128)S(1)} %convert_element_type.574), kind=kLoop, calls=%fused_computation.602 | loop fusion | bytes 57344 | tf_op jit(solution)/shard_map/slice | solution.py:82
  404.1 71.2 %while.122 = (s32[]{:T(128)}, f32[24,64,128]{2,1,0:T(8,128)S(1)}, s32[]{:T(128)}, f32[2,128,24,64]{1,0,3,2:T(2,128)}, f32[2,24,64,128]{3,2,1,0:T(8,128)}, /*inde...) while((s32[]{:T(128)}, f32[24,64,128]{2,1,0:T(8,128)S(1)}, ...), condition=%wide.region_48.50_spmd.clone, body=%wide.region_46.49_spmd.clone.sunk | while | flops 935139840 | bytes 10227911 | solution.py:143
  477.2 68.8 %while.118 = (s32[]{:T(128)}, f32[24,64,128]{2,1,0:T(8,128)}, s32[]{:T(128)}, f32[2,128,24,64]{1,0,3,2:T(2,128)}, f32[2,128,24]{2,1,0:T(8,128)S(1)}, /*index=5*/...) while((s32[]{:T(128)}, f32[24,64,128]{2,1,0:T(8,128)}, ...), condition=%wide.region_9.10_spmd.clone, body=%wide.region_7.9_spmd.clone.sunk | while | flops 934943232 | bytes 14945990 | solution.py:143
  596.4 64.2 %while.120 = (s32[]{:T(128)}, f32[24,64,128]{2,1,0:T(8,128)S(1)}, s32[]{:T(128)}, f32[2,128,24,64]{1,0,3,2:T(2,128)}, f32[2,24,64,128]{3,2,1,0:T(8,128)}, /*inde...) while((s32[]{:T(128)}, f32[24,64,128]{2,1,0:T(8,128)S(1)}, ...), condition=%wide.region_26.28_spmd.clone, body=%wide.region_24.27_spmd.clone.sunk | while | flops 935139840 | bytes 10227911 | solution.py:143
  681.1 55.0 %all-gather.51.cloned.1.call-done = bf16[1,1024,4096]{2,1,0:T(8,128)(2,1)} async-done(((bf16[1,32,4096]{2,1,0:T(8,128)(2,1)}), bf16[1,1024,4096]{2,1,0:T(8,128)(2,1)}) %all-gather.51.cloned.1.call-update) | async-done | bytes 8388624 | tf_op jit(solution)/shard_map/all_gather | solution.py:260
  744.0 55.9 %all-gather.53.cloned.1.call-done = bf16[1,2048,1024]{2,1,0:T(8,128)(2,1)} async-done(((bf16[1,64,1024]{2,1,0:T(8,128)(2,1)}), bf16[1,2048,1024]{2,1,0:T(8,128)(2,1)}) %all-gather.53.cloned.1.call-update) | async-done | bytes 4194320 | tf_op jit(solution)/shard_map/all_gather | solution.py:261
  824.0 62.6 %while.119 = (s32[]{:T(128)}, f32[24,64,128]{2,1,0:T(8,128)S(1)}, s32[]{:T(128)}, f32[2,128,24,64]{1,0,3,2:T(2,128)}, f32[2,128,24]{2,1,0:T(8,128)S(1)}, /*index...) while((s32[]{:T(128)}, f32[24,64,128]{2,1,0:T(8,128)S(1)}, ...), condition=%wide.region_17.18_spmd.clone, body=%wide.region_15.17_spmd.clone.sunk | while | flops 934943232 | bytes 8654506 | solution.py:143
  902.4 105.9 %while.121 = (s32[]{:T(128)}, f32[24,64,128]{2,1,0:T(8,128)}, f32[2,128,24,64]{1,0,3,2:T(2,128)}, f32[2,128,128]{2,1,0:T(8,128)}, f32[2,128,128]{2,1,0:T(8,128)}...) while((s32[]{:T(128)}, f32[24,64,128]{2,1,0:T(8,128)}, ...), condition=%wide.region_44.46_spmd.clone, body=%wide.region_34.45_spmd.clone.sunk | while | flops 2201735680 | bytes 36228012 | solution.py:143
  932.4 19.1 dynamic_update_slice.171
  985.6 19.1 dynamic_update_slice.171
  1058.9 132.2 %while.123 = (s32[]{:T(128)}, f32[24,64,128]{2,1,0:T(8,128)}, f32[2,128,24,64]{1,0,3,2:T(2,128)}, f32[2,128,128]{2,1,0:T(8,128)}, f32[2,128,128]{2,1,0:T(8,128)}...) while((s32[]{:T(128)}, f32[24,64,128]{2,1,0:T(8,128)}, ...), condition=%wide.region_66.68_spmd.clone, body=%wide.region_56.67_spmd.clone.sunk | while | flops 2201735680 | bytes 36805648 | solution.py:143
  1326.1 27.4 reduce-scatter.45.cloned.1.call-done
  1354.3 133.5 %reduce-scatter.47.cloned.1.call-done = f32[32,2]{1,0:T(8,128)} async-done(((f32[1024,2]{1,0:T(8,128)}), f32[32,2]{1,0:T(8,128)}) %reduce-scatter.47.cloned.1.call-update) | async-done | bytes 272
  1489.2 126.0 %all-reduce.68.cloned.1.call-done = (f32[4,1792]{1,0:T(4,128)}, f32[4,1792]{1,0:T(4,128)}, f32[1536]{0:T(1024)}, f32[1536]{0:T(1024)}, f32[2,24]{1,0:T(2,128)}, /*index=5*/f32[2,24]{1,0:T(2,128)}, f32[2,24]{1,0:T(2,128)}) async-done(((f32[4,1792]{1,0:T(4,128)}, f32[4,1792]{1,0:T(4,128)}, f32[1536]{0:T(1024)}, f32[1536]{0:T(1024)}, f32[2,24]{1,0:T(2,128)}, /*index=5*/f32[2,24]{1,0:T(2,128)}, ...) | async-done | bytes 70224
  1624.6 133.1 %reduce-scatter.33.cloned.1.call-done = f32[16,1024]{1,0:T(8,128)} async-done(((f32[512,1024]{1,0:T(8,128)}), f32[16,1024]{1,0:T(8,128)}) %reduce-scatter.33.cloned.1.call-update) | async-done | bytes 65552 | tf_op jit(solution)/shard_map/reduce_scatter | solution.py:311
  1757.7 136.3 %reduce-scatter.35.cloned.1.call-done = f32[16,1024]{1,0:T(8,128)} async-done(((f32[512,1024]{1,0:T(8,128)}), f32[16,1024]{1,0:T(8,128)}) %reduce-scatter.35.cloned.1.call-update) | async-done | bytes 65552 | tf_op jit(solution)/shard_map/reduce_scatter | solution.py:311
  1895.5 101.9 %reduce-scatter.31.cloned.1.call-done = f32[32,768]{1,0:T(8,128)} async-done(((f32[1024,768]{1,0:T(8,128)}), f32[32,768]{1,0:T(8,128)}) %reduce-scatter.31.cloned.1.call-update) | async-done | bytes 98320 | tf_op jit(solution)/shard_map/reduce_scatter | solution.py:310
  1997.4 106.4 %reduce-scatter.29.cloned.1.call-done = f32[32,768]{1,0:T(8,128)} async-done(((f32[1024,768]{1,0:T(8,128)}), f32[32,768]{1,0:T(8,128)}) %reduce-scatter.29.cloned.1.call-update) | async-done | bytes 98320 | tf_op jit(solution)/shard_map/reduce_scatter | solution.py:310
  2105.5 117.8 %reduce-scatter.25.cloned.1.call-done = f32[48,1024]{1,0:T(8,128)} async-done(((f32[1536,1024]{1,0:T(8,128)}), f32[48,1024]{1,0:T(8,128)}) %reduce-scatter.25.cloned.1.call-update) | async-done | bytes 196624 | tf_op jit(solution)/shard_map/reduce_scatter | solution.py:309
  2223.4 119.3 %reduce-scatter.27.cloned.1.call-done = f32[48,1024]{1,0:T(8,128)} async-done(((f32[1536,1024]{1,0:T(8,128)}), f32[48,1024]{1,0:T(8,128)}) %reduce-scatter.27.cloned.1.call-update) | async-done | bytes 196624 | tf_op jit(solution)/shard_map/reduce_scatter | solution.py:309
  2344.4 148.8 %reduce-scatter.41.cloned.1.call-done = f32[64,1024]{1,0:T(8,128)} async-done(((f32[2048,1024]{1,0:T(8,128)}), f32[64,1024]{1,0:T(8,128)}) %reduce-scatter.41.cloned.1.call-update) | async-done | bytes 262160 | tf_op jit(solution)/shard_map/reduce_scatter | solution.py:313
  2493.3 148.8 %reduce-scatter.43.cloned.1.call-done = f32[64,1024]{1,0:T(8,128)} async-done(((f32[2048,1024]{1,0:T(8,128)}), f32[64,1024]{1,0:T(8,128)}) %reduce-scatter.43.cloned.1.call-update) | async-done | bytes 262160 | tf_op jit(solution)/shard_map/reduce_scatter | solution.py:313
  2643.9 164.0 %reduce-scatter.23.cloned.1.call-done = f32[32,3352]{1,0:T(8,128)} async-done(((f32[1024,3352]{1,0:T(8,128)}), f32[32,3352]{1,0:T(8,128)}) %reduce-scatter.23.cloned.1.call-update) | async-done | bytes 429072 | tf_op jit(solution)/shard_map/reduce_scatter | solution.py:306
  2808.0 167.8 %reduce-scatter.21.cloned.1.call-done = f32[32,3352]{1,0:T(8,128)} async-done(((f32[1024,3352]{1,0:T(8,128)}), f32[32,3352]{1,0:T(8,128)}) %reduce-scatter.21.cloned.1.call-update) | async-done | bytes 429072 | tf_op jit(solution)/shard_map/reduce_scatter | solution.py:306
  2977.9 181.9 %reduce-scatter.37.cloned.1.call-done = f32[32,4096]{1,0:T(8,128)} async-done(((f32[1024,4096]{1,0:T(8,128)}), f32[32,4096]{1,0:T(8,128)}) %reduce-scatter.37.cloned.1.call-update) | async-done | bytes 524304 | tf_op jit(solution)/shard_map/reduce_scatter | solution.py:312
  3159.8 186.9 %reduce-scatter.39.cloned.1.call-done = f32[32,4096]{1,0:T(8,128)} async-done(((f32[1024,4096]{1,0:T(8,128)}), f32[32,4096]{1,0:T(8,128)}) %reduce-scatter.39.cloned.1.call-update) | async-done | bytes 524304 | tf_op jit(solution)/shard_map/reduce_scatter | solution.py:312
  (1260 shorter events, 889.0 us)
Async XLA Ops:
  10.3 360.1 %all-gather.35.cloned.1.call-start = ((), (), s32[]{:S(2)}) async-start(), calls=%async_computation.32 | async-start | bytes 1622016 | tf_op jit(solution)/shard_map/all_gather | solution.py:258
  11.8 364.8 %all-gather.37.cloned.1.call-start = ((), (), s32[]{:S(2)}) async-start(), calls=%async_computation.33 | async-start | bytes 1081344 | tf_op jit(solution)/shard_map/all_gather | solution.py:259
  13.3 366.0 %all-gather.31.cloned.1.call-start = ((), (), s32[]{:S(2)}) async-start(), calls=%async_computation.30 | async-start | bytes 7299072 | tf_op jit(solution)/shard_map/all_gather | solution.py:254
  15.2 536.3 %all-gather.33.cloned.1.call-start = ((), (), s32[]{:S(2)}) async-start(), calls=%async_computation.31 | async-start | bytes 3244032 | tf_op jit(solution)/shard_map/all_gather | solution.py:257
  16.0 542.8 %all-gather.39.cloned.1.call-start = ((), (), s32[]{:S(2)}) async-start(), calls=%async_computation.34 | async-start | bytes 8650752 | tf_op jit(solution)/shard_map/all_gather | solution.py:260
  16.9 548.3 %all-gather.41.cloned.1.call-start = ((), (), s32[]{:S(2)}) async-start(), calls=%async_computation.35 | async-start | bytes 4325376 | tf_op jit(solution)/shard_map/all_gather | solution.py:261
  17.8 552.8 %all-gather.43.cloned.1.call-start = ((), (), s32[]{:S(2)}) async-start(), calls=%async_computation.36 | async-start | bytes 7299072 | tf_op jit(solution)/shard_map/all_gather | solution.py:254
  18.3 565.4 %all-gather.47.cloned.1.call-start = ((), (), s32[]{:S(2)}) async-start(), calls=%async_computation.38 | async-start | bytes 1622016 | tf_op jit(solution)/shard_map/all_gather | solution.py:258
  18.9 653.9 %all-gather.49.cloned.1.call-start = ((), (), s32[]{:S(2)}) async-start(), calls=%async_computation.39 | async-start | bytes 1081344 | tf_op jit(solution)/shard_map/all_gather | solution.py:259
  19.5 656.1 %all-gather.45.cloned.1.call-start = ((), (), s32[]{:S(2)}) async-start(), calls=%async_computation.37 | async-start | bytes 3244032 | tf_op jit(solution)/shard_map/all_gather | solution.py:257
  20.3 715.9 %all-gather.51.cloned.1.call-start = ((), (), s32[]{:S(2)}) async-start(), calls=%async_computation.40 | async-start | bytes 8650752 | tf_op jit(solution)/shard_map/all_gather | solution.py:260
  26.1 319.1 %all-to-all-start = ((bf16[32,8,1024]{2,1,0:T(8,128)(2,1)}), bf16[32,8,1024]{2,1,0:T(8,128)(2,1)}, u32[]{:S(2)}, u32[]{:S(2)}) async-start(bf16[32,8,1024]{2,1,0:T(8,128)(2,1)} %bitcast.3), calls=%async_computation | async-start | bytes 1048576 | tf_op jit(solution)/shard_map/all_to_all | solution.py:231
  33.5 766.3 %all-gather.53.cloned.1.call-start = ((), (), s32[]{:S(2)}) async-start(), calls=%async_computation.41 | async-start | bytes 4325376 | tf_op jit(solution)/shard_map/all_gather | solution.py:261
  293.7 597.3 %copy-start.134 = (f32[1536]{0:T(1024)}, f32[1536]{0:T(1024)S(1)}, u32[]{:S(2)}) copy-start(f32[1536]{0:T(1024)S(1)} %convert_element_type.577) | copy-start | bytes 18436
  345.2 20.0 all-to-all-start.2
  348.6 1004.9 %reduce-scatter.45.cloned.1.call-start = ((), (), s32[]{:S(2)}) async-start(), calls=%async_computation.42 | async-start | bytes 540672
  1218.6 269.3 %reduce-scatter.47.cloned.1.call-start = ((), (), s32[]{:S(2)}) async-start(), calls=%async_computation.43 | async-start | bytes 540672
  1221.2 394.0 %all-reduce.68.cloned.1.call-start = ((), (), s32[]{:S(2)}) async-start(), calls=%async_computation.44 | async-start | bytes 153600
  1223.2 534.5 %reduce-scatter.33.cloned.1.call-start = ((), (), s32[]{:S(2)}) async-start(), calls=%async_computation.24 | async-start | bytes 2162688 | tf_op jit(solution)/shard_map/reduce_scatter | solution.py:311
  1225.0 668.9 %reduce-scatter.35.cloned.1.call-start = ((), (), s32[]{:S(2)}) async-start(), calls=%async_computation.25 | async-start | bytes 2162688 | tf_op jit(solution)/shard_map/reduce_scatter | solution.py:311
  1226.9 770.6 %reduce-scatter.31.cloned.1.call-start = ((), (), s32[]{:S(2)}) async-start(), calls=%async_computation.23 | async-start | bytes 3244032 | tf_op jit(solution)/shard_map/reduce_scatter | solution.py:310
  1229.3 874.6 %reduce-scatter.29.cloned.1.call-start = ((), (), s32[]{:S(2)}) async-start(), calls=%async_computation.22 | async-start | bytes 3244032 | tf_op jit(solution)/shard_map/reduce_scatter | solution.py:310
  1232.8 990.6 %reduce-scatter.25.cloned.1.call-start = ((), (), s32[]{:S(2)}) async-start(), calls=%async_computation.20 | async-start | bytes 6488064 | tf_op jit(solution)/shard_map/reduce_scatter | solution.py:309
  1237.5 1105.1 %reduce-scatter.27.cloned.1.call-start = ((), (), s32[]{:S(2)}) async-start(), calls=%async_computation.21 | async-start | bytes 6488064 | tf_op jit(solution)/shard_map/reduce_scatter | solution.py:309
  1242.4 1250.9 %reduce-scatter.41.cloned.1.call-start = ((), (), s32[]{:S(2)}) async-start(), calls=%async_computation.28 | async-start | bytes 8650752 | tf_op jit(solution)/shard_map/reduce_scatter | solution.py:313
  1249.3 1392.8 %reduce-scatter.43.cloned.1.call-start = ((), (), s32[]{:S(2)}) async-start(), calls=%async_computation.29 | async-start | bytes 8650752 | tf_op jit(solution)/shard_map/reduce_scatter | solution.py:313
  1256.1 1551.8 %reduce-scatter.23.cloned.1.call-start = ((), (), s32[]{:S(2)}) async-start(), calls=%async_computation.19 | async-start | bytes 14598144 | tf_op jit(solution)/shard_map/reduce_scatter | solution.py:306
  1265.7 1710.0 %reduce-scatter.21.cloned.1.call-start = ((), (), s32[]{:S(2)}) async-start(), calls=%async_computation.18 | async-start | bytes 14598144 | tf_op jit(solution)/shard_map/reduce_scatter | solution.py:306
  1274.4 1885.4 %reduce-scatter.37.cloned.1.call-start = ((), (), s32[]{:S(2)}) async-start(), calls=%async_computation.26 | async-start | bytes 17301504 | tf_op jit(solution)/shard_map/reduce_scatter | solution.py:312
  1285.3 2061.4 %reduce-scatter.39.cloned.1.call-start = ((), (), s32[]{:S(2)}) async-start(), calls=%async_computation.27 | async-start | bytes 17301504 | tf_op jit(solution)/shard_map/reduce_scatter | solution.py:312
  1300.7 19.5 all-to-all-start.3
  1320.3 301.7 %all-to-all-start.1 = ((bf16[32,8,1024]{2,1,0:T(8,128)(2,1)}), bf16[32,8,1024]{2,1,0:T(8,128)(2,1)S(1)}, u32[]{:S(2)}, u32[]{:S(2)}) async-start(bf16[32,8,1024]{2,1,0:T(8,128)(2,1)} %bitcast.52), calls=%async_computation.1 | async-start | bytes 1048576 | tf_op jit(solution)/shard_map/all_to_all | solution.py:291
  (283 other events, 6052.3 us)
Sparse Core Ops, SparseCore 0:
  11.8 3.0 sort.39.cloned.1.call-done
  (1 shorter events, 0.0 us)
Sparse Core Ops, SparseCore 1:
  13.6 60.2 all-gather.34
  76.6 53.6 all-gather.36
  133.1 71.1 all-gather.30
  207.1 59.5 all-gather.32
  269.6 76.2 all-gather.38
  349.4 61.5 all-gather.40
  413.7 70.7 all-gather.42
  487.2 53.3 all-gather.46
  543.3 52.6 all-gather.48
  598.9 58.2 all-gather.44
  660.4 75.6 all-gather.50
  739.6 60.2 all-gather.52
  1218.6 134.8 reduce-scatter.44
  1355.8 132.0 reduce-scatter.46
  1495.4 119.7 all-reduce.67
  1617.5 140.1 reduce-scatter.32
  1759.9 134.0 reduce-scatter.34
  1899.4 98.0 reduce-scatter.30
  2002.7 101.1 reduce-scatter.28
  2109.5 113.8 reduce-scatter.24
  2228.9 113.7 reduce-scatter.26
  2344.8 148.4 reduce-scatter.40
  2495.4 146.6 reduce-scatter.42
  2648.1 159.8 reduce-scatter.22
  2813.8 161.8 reduce-scatter.20
  2978.0 181.7 reduce-scatter.36
  3162.1 184.5 reduce-scatter.38
where the time goes:
time: 3390 us; the launch traced here: 3360 us
  waiting for transfers between devices  2130 us (63%)
  local copies, waits for them, and re-layouts  487 us (14%)
  matrix products  316 us (9%)
  blocking collectives  206 us (6%)
  other arithmetic  162 us (5%)
    reduce_scatter x2, waiting for transfers between devices, shards(): lax.psum_scatter(weight_terms[7], 'dp', scatter_dimension=0, tiled=True)  369 us
    reduce_scatter x2, waiting for transfers between devices, shards(): lax.psum_scatter(weight_terms[1], 'dp', scatter_dimension=0, tiled=True)  332 us
    reduce_scatter x2, waiting for transfers between devices, shards(): lax.psum_scatter(weight_terms[8], 'dp', scatter_dimension=0, tiled=True)  298 us
    unnamed x30, waiting for transfers between devices  291 us
    reduce_scatter x2, waiting for transfers between devices, shards(): lax.psum_scatter(weight_terms[6], 'dp', scatter_dimension=0, tiled=True)  269 us
    reduce_scatter x2, waiting for transfers between devices, shards(): lax.psum_scatter(weight_terms[4], 'dp', scatter_dimension=0, tiled=True)  237 us
    dynamic_update_slice x24, local copies, waits for them, and re-layouts, state_space(): _, outputs = lax.scan(jax.checkpoint(block_step), start, inputs)  231 us
    reduce_scatter x2, waiting for transfers between devices, shards(): lax.psum_scatter(weight_terms[5], 'dp', scatter_dimension=0, tiled=True)  208 us
  transfers between devices with their start and end apart: 31, of which 18 were waited for; matrix products, arithmetic and copies ran while one was open for 16% of the time, Pallas kernels for 0%

commit v1 on v0

--- a/solution.py
+++ b/solution.py
@@ -99,49 +99,17 @@
     return jnp.concatenate([front * cosine - rear * sine, rear * cosine + front * sine], axis=-1)
 
 
-def block_step(carry, inputs):
-    state, last_segment = carry
-    x_part, b_part, c_part, dt_part, decay_log, seg_part = inputs
-    cumul = jnp.cumsum(decay_log, axis=0)
-    block_len = seg_part.shape[0]
-    rows_index = jnp.arange(block_len, dtype=jnp.int32)
-    inside = (seg_part[:, None] == seg_part[None, :]) & (rows_index[:, None] >= rows_index[None, :])
-    gaps = cumul[:, None, :] - cumul[None, :, :]
-    decay = jnp.exp(jnp.minimum(gaps, 0.0)) * inside[:, :, None].astype(cumul.dtype)
-    affinity = project(c_part, b_part.T, HIGHEST)
-    scaled = x_part * dt_part[:, :, None]
-    within = jnp.einsum("ijh,jhp->ihp", decay * affinity[:, :, None], scaled, precision=HIGHEST)
-    enters = (seg_part == last_segment).astype(cumul.dtype)
-    from_state = jnp.einsum("in,hpn->ihp", c_part, state, precision=HIGHEST)
-    carried = from_state * (jnp.exp(cumul) * enters[:, None])[:, :, None]
-    final_segment = seg_part[block_len - 1]
-    same_final = (seg_part == final_segment).astype(cumul.dtype)
-    toward = jnp.exp(cumul[block_len - 1][None, :] - cumul) * same_final[:, None]
-    fresh = jnp.einsum("jh,jhp,jn->hpn", toward, scaled, b_part, precision=HIGHEST)
-    retain = jnp.exp(cumul[block_len - 1]) * (final_segment == last_segment).astype(cumul.dtype)
-    new_state = state * retain[:, None, None] + fresh
-    return ((new_state, final_segment), within + carried)
-
-
 def state_space(x_heads, b_all, c_all, dt_all, rates, segment):
     rows_count = x_heads.shape[0]
-    blocks = rows_count // SCAN_BLOCK
-
-    def split_rows(values):
-        return values.reshape((blocks, SCAN_BLOCK) + values.shape[1:])
-
-    start = (jnp.zeros((HEADS, HDIM, STATE), jnp.float32), jnp.array(-1, dtype=jnp.int32))
-    decay_log = dt_all * rates[None, :]
-    inputs = (
-        split_rows(x_heads),
-        split_rows(b_all),
-        split_rows(c_all),
-        split_rows(dt_all),
-        split_rows(decay_log),
-        split_rows(segment),
-    )
-    _, outputs = lax.scan(jax.checkpoint(block_step), start, inputs)
-    return outputs.reshape(rows_count, HEADS, HDIM)
+    rows_index = jnp.arange(rows_count, dtype=jnp.int32)
+    inside = (segment[:, None] == segment[None, :]) & (rows_index[:, None] >= rows_index[None, :])
+    mask = inside.astype(jnp.float32)
+    cumul = project(mask, dt_all * rates[None, :], HIGHEST).T
+    gaps = cumul[:, :, None] - cumul[:, None, :]
+    decay = jnp.exp(jnp.where(inside[None], jnp.minimum(gaps, 0.0), -1e30))
+    affinity = project(c_all, b_all.T, HIGHEST)
+    scaled = x_heads * dt_all[:, :, None]
+    return jnp.einsum("hij,jhp->ihp", decay * affinity[None], scaled, precision=HIGHEST)
 
 
 def attention(normed, w_qkv, w_attn, segment, position, precise, rounders):
@@ -262,20 +230,6 @@
         )
         return tuple((piece.astype(jnp.float32) for piece in pieces))
 
-    def gather_layer_again(layer_idx):
-        pieces = (
-            lax.all_gather(norm_gains[layer_idx], "dp", axis=1, tiled=True),
-            lax.all_gather(in_proj[layer_idx], "dp", axis=0, tiled=True),
-            lax.all_gather(conv_weight[layer_idx], "dp", axis=1, tiled=True),
-            lax.all_gather(ssm_gain[layer_idx], "dp", axis=0, tiled=True),
-            lax.all_gather(mixer_out[layer_idx], "dp", axis=0, tiled=True),
-            lax.all_gather(qkv_proj[layer_idx], "dp", axis=0, tiled=True),
-            lax.all_gather(attn_out[layer_idx], "dp", axis=0, tiled=True),
-            lax.all_gather(gate_up[layer_idx], "dp", axis=0, tiled=True),
-            lax.all_gather(down_proj[layer_idx], "dp", axis=0, tiled=True),
-        )
-        return tuple((piece.astype(jnp.float32) for piece in pieces))
-
     def heads_of(layer_idx):
         return (a_log[layer_idx], d_skip[layer_idx], dt_bias[layer_idx])
 
@@ -285,8 +239,8 @@
     inputs_kept = []
     for layer_idx in range(LAYERS):
         weights = gather_layer(layer_idx)
-        inputs_kept.append(hidden)
-        hidden = layer_step(hidden, weights, heads_of(layer_idx))
+        hidden, puller = jax.vjp(layer_step, hidden, weights, heads_of(layer_idx))
+        inputs_kept.append(puller)
     leaving = hidden.astype(jnp.bfloat16)[places].reshape(devices, share, model_width)
     returned = lax.all_to_all(leaving, "dp", split_axis=0, concat_axis=0, tiled=True)
     out_tokens = (
@@ -298,9 +252,11 @@
     owned_parts = [None] * LAYERS
     head_parts = [None] * LAYERS
     for layer_idx in reversed(range(LAYERS)):
-        weights = gather_layer_again(layer_idx)
-        _, puller = jax.vjp(layer_step, inputs_kept[layer_idx], weights, heads_of(layer_idx))
-        flowing, weight_terms, head_terms = puller(flowing)
+        flowing, weight_terms, head_terms = inputs_kept[layer_idx](flowing)
+        weight_terms = tuple(
+            term.astype(jnp.bfloat16) if place > 3 or place == 1 else term
+            for place, term in enumerate(weight_terms)
+        )
         owned_parts[layer_idx] = (
             lax.psum_scatter(weight_terms[0], "dp", scatter_dimension=1, tiled=True),
             lax.psum_scatter(weight_terms[1], "dp", scatter_dimension=0, tiled=True),
@@ -315,7 +271,7 @@
         head_parts[layer_idx] = head_terms
     stacked = tuple(
         (
-            jnp.stack([owned_parts[layer_idx][member] for layer_idx in range(LAYERS)])
+            jnp.stack([owned_parts[layer_idx][member] for layer_idx in range(LAYERS)]).astype(jnp.float32)
             for member in range(9)
         )
     )

time: 3390 us -> 2870 us (0.85)
  local copies, waits for them, and re-layouts: 487 us -> 159 us
  matrix products: 316 us -> 199 us
  other arithmetic: 162 us -> 93 us
    dynamic_update_slice x24 -> x0, local copies, waits for them, and re-layouts: 231 us -> none  [state_space(): _, outputs = lax.scan(jax.checkpoint(block_step), start, inputs)]
    dot_general x52 -> x6, matrix products: 141 us -> 47.8 us  [state_space(): jnp.einsum('hij,jhp->ihp', decay * affinity[None], scaled, precision=HIGH...]
    reduce_scatter x2, waiting for transfers between devices: 332 us -> 243 us  [shards(): lax.psum_scatter(weight_terms[1], 'dp', scatter_dimension=0, tiled=True)]
    reduce_scatter x2, waiting for transfers between devices: 369 us -> 298 us  [shards(): lax.psum_scatter(weight_terms[7], 'dp', scatter_dimension=0, tiled=True)]
    all_gather x2, waiting for transfers between devices: 0.03 us -> 63.2 us  [gather_layer(): lax.all_gather(in_proj[layer_idx], 'dp', axis=0, tiled=True)]
    all_gather x2, waiting for transfers between devices: 0.03 us -> 51.1 us  [gather_layer(): lax.all_gather(attn_out[layer_idx], 'dp', axis=0, tiled=True)]
    all_gather x2, waiting for transfers between devices: 0.03 us -> 50.8 us  [gather_layer(): lax.all_gather(qkv_proj[layer_idx], 'dp', axis=0, tiled=True)]
    all_gather x2, waiting for transfers between devices: 0.01 us -> 38 us  [gather_layer(): lax.all_gather(mixer_out[layer_idx], 'dp', axis=0, tiled=True)]
  transfers between devices with their start and end apart: 31 -> 31, of which waited for: 18 -> 24; matrix products, arithmetic and copies ran while one was open for 16% -> 10% of each run, Pallas kernels for 0% -> 0%
where the time goes in v1:
time: 2870 us; the launch traced here: 2860 us
  waiting for transfers between devices  2160 us (75%)
  blocking collectives  207 us (7%)
  matrix products  199 us (7%)
  local copies, waits for them, and re-layouts  159 us (6%)
  other arithmetic  93 us (3%)
    unnamed x30, waiting for transfers between devices  302 us
    reduce_scatter x2, waiting for transfers between devices, shards(): lax.psum_scatter(weight_terms[7], 'dp', scatter_dimension=0, tiled=True)  298 us
    reduce_scatter x2, waiting for transfers between devices, shards(): lax.psum_scatter(weight_terms[8], 'dp', scatter_dimension=0, tiled=True)  283 us
    reduce_scatter x2, waiting for transfers between devices, shards(): lax.psum_scatter(weight_terms[6], 'dp', scatter_dimension=0, tiled=True)  266 us
    reduce_scatter x2, waiting for transfers between devices, shards(): lax.psum_scatter(weight_terms[1], 'dp', scatter_dimension=0, tiled=True)  243 us
    reduce_scatter x2, waiting for transfers between devices, shards(): lax.psum_scatter(weight_terms[4], 'dp', scatter_dimension=0, tiled=True)  212 us
    reduce_scatter x2, waiting for transfers between devices, shards(): lax.psum_scatter(weight_terms[5], 'dp', scatter_dimension=0, tiled=True)  200 us
    dot_general x46, matrix products, project(): jnp.dot(left, right, preferred_element_type=jnp.float32, precision=precise)  137 us
  transfers between devices with their start and end apart: 31, of which 24 were waited for; matrix products, arithmetic and copies ran while one was open for 10% of the time, Pallas kernels for 0%

profile of v1, /device:TPU:0, one launch (start us, length us, event | category | flops | bytes accessed | tf_op | source)
XLA Modules:
  0.0 2857.4 jit_solution(1552406119455191991)
XLA Ops:
  35.5 44.6 %all-gather = bf16[1,2,1024]{1,0,2:T(2,128)(2,1)S(1)} all-gather(bf16[1,2,32]{1,0,2:T(2,128)(2,1)S(1)} %copy.179), channel_id=2, replica_groups=mesh['dp'=32] {'dp'}, dimensions={2}, use_global_device_ids=true | all-gather | bytes 4224 | tf_op jit(solution)/shard_map/all_gather | solution.py:221
  86.9 40.8 %all-gather.2 = bf16[1,4,1792]{1,0,2:T(2,128)(2,1)S(1)} all-gather(bf16[1,4,56]{1,0,2:T(2,128)(2,1)S(1)} %copy.180), channel_id=4, replica_groups=mesh['dp'=32] {'dp'}, dimensions={2}, use_global_device_ids=true | all-gather | bytes 14784 | tf_op jit(solution)/shard_map/all_gather | solution.py:223
  128.8 37.5 %slice_reduce_fusion.7 = (f32[1792]{0:T(1024)S(1)}, f32[1792]{0:T(1024)S(1)}, f32[1792]{0:T(1024)S(1)}, f32[1792]{0:T(1024)S(1)}) fusion(f32[1,4,1792]{1,0,2:T(1,128)S(1)} %convert_element_type.372), kind=kLoop, calls=%fused_computation.289 | loop fusion | bytes 57344 | tf_op jit(solution)/shard_map/jvp()/slice | solution.py:82
  169.0 38.9 %all-reduce.61 = (bf16[1536]{0:T(1024)(128)(2,1)S(1)}, bf16[1536]{0:T(1024)(128)(2,1)S(1)}) all-reduce(bf16[1536]{0:T(1024)(128)(2,1)S(1)} %dynamic-update-slice, bf16[1536]{0:T(1024)(128)(2,1)S(1)} %dynamic-update-slice.1), channel_id=5, replica_groups=mesh['dp'=32] {'dp'}, use_global_device_ids=true, to_apply=%add.54 | all-reduce | flops 3072 | bytes 12288
  208.0 42.6 %all-gather.9 = bf16[1,2,1024]{1,0,2:T(2,128)(2,1)S(1)} all-gather(bf16[1,2,32]{1,0,2:T(2,128)(2,1)S(1)} %copy.181), channel_id=11, replica_groups=mesh['dp'=32] {'dp'}, dimensions={2}, use_global_device_ids=true | all-gather | bytes 4224 | tf_op jit(solution)/shard_map/all_gather | solution.py:221
  251.2 40.3 %all-gather.11 = bf16[1,4,1792]{1,0,2:T(2,128)(2,1)S(1)} all-gather(bf16[1,4,56]{1,0,2:T(2,128)(2,1)S(1)} %copy.182), channel_id=13, replica_groups=mesh['dp'=32] {'dp'}, dimensions={2}, use_global_device_ids=true | all-gather | bytes 14784 | tf_op jit(solution)/shard_map/all_gather | solution.py:223
  301.8 38.3 %slice_reduce_fusion.3 = (f32[1792]{0:T(1024)}, f32[1792]{0:T(1024)}, f32[1792]{0:T(1024)}, f32[1792]{0:T(1024)}) fusion(f32[1,4,1792]{1,0,2:T(1,128)S(1)} %convert_element_type.375), kind=kLoop, calls=%fused_computation.285 | loop fusion | bytes 57344 | tf_op jit(solution)/shard_map/jvp()/slice | solution.py:82
  348.5 13.1 all-to-all-done.2
  418.0 50.8 %all-gather.47.cloned.1.call-done = bf16[1,1024,768]{2,1,0:T(8,128)(2,1)} async-done(((bf16[1,32,768]{2,1,0:T(8,128)(2,1)}), bf16[1,1024,768]{2,1,0:T(8,128)(2,1)}) %all-gather.47.cloned.1.call-update) | async-done | bytes 1572880 | tf_op jit(solution)/shard_map/all_gather | solution.py:226
  479.4 63.2 %all-gather.43.cloned.1.call-done = bf16[1,1024,3352]{2,1,0:T(8,128)(2,1)} async-done(((bf16[1,32,3352]{2,1,0:T(8,128)(2,1)}), bf16[1,1024,3352]{2,1,0:T(8,128)(2,1)}) %all-gather.43.cloned.1.call-update) | async-done | bytes 6864912 | tf_op jit(solution)/shard_map/all_gather | solution.py:222
  565.0 37.9 %all-gather.45.cloned.1.call-done = bf16[1,1536,1024]{2,1,0:T(8,128)(2,1)} async-done(((bf16[1,48,1024]{2,1,0:T(8,128)(2,1)}), bf16[1,1536,1024]{2,1,0:T(8,128)(2,1)}) %all-gather.45.cloned.1.call-update) | async-done | bytes 3145744 | tf_op jit(solution)/shard_map/all_gather | solution.py:225
  607.1 51.1 %all-gather.49.cloned.1.call-done = bf16[1,512,1024]{2,1,0:T(8,128)(2,1)} async-done(((bf16[1,16,1024]{2,1,0:T(8,128)(2,1)}), bf16[1,512,1024]{2,1,0:T(8,128)(2,1)}) %all-gather.49.cloned.1.call-update) | async-done | bytes 1048592 | tf_op jit(solution)/shard_map/all_gather | solution.py:227
  661.5 75.9 %all-gather.51.cloned.1.call-done = bf16[1,1024,4096]{2,1,0:T(8,128)(2,1)} async-done(((bf16[1,32,4096]{2,1,0:T(8,128)(2,1)}), bf16[1,1024,4096]{2,1,0:T(8,128)(2,1)}) %all-gather.51.cloned.1.call-update) | async-done | bytes 8388624 | tf_op jit(solution)/shard_map/all_gather | solution.py:228
  745.1 56.0 %all-gather.53.cloned.1.call-done = bf16[1,2048,1024]{2,1,0:T(8,128)(2,1)} async-done(((bf16[1,64,1024]{2,1,0:T(8,128)(2,1)}), bf16[1,2048,1024]{2,1,0:T(8,128)(2,1)}) %all-gather.53.cloned.1.call-update) | async-done | bytes 4194320 | tf_op jit(solution)/shard_map/all_gather | solution.py:229
  883.6 10.7 fusion.166
  906.2 12.6 multiply_reduce_fusion.5
  1012.7 10.4 all-to-all-done.3
  1026.2 39.5 %reduce-scatter.45.cloned.1.call-done = f32[32,2]{1,0:T(8,128)} async-done(((f32[1024,2]{1,0:T(8,128)}), f32[32,2]{1,0:T(8,128)}) %reduce-scatter.45.cloned.1.call-update) | async-done | bytes 272
  1066.5 133.1 %reduce-scatter.47.cloned.1.call-done = f32[32,2]{1,0:T(8,128)} async-done(((f32[1024,2]{1,0:T(8,128)}), f32[32,2]{1,0:T(8,128)}) %reduce-scatter.47.cloned.1.call-update) | async-done | bytes 272
  1200.9 125.8 %all-reduce.64.cloned.1.call-done = (f32[4,1792]{1,0:T(4,128)}, f32[4,1792]{1,0:T(4,128)}, f32[1536]{0:T(1024)}, f32[1536]{0:T(1024)}, f32[2,24]{1,0:T(2,128)}, /*index=5*/f32[2,24]{1,0:T(2,128)}, f32[2,24]{1,0:T(2,128)}) async-done(((f32[4,1792]{1,0:T(4,128)}, f32[4,1792]{1,0:T(4,128)}, f32[1536]{0:T(1024)}, f32[1536]{0:T(1024)}, f32[2,24]{1,0:T(2,128)}, /*index=5*/f32[2,24]{1,0:T(2,128)}, ...) | async-done | bytes 70224
  1336.1 131.5 %reduce-scatter.33.cloned.1.call-done = bf16[16,1024]{1,0:T(8,128)(2,1)} async-done(((bf16[512,1024]{1,0:T(8,128)(2,1)}), bf16[16,1024]{1,0:T(8,128)(2,1)}) %reduce-scatter.33.cloned.1.call-update) | async-done | bytes 32784 | tf_op jit(solution)/shard_map/reduce_scatter | solution.py:267
  1467.6 134.7 %reduce-scatter.35.cloned.1.call-done = bf16[16,1024]{1,0:T(8,128)(2,1)} async-done(((bf16[512,1024]{1,0:T(8,128)(2,1)}), bf16[16,1024]{1,0:T(8,128)(2,1)}) %reduce-scatter.35.cloned.1.call-update) | async-done | bytes 32784 | tf_op jit(solution)/shard_map/reduce_scatter | solution.py:267
  1603.7 97.9 %reduce-scatter.29.cloned.1.call-done = bf16[32,768]{1,0:T(8,128)(2,1)} async-done(((bf16[1024,768]{1,0:T(8,128)(2,1)}), bf16[32,768]{1,0:T(8,128)(2,1)}) %reduce-scatter.29.cloned.1.call-update) | async-done | bytes 49168 | tf_op jit(solution)/shard_map/reduce_scatter | solution.py:266
  1701.6 102.2 %reduce-scatter.31.cloned.1.call-done = bf16[32,768]{1,0:T(8,128)(2,1)} async-done(((bf16[1024,768]{1,0:T(8,128)(2,1)}), bf16[32,768]{1,0:T(8,128)(2,1)}) %reduce-scatter.31.cloned.1.call-update) | async-done | bytes 49168 | tf_op jit(solution)/shard_map/reduce_scatter | solution.py:266
  1805.3 105.2 %reduce-scatter.25.cloned.1.call-done = bf16[48,1024]{1,0:T(8,128)(2,1)} async-done(((bf16[1536,1024]{1,0:T(8,128)(2,1)}), bf16[48,1024]{1,0:T(8,128)(2,1)}) %reduce-scatter.25.cloned.1.call-update) | async-done | bytes 98320 | tf_op jit(solution)/shard_map/reduce_scatter | solution.py:265
  1910.5 106.5 %reduce-scatter.27.cloned.1.call-done = bf16[48,1024]{1,0:T(8,128)(2,1)} async-done(((bf16[1536,1024]{1,0:T(8,128)(2,1)}), bf16[48,1024]{1,0:T(8,128)(2,1)}) %reduce-scatter.27.cloned.1.call-update) | async-done | bytes 98320 | tf_op jit(solution)/shard_map/reduce_scatter | solution.py:265
  2018.7 142.2 %reduce-scatter.41.cloned.1.call-done = bf16[64,1024]{1,0:T(8,128)(2,1)} async-done(((bf16[2048,1024]{1,0:T(8,128)(2,1)}), bf16[64,1024]{1,0:T(8,128)(2,1)}) %reduce-scatter.41.cloned.1.call-update) | async-done | bytes 131088 | tf_op jit(solution)/shard_map/reduce_scatter | solution.py:269
  2160.8 140.8 %reduce-scatter.43.cloned.1.call-done = bf16[64,1024]{1,0:T(8,128)(2,1)} async-done(((bf16[2048,1024]{1,0:T(8,128)(2,1)}), bf16[64,1024]{1,0:T(8,128)(2,1)}) %reduce-scatter.43.cloned.1.call-update) | async-done | bytes 131088 | tf_op jit(solution)/shard_map/reduce_scatter | solution.py:269
  2303.4 119.1 %reduce-scatter.21.cloned.1.call-done = bf16[32,3352]{1,0:T(8,128)(2,1)} async-done(((bf16[1024,3352]{1,0:T(8,128)(2,1)}), bf16[32,3352]{1,0:T(8,128)(2,1)}) %reduce-scatter.21.cloned.1.call-update) | async-done | bytes 214544 | tf_op jit(solution)/shard_map/reduce_scatter | solution.py:262
  2422.5 123.9 %reduce-scatter.23.cloned.1.call-done = bf16[32,3352]{1,0:T(8,128)(2,1)} async-done(((bf16[1024,3352]{1,0:T(8,128)(2,1)}), bf16[32,3352]{1,0:T(8,128)(2,1)}) %reduce-scatter.23.cloned.1.call-update) | async-done | bytes 214544 | tf_op jit(solution)/shard_map/reduce_scatter | solution.py:262
  2548.4 148.6 %reduce-scatter.37.cloned.1.call-done = bf16[32,4096]{1,0:T(8,128)(2,1)} async-done(((bf16[1024,4096]{1,0:T(8,128)(2,1)}), bf16[32,4096]{1,0:T(8,128)(2,1)}) %reduce-scatter.37.cloned.1.call-update) | async-done | bytes 262160 | tf_op jit(solution)/shard_map/reduce_scatter | solution.py:268
  2697.0 149.0 %reduce-scatter.39.cloned.1.call-done = bf16[32,4096]{1,0:T(8,128)(2,1)} async-done(((bf16[1024,4096]{1,0:T(8,128)(2,1)}), bf16[32,4096]{1,0:T(8,128)(2,1)}) %reduce-scatter.39.cloned.1.call-update) | async-done | bytes 262160 | tf_op jit(solution)/shard_map/reduce_scatter | solution.py:268
  (778 shorter events, 373.8 us)
Async XLA Ops:
  10.3 354.1 %all-gather.35.cloned.1.call-start = ((), (), s32[]{:S(2)}) async-start(), calls=%async_computation.32 | async-start | bytes 1622016 | tf_op jit(solution)/shard_map/all_gather | solution.py:226
  11.8 360.2 %all-gather.31.cloned.1.call-start = ((), (), s32[]{:S(2)}) async-start(), calls=%async_computation.30 | async-start | bytes 7299072 | tf_op jit(solution)/shard_map/all_gather | solution.py:222
  13.7 380.9 %all-gather.33.cloned.1.call-start = ((), (), s32[]{:S(2)}) async-start(), calls=%async_computation.31 | async-start | bytes 3244032 | tf_op jit(solution)/shard_map/all_gather | solution.py:225
  15.4 383.7 %all-gather.37.cloned.1.call-start = ((), (), s32[]{:S(2)}) async-start(), calls=%async_computation.33 | async-start | bytes 1081344 | tf_op jit(solution)/shard_map/all_gather | solution.py:227
  16.2 386.2 %all-gather.39.cloned.1.call-start = ((), (), s32[]{:S(2)}) async-start(), calls=%async_computation.34 | async-start | bytes 8650752 | tf_op jit(solution)/shard_map/all_gather | solution.py:228
  17.1 395.3 %all-gather.41.cloned.1.call-start = ((), (), s32[]{:S(2)}) async-start(), calls=%async_computation.35 | async-start | bytes 4325376 | tf_op jit(solution)/shard_map/all_gather | solution.py:229
  17.9 450.9 %all-gather.47.cloned.1.call-start = ((), (), s32[]{:S(2)}) async-start(), calls=%async_computation.38 | async-start | bytes 1622016 | tf_op jit(solution)/shard_map/all_gather | solution.py:226
  18.5 524.1 %all-gather.43.cloned.1.call-start = ((), (), s32[]{:S(2)}) async-start(), calls=%async_computation.36 | async-start | bytes 7299072 | tf_op jit(solution)/shard_map/all_gather | solution.py:222
  19.1 583.9 %all-gather.45.cloned.1.call-start = ((), (), s32[]{:S(2)}) async-start(), calls=%async_computation.37 | async-start | bytes 3244032 | tf_op jit(solution)/shard_map/all_gather | solution.py:225
  19.6 638.6 %all-gather.49.cloned.1.call-start = ((), (), s32[]{:S(2)}) async-start(), calls=%async_computation.39 | async-start | bytes 1081344 | tf_op jit(solution)/shard_map/all_gather | solution.py:227
  20.4 717.0 %all-gather.51.cloned.1.call-start = ((), (), s32[]{:S(2)}) async-start(), calls=%async_computation.40 | async-start | bytes 8650752 | tf_op jit(solution)/shard_map/all_gather | solution.py:228
  26.2 317.1 %all-to-all-start = ((bf16[32,8,1024]{2,1,0:T(8,128)(2,1)}), bf16[32,8,1024]{2,1,0:T(8,128)(2,1)S(1)}, u32[]{:S(2)}, u32[]{:S(2)}) async-start(bf16[32,8,1024]{2,1,0:T(8,128)(2,1)} %bitcast.3), calls=%async_computation | async-start | bytes 1048576 | tf_op jit(solution)/shard_map/all_to_all | solution.py:199
  33.5 767.6 %all-gather.53.cloned.1.call-start = ((), (), s32[]{:S(2)}) async-start(), calls=%async_computation.41 | async-start | bytes 4325376 | tf_op jit(solution)/shard_map/all_gather | solution.py:229
  34.7 784.6 %copy-start.63 = (pred[256,256]{0,1:T(8,128)(4,1)}, pred[256,256]{0,1:T(8,128)(4,1)S(1)}, u32[]{:S(2)}) copy-start(pred[256,256]{0,1:T(8,128)(4,1)S(1)} %fusion.182) | copy-start | bytes 196612
  343.3 18.2 all-to-all-start.2
  346.0 719.7 %reduce-scatter.45.cloned.1.call-start = ((), (), s32[]{:S(2)}) async-start(), calls=%async_computation.42 | async-start | bytes 540672
  930.5 269.0 %reduce-scatter.47.cloned.1.call-start = ((), (), s32[]{:S(2)}) async-start(), calls=%async_computation.43 | async-start | bytes 540672
  940.5 386.2 %all-reduce.64.cloned.1.call-start = ((), (), s32[]{:S(2)}) async-start(), calls=%async_computation.44 | async-start | bytes 153600
  942.4 525.2 %reduce-scatter.33.cloned.1.call-start = ((), (), s32[]{:S(2)}) async-start(), calls=%async_computation.24 | async-start | bytes 1081344 | tf_op jit(solution)/shard_map/reduce_scatter | solution.py:267
  944.0 658.3 %reduce-scatter.35.cloned.1.call-start = ((), (), s32[]{:S(2)}) async-start(), calls=%async_computation.25 | async-start | bytes 1081344 | tf_op jit(solution)/shard_map/reduce_scatter | solution.py:267
  945.5 756.1 %reduce-scatter.29.cloned.1.call-start = ((), (), s32[]{:S(2)}) async-start(), calls=%async_computation.22 | async-start | bytes 1622016 | tf_op jit(solution)/shard_map/reduce_scatter | solution.py:266
  948.4 855.4 %reduce-scatter.31.cloned.1.call-start = ((), (), s32[]{:S(2)}) async-start(), calls=%async_computation.23 | async-start | bytes 1622016 | tf_op jit(solution)/shard_map/reduce_scatter | solution.py:266
  950.3 960.1 %reduce-scatter.25.cloned.1.call-start = ((), (), s32[]{:S(2)}) async-start(), calls=%async_computation.20 | async-start | bytes 3244032 | tf_op jit(solution)/shard_map/reduce_scatter | solution.py:265
  954.2 1062.7 %reduce-scatter.27.cloned.1.call-start = ((), (), s32[]{:S(2)}) async-start(), calls=%async_computation.21 | async-start | bytes 3244032 | tf_op jit(solution)/shard_map/reduce_scatter | solution.py:265
  958.0 1202.8 %reduce-scatter.41.cloned.1.call-start = ((), (), s32[]{:S(2)}) async-start(), calls=%async_computation.28 | async-start | bytes 4325376 | tf_op jit(solution)/shard_map/reduce_scatter | solution.py:269
  963.5 1338.0 %reduce-scatter.43.cloned.1.call-start = ((), (), s32[]{:S(2)}) async-start(), calls=%async_computation.29 | async-start | bytes 4325376 | tf_op jit(solution)/shard_map/reduce_scatter | solution.py:269
  969.1 1453.5 %reduce-scatter.21.cloned.1.call-start = ((), (), s32[]{:S(2)}) async-start(), calls=%async_computation.18 | async-start | bytes 7299072 | tf_op jit(solution)/shard_map/reduce_scatter | solution.py:262
  975.6 1570.8 %reduce-scatter.23.cloned.1.call-start = ((), (), s32[]{:S(2)}) async-start(), calls=%async_computation.19 | async-start | bytes 7299072 | tf_op jit(solution)/shard_map/reduce_scatter | solution.py:262
  982.2 1714.8 %reduce-scatter.37.cloned.1.call-start = ((), (), s32[]{:S(2)}) async-start(), calls=%async_computation.26 | async-start | bytes 8650752 | tf_op jit(solution)/shard_map/reduce_scatter | solution.py:268
  990.6 1855.4 %reduce-scatter.39.cloned.1.call-start = ((), (), s32[]{:S(2)}) async-start(), calls=%async_computation.27 | async-start | bytes 8650752 | tf_op jit(solution)/shard_map/reduce_scatter | solution.py:268
  1003.7 19.4 all-to-all-start.3
  1023.1 310.5 %all-to-all-start.1 = ((bf16[32,8,1024]{2,1,0:T(8,128)(2,1)}), bf16[32,8,1024]{2,1,0:T(8,128)(2,1)S(1)}, u32[]{:S(2)}, u32[]{:S(2)}) async-start(bf16[32,8,1024]{2,1,0:T(8,128)(2,1)} %bitcast.55), calls=%async_computation.1 | async-start | bytes 1048576 | tf_op jit(solution)/shard_map/all_to_all | solution.py:245
  (224 other events, 7295.9 us)
Sparse Core Ops, SparseCore 0:
  11.8 3.1 sort.39.cloned.1.call-done
  (1 shorter events, 0.0 us)
Sparse Core Ops, SparseCore 1:
  13.6 60.9 all-gather.34
  77.9 73.4 all-gather.30
  154.1 57.9 all-gather.32
  214.9 52.5 all-gather.36
  271.0 77.7 all-gather.38
  352.2 60.2 all-gather.40
  415.2 53.6 all-gather.46
  471.6 70.9 all-gather.42
  545.3 57.6 all-gather.44
  605.8 52.3 all-gather.48
  661.5 75.9 all-gather.50
  740.9 60.2 all-gather.52
  930.6 135.0 reduce-scatter.44
  1067.9 131.5 reduce-scatter.46
  1207.1 119.5 all-reduce.63
  1329.0 138.6 reduce-scatter.32
  1469.9 132.4 reduce-scatter.34
  1607.6 94.0 reduce-scatter.28
  1706.7 97.0 reduce-scatter.30
  1809.2 101.2 reduce-scatter.24
  1915.8 101.1 reduce-scatter.26
  2019.1 141.7 reduce-scatter.40
  2163.0 138.5 reduce-scatter.42
  2307.3 115.2 reduce-scatter.20
  2428.1 118.3 reduce-scatter.22
  2548.7 148.2 reduce-scatter.36
  2699.3 146.6 reduce-scatter.38

commit v2 on v1

v2 whole, which is shorter than its diff:
```python
import functools

import jax
import jax.numpy as jnp
from jax import lax
from jax.experimental import pallas as pl
from jax.experimental.pallas import tpu as pltpu
from jax.sharding import PartitionSpec as P

FF = 2048
HEADS = 24
HDIM = 64
STATE = 128
QH = 8
KVH = 2
HD = 64
LAYERS = 2
INNER = 1536
CONVCH = 1792
TAPS = 4
EPSILON = 1e-05
ROPE_BASE = 100000000000.0
SCORE_SCALE = 0.125
HIGHEST = lax.Precision.HIGHEST
F32 = jnp.float32
BF16 = jnp.bfloat16
MESH = pl.DeviceIdType.MESH

AG_CHUNKS = [(1, 3, (4, 3, 1, 2)), (0, 2, (1, 4, 3, 2)), (0, 3, (4, 3, 2, 1)), (0, 5, (2, 4, 3, 1)), (0, 0, (4, 3, 2, 1)), (1, 2, (1, 4, 3, 2)), (1, 1, (4, 3, 1, 2)), (1, 5, (4, 3, 1, 2)), (0, 4, (2, 1, 4, 3)), (1, 4, (4, 3, 1, 2)), (0, 1, (2, 1, 4, 3)), (1, 0, (4, 3, 2, 1))]
AG_EVENTS = [(1, 0), (0, 0), (5, 0), (2, 0), (3, 0), (8, 0), (10, 0), (4, 0), (6, 0), (7, 0), (8, 1), (0, 1), (10, 1), (2, 1), (0, 2), (9, 0), (2, 2), (0, 3), (2, 3), (11, 0), (4, 1), (1, 1), (6, 1), (5, 1), (7, 1), (6, 2), (3, 1), (4, 2), (7, 2), (6, 3), (9, 1), (7, 3), (11, 1), (4, 3), (8, 2), (1, 2), (5, 2), (10, 2), (3, 2), (11, 2), (9, 2), (1, 3), (5, 3), (3, 3), (8, 3), (10, 3), (9, 3), (11, 3)]
RS_CHUNKS = [(0, 0, 1792, (1, 2, 3, 4)), (1, 0, 512, (2, 3, 4, 1)), (2, 384, 768, (2, 3, 4, 1)), (0, 1792, 3352, (3, 4, 1, 2)), (4, 2048, 4096, (1, 2, 3, 4)), (5, 0, 512, (1, 2, 3, 4)), (5, 512, 1024, (1, 2, 3, 4)), (4, 0, 2048, (2, 3, 4, 1)), (3, 512, 1024, (3, 4, 1, 2)), (1, 512, 1024, (1, 2, 3, 4)), (2, 0, 384, (2, 1, 3, 4)), (3, 0, 512, (1, 2, 3, 4))]
RS_EVENTS = [(0, -1), (1, -1), (2, -1), (3, -1), (4, -1), (5, -1), (6, -1), (7, -1), (8, -1), (9, -1), (10, -1), (11, -1), (1, 0), (2, 0), (0, 0), (3, 0), (8, 0), (1, 1), (2, 1), (7, 0), (10, 0), (3, 1), (4, 0), (8, 1), (1, 2), (2, 2), (0, 1), (5, 0), (7, 1), (0, 2), (4, 1), (6, 0), (5, 1), (7, 2), (4, 2), (0, 3), (9, 0), (6, 1), (5, 2), (11, 0), (10, 1), (9, 1), (4, 3), (6, 2), (11, 1), (3, 2), (8, 2), (10, 2), (5, 3), (1, 3), (2, 3), (9, 2), (6, 3), (3, 3), (10, 3), (11, 2), (7, 3), (8, 3), (9, 3), (11, 3)]

SMALL_ROWS = 16


def dot(left, right):
    return jnp.dot(left, right, preferred_element_type=F32)


def dot_rt(left, right):
    return lax.dot_general(left, right, (((1,), (1,)), ((), ())), preferred_element_type=F32)


def flip(me, bit):
    step = 1 << bit
    return me + step * (1 - 2 * ((me // step) % 2))


def place(bits, free, mine, flipped=()):
    return tuple(
        slice(None) if b in free else 1 - mine[b] if b in flipped else mine[b]
        for b in reversed(range(bits))
    )


def greet(me, bits):
    barrier = pltpu.get_barrier_semaphore()
    for b in range(bits):
        pl.semaphore_signal(barrier, inc=1, device_id=(flip(me, b),), device_id_type=MESH)
    pl.semaphore_wait(barrier, bits)


def remote(me, src, dst, send, recv, bit):
    return pltpu.make_async_remote_copy(
        src_ref=src,
        dst_ref=dst,
        send_sem=send,
        recv_sem=recv,
        device_id=(flip(me, bit),),
        device_id_type=MESH,
    )


def gather_kernel(devices, chunks, events, layers, arrays, *refs):
    bits = devices.bit_length() - 1
    ins = refs[:arrays]
    outs = refs[arrays : arrays + layers * arrays]
    send_sem, recv_sem, csend_sem, crecv_sem, own_sem = refs[arrays + layers * arrays :]
    me = lax.axis_index("dp")
    mine = [(me // (1 << b)) % 2 for b in range(bits)]
    greet(me, bits)
    own, sends, cores, pending = [], [], [], {}
    for c, (l, a, order) in enumerate(chunks):
        here = outs[l * arrays + a].at[place(bits, (), mine)]
        src = ins[a].at[l]
        copy = remote(me, src, here, send_sem.at[c, 0], recv_sem.at[c, 0], order[0])
        copy.start()
        pending[c] = copy
        sends.append(copy)
        local = pltpu.make_async_copy(src, here, own_sem.at[c])
        local.start()
        own.append(local)
    for c, (l, a, order) in enumerate(chunks):
        here = outs[l * arrays + a].at[place(bits, (), mine)]
        copy = remote(me, ins[a].at[l], here, csend_sem.at[c, 0], crecv_sem.at[c, 0], 0)
        copy.start()
        sends.append(copy)
        cores.append(copy)
    for local in own:
        local.wait()
    for c, s in events:
        l, a, order = chunks[c]
        full = outs[l * arrays + a]
        pending[c].wait_recv()
        if s + 1 < bits - 1:
            view = full.at[place(bits, order[: s + 1], mine)]
            copy = remote(
                me, view, view, send_sem.at[c, s + 1], recv_sem.at[c, s + 1], order[s + 1]
            )
            copy.start()
            pending[c] = copy
            sends.append(copy)
        new = full.at[place(bits, order[:s], mine, (order[s],))]
        copy = remote(me, new, new, csend_sem.at[c, s + 1], crecv_sem.at[c, s + 1], 0)
        copy.start()
        sends.append(copy)
        cores.append(copy)
    for copy in sends:
        copy.wait_send()
    for copy in cores:
        copy.wait_recv()


def gather_all(shards, devices):
    bits = devices.bit_length() - 1
    layers = shards[0].shape[0]
    chunks = list(AG_CHUNKS)
    events = list(AG_EVENTS)
    extra = len(shards) - 1
    for layer in range(layers):
        c = len(chunks)
        chunks.append((layer, extra, (4, 3, 2, 1)))
        for s in range(bits - 1):
            events.insert(3 + layer + 6 * s, (c, s))
    n = len(chunks)
    outs = [
        jax.ShapeDtypeStruct((2,) * bits + s.shape[1:], s.dtype)
        for _ in range(layers)
        for s in shards
    ]
    res = pl.pallas_call(
        functools.partial(gather_kernel, devices, chunks, events, layers, len(shards)),
        out_shape=outs,
        in_specs=[pl.BlockSpec(memory_space=pltpu.VMEM)] * len(shards),
        out_specs=[pl.BlockSpec(memory_space=pl.ANY)] * len(outs),
        scratch_shapes=[pltpu.SemaphoreType.DMA((n, bits - 1))] * 2
        + [pltpu.SemaphoreType.DMA((n, bits))] * 2
        + [pltpu.SemaphoreType.DMA((n,))],
        compiler_params=pltpu.CompilerParams(collective_id=0, has_side_effects=True),
        name="gather_all",
    )(*shards)
    full = [r.reshape((devices * r.shape[-2], r.shape[-1])) for r in res]
    return [full[l * len(shards) : (l + 1) * len(shards)] for l in range(layers)]


PAIRS = ((0, 0), (1, 2), (0, 1), (2, 2), (3, 3), (4, 4))


def scatter_kernel(devices, arrs, nx, ny, *refs):
    bits = devices.bit_length() - 1
    chunks, events = RS_CHUNKS, RS_EVENTS
    half = devices // 2
    na, nc = len(arrs), len(chunks)
    groups, at = [], 0
    for size in (nx, ny, 1, na, 1, nx, ny, nc, nc * (bits - 1), bits - 1, bits):
        groups.append(refs[at : at + size])
        at += size
    xs, ys, small, outs, small_out, xr, yr, sums, parts, small_mid, small_got = groups
    small, small_out = small[0], small_out[0]
    xs_s, xs_r, ys_s, ys_r, st_s, st_r, sm_s, sm_r = refs[at:]
    me = lax.axis_index("dp")
    mine = [(me // (1 << b)) % 2 for b in range(bits)]
    greet(me, bits)
    core = mine[0]
    swaps_x, swaps_y, got_x, got_y = {}, {}, set(), set()
    for a, _, _, _ in chunks:
        xi, yi = PAIRS[a]
        if xi not in swaps_x:
            swaps_x[xi] = remote(
                me, xs[xi].at[:, 1 - core], xr[xi], xs_s.at[xi], xs_r.at[xi], 0
            )
            swaps_x[xi].start()
        if yi not in swaps_y:
            swaps_y[yi] = remote(me, ys[yi], yr[yi], ys_s.at[yi], ys_r.at[yi], 0)
            swaps_y[yi].start()
    sends, pending = [], {}

    def small_send(s):
        src = small if s == 0 else small_mid[s - 1]
        copy = remote(me, src, small_got[s], sm_s.at[s], sm_r.at[s], s)
        copy.start()
        pending["small"] = copy
        sends.append(copy)

    def small_receive(s):
        src = small if s == 0 else small_mid[s - 1]
        pending["small"].wait_recv()
        total = src[...] + small_got[s][...]
        if s + 1 < bits:
            small_mid[s][...] = total
            small_send(s + 1)
        else:
            small_out[...] = total

    def send(c, s):
        order = chunks[c][3]
        index = tuple(
            1 - mine[q] if q == order[s] else mine[q] if q in order[:s] else slice(None)
            for q in reversed(range(1, bits))
        )
        copy = remote(
            me,
            sums[c].at[index],
            parts[c * (bits - 1) + s],
            st_s.at[c, s],
            st_r.at[c, s],
            order[s],
        )
        copy.start()
        pending[c] = copy
        sends.append(copy)

    def compute(c):
        a, first, end, _ = chunks[c]
        xi, yi = PAIRS[a]
        rows = arrs[a][0]
        if xi not in got_x:
            swaps_x[xi].wait_recv()
            got_x.add(xi)
        if yi not in got_y:
            swaps_y[yi].wait_recv()
            got_y.add(yi)

        def tile(start, width, offset):
            left = xs[xi][:, core].reshape(half * rows, -1)
            other = xr[xi][...].reshape(half * rows, -1)
            value = dot(left, ys[yi][:, pl.ds(start, width)])
            value = value + dot(other, yr[yi][:, pl.ds(start, width)])
            sums[c][..., pl.ds(offset, width)] = value.astype(BF16).reshape(
                (2,) * (bits - 1) + (rows, width)
            )

        width, step = end - first, 256
        whole = width // step

        @pl.loop(0, whole)
        def _(i):
            tile(
                pl.multiple_of(first + i * step, 128), step, pl.multiple_of(i * step, 128)
            )

        if width % step:
            tile(first + whole * step, width % step, whole * step)
        send(c, 0)

    def receive(c, s):
        a, first, end, order = chunks[c]
        pending[c].wait_recv()
        fixed = order[: s + 1]
        free = [q for q in reversed(range(1, bits)) if q not in fixed]

        def add(j, last):
            here, there, pos = [], [], len(free)
            for q in reversed(range(1, bits)):
                if q in fixed:
                    here.append(mine[q])
                else:
                    pos -= 1
                    value = (j // (1 << pos)) % 2
                    here.append(value)
                    there.append(value)
            part = parts[c * (bits - 1) + s]
            total = part[tuple(there)].astype(F32) + sums[c][tuple(here)].astype(F32)
            if last:
                outs[a][:, first:end] = total
            else:
                sums[c][tuple(here)] = total.astype(BF16)

        if not free:
            add(0, True)
        else:

            @pl.loop(0, 1 << len(free))
            def _(j):
                add(j, False)

            send(c, s + 1)

    small_send(0)
    taken = 0
    for at, (c, s) in enumerate(events):
        if s < 0:
            compute(c)
        else:
            receive(c, s)
            if taken < bits and at % 4 == 0:
                small_receive(taken)
                taken += 1
    for copy in list(swaps_x.values()) + list(swaps_y.values()) + sends:
        copy.wait_send()


def scatter_layer(turned, grads, small, devices, layer):
    bits = devices.bit_length() - 1
    nx, ny = len(turned), len(grads)
    half = devices // 2
    split = [x.reshape(half, 2, x.shape[0] // devices, x.shape[1]) for x in turned]
    arrs = [(turned[xi].shape[0] // devices, grads[yi].shape[1]) for xi, yi in PAIRS]
    scratch = [pltpu.VMEM((half, x.shape[0] // devices, x.shape[1]), BF16) for x in turned]
    scratch += [pltpu.VMEM(y.shape, BF16) for y in grads]
    for a, first, end, _ in RS_CHUNKS:
        scratch.append(pltpu.VMEM((2,) * (bits - 1) + (arrs[a][0], end - first), BF16))
    for a, first, end, _ in RS_CHUNKS:
        for s in range(bits - 1):
            scratch.append(pltpu.VMEM((2,) * (bits - 2 - s) + (arrs[a][0], end - first), BF16))
    scratch += [pltpu.VMEM(small.shape, F32)] * (2 * bits - 1)
    dma = pltpu.SemaphoreType.DMA
    scratch += [dma((nx,))] * 2 + [dma((ny,))] * 2 + [dma((len(RS_CHUNKS), bits - 1))] * 2
    scratch += [dma((bits,))] * 2
    vmem = pl.BlockSpec(memory_space=pltpu.VMEM)
    outs = [jax.ShapeDtypeStruct(shape, F32) for shape in arrs]
    outs.append(jax.ShapeDtypeStruct(small.shape, F32))
    return pl.pallas_call(
        functools.partial(scatter_kernel, devices, arrs, nx, ny),
        out_shape=outs,
        in_specs=[vmem] * (nx + ny + 1),
        out_specs=[vmem] * len(outs),
        scratch_shapes=scratch,
        compiler_params=pltpu.CompilerParams(
            collective_id=1, has_side_effects=True, vmem_limit_bytes=60 * 1024 * 1024
        ),
        name="scatter_layer",
    )(*split, *grads, small)


def scatter_plain(turned, grads, small):
    owned = [
        lax.psum_scatter(
            dot(turned[xi], grads[yi]).astype(BF16), "dp", scatter_dimension=0, tiled=True
        ).astype(F32)
        for xi, yi in PAIRS
    ]
    return owned + [lax.psum(small, "dp")]


def doc_layout(doc_lengths, rows_count):
    rows_index = jnp.arange(rows_count, dtype=jnp.int32)
    doc_ends = jnp.cumsum(doc_lengths, dtype=jnp.int32)
    later = (rows_index[:, None] >= doc_ends[None, :]).astype(jnp.int32)
    segment = jnp.sum(later, axis=1, dtype=jnp.int32)
    position = rows_index - jnp.sum(later * doc_lengths[None, :], axis=1, dtype=jnp.int32)
    return (segment, position)


def causal_conv(channels, kernel, position):
    summed = channels * kernel[TAPS - 1]
    for offset in range(1, TAPS):
        shifted = jnp.pad(channels, ((offset, 0), (0, 0)))[: channels.shape[0]]
        valid = (position >= offset).astype(channels.dtype)
        summed = summed + shifted * kernel[TAPS - 1 - offset] * valid[:, None]
    return summed


def mixer_core(inner, kernel, head_params, position, inside):
    log_rates, skip_coef, step_bias = head_params
    rows_count = inner.shape[0]
    gate_z = inner[:, :INNER]
    conv_in = inner[:, INNER : INNER + CONVCH]
    step_raw = inner[:, INNER + CONVCH :]
    conv_out = jax.nn.silu(causal_conv(conv_in, kernel, position))
    x_heads = conv_out[:, :INNER].reshape(rows_count, HEADS, HDIM)
    b_all = conv_out[:, INNER : INNER + STATE]
    c_all = conv_out[:, INNER + STATE :]
    dt_all = jax.nn.softplus(step_raw + step_bias[None, :])
    rates = -jnp.exp(log_rates)
    cumul = jnp.dot(inside.astype(F32), dt_all * rates[None, :], precision=HIGHEST).T
    gaps = cumul[:, :, None] - cumul[:, None, :]
    decay = jnp.exp(jnp.where(inside[None], jnp.minimum(gaps, 0.0), -1e30))
    affinity = jnp.dot(c_all, b_all.T, precision=HIGHEST)
    scaled = x_heads * dt_all[:, :, None]
    scanned = jnp.einsum("hij,jhp->ihp", decay * affinity[None], scaled, precision=HIGHEST)
    scanned = scanned + skip_coef[None, :, None] * x_heads
    return scanned.reshape(rows_count, INNER) * jax.nn.silu(gate_z)


def rotate(values, cosine, sine):
    front, rear = values[..., : HD // 2], values[..., HD // 2 :]
    return jnp.concatenate([front * cosine - rear * sine, rear * cosine + front * sine], axis=-1)


def attention_forward(packed, tables, inside):
    rows = packed.shape[0]
    cosine, sine = tables
    heads = packed[:, : (QH + KVH) * HD].reshape(rows, QH + KVH, HD)
    turned = rotate(heads, cosine[:, None], sine[:, None]).astype(BF16)
    query = turned[:, :QH].reshape(rows, KVH, QH // KVH, HD)
    key = turned[:, QH:]
    value = packed[:, (QH + KVH) * HD :].astype(BF16).reshape(rows, KVH, HD)
    scores = jnp.einsum("skgd,tkd->kgst", query, key, preferred_element_type=F32) * SCORE_SCALE
    scores = jnp.where(inside[None, None], scores, -1e30)
    expo = jnp.exp(scores - jnp.max(scores, axis=-1, keepdims=True))
    probs = expo / jnp.sum(expo, axis=-1, keepdims=True)
    low = probs.astype(BF16)
    context = jnp.einsum("kgst,tkd->skgd", low, value, preferred_element_type=F32)
    return context.reshape(rows, QH * HD).astype(BF16), (query, key, value, probs, low)


def attention_backward(dcontext, kept, tables):
    query, key, value, probs, low = kept
    rows = dcontext.shape[0]
    cosine, sine = tables
    grad = dcontext.reshape(rows, KVH, QH // KVH, HD)
    dvalue = jnp.einsum("kgst,skgd->tkd", low, grad, preferred_element_type=F32)
    dprobs = jnp.einsum("skgd,tkd->kgst", grad, value, preferred_element_type=F32)
    dscores = probs * (dprobs - jnp.sum(probs * dprobs, axis=-1, keepdims=True))
    dscores = (dscores * SCORE_SCALE).astype(BF16)
    dquery = jnp.einsum("kgst,tkd->skgd", dscores, key, preferred_element_type=F32)
    dkey = jnp.einsum("kgst,skgd->tkd", dscores, query, preferred_element_type=F32)
    both = jnp.concatenate([dquery.reshape(rows, QH, HD), dkey], axis=1)
    both = rotate(both, cosine[:, None], -sine[:, None]).reshape(rows, (QH + KVH) * HD)
    return jnp.concatenate([both, dvalue.reshape(rows, KVH * HD)], axis=1).astype(BF16)


def inverse_rms(values):
    return lax.rsqrt(jnp.mean(values * values, axis=-1, keepdims=True) + EPSILON)


def norm_backward(grad, values, scale, gain):
    normed = values * scale
    grad_gain = jnp.sum(grad * normed, axis=0)
    inner = grad * gain
    return scale * (inner - normed * jnp.mean(inner * normed, axis=-1, keepdims=True)), grad_gain


def layer_forward(hidden, weights, small, heads, layout):
    w_in, w_mix, w_qkv, w_attn, w_gate_up, w_down = weights
    gains, kernel, gain_inner = small
    position, inside, tables = layout
    scale = inverse_rms(hidden)
    normed = (hidden * scale * gains[0]).astype(BF16)
    inner = dot(normed, w_in)
    packed = dot(normed, w_qkv)
    core = functools.partial(mixer_core, position=position, inside=inside)
    gated, pull_core = jax.vjp(core, inner, kernel, heads)
    scale_inner = inverse_rms(gated)
    mixed = (gated * scale_inner * gain_inner).astype(BF16)
    context, kept_attn = attention_forward(packed, tables, inside)
    middle = hidden + dot(mixed, w_mix) + dot(context, w_attn)
    scale_two = inverse_rms(middle)
    normed_two = (middle * scale_two * gains[1]).astype(BF16)
    both = dot(normed_two, w_gate_up)
    active = (jax.nn.silu(both[:, :FF]) * both[:, FF:]).astype(BF16)
    out = middle + dot(active, w_down)
    kept = (
        hidden,
        scale,
        normed,
        pull_core,
        gated,
        scale_inner,
        mixed,
        context,
        kept_attn,
        middle,
        scale_two,
        normed_two,
        both,
        active,
    )
    return out, kept


def layer_backward(grad, kept, weights, small, layout):
    w_in, w_mix, w_qkv, w_attn, w_gate_up, w_down = weights
    gains, kernel, gain_inner = small
    position, inside, tables = layout
    (
        hidden,
        scale,
        normed,
        pull_core,
        gated,
        scale_inner,
        mixed,
        context,
        kept_attn,
        middle,
        scale_two,
        normed_two,
        both,
        active,
    ) = kept
    ddown = grad.astype(BF16)
    dactive = dot_rt(ddown, w_down)
    gate, up = both[:, :FF], both[:, FF:]
    sig = jax.nn.sigmoid(gate)
    dgate = dactive * up * (sig * (1.0 + gate * (1.0 - sig)))
    dboth = jnp.concatenate([dgate, dactive * (gate * sig)], axis=1).astype(BF16)
    dmiddle, dgain_two = norm_backward(dot_rt(dboth, w_gate_up), middle, scale_two, gains[1])
    dmiddle = grad + dmiddle
    dbranch = dmiddle.astype(BF16)
    dgated, dgain_inner = norm_backward(dot_rt(dbranch, w_mix), gated, scale_inner, gain_inner)
    dcontext = dot_rt(dbranch, w_attn).astype(BF16)
    dpacked = attention_backward(dcontext, kept_attn, tables)
    dinner, dkernel, dheads = pull_core(dgated)
    dinner = dinner.astype(BF16)
    dnormed = dot_rt(dinner, w_in) + dot_rt(dpacked, w_qkv)
    dhidden, dgain = norm_backward(dnormed, hidden, scale, gains[0])
    turned = [x.T for x in (normed, mixed, context, normed_two, active)]
    grads = [dinner, dpacked, dbranch, dboth, ddown]
    flat = [dgain, dgain_two, dkernel.reshape(-1), dgain_inner] + list(dheads)
    return dmiddle + dhidden, turned, grads, jnp.concatenate(flat)


def shards(
    tokens,
    cotangent,
    destination,
    lengths,
    norm_gains,
    in_proj,
    conv_weight,
    ssm_gain,
    mixer_out,
    qkv_proj,
    attn_out,
    gate_up,
    down_proj,
    a_log,
    d_skip,
    dt_bias,
):
    devices = lax.axis_size("dp")
    me = lax.axis_index("dp")
    rows_here, width = tokens.shape
    share = rows_here // devices
    own_kernels = devices == 32
    index = jnp.arange(rows_here, dtype=jnp.int32)
    slabs = destination.reshape(devices, rows_here)

    own = lax.dynamic_slice_in_dim(slabs, me, 1, 0)[0] // rows_here
    same = (own[:, None] == own[None, :]) & (index[None, :] < index[:, None])
    slot = own * share + jnp.sum(same.astype(jnp.int32), axis=1)
    leave = (slot[None, :] == index[:, None]).astype(BF16)
    outgoing = [dot(leave, x).astype(BF16) for x in (tokens, cotangent)]

    def exchange(rows):
        split = rows.reshape(devices, share, width)
        moved = lax.all_to_all(split, "dp", split_axis=0, concat_axis=0, tiled=True)
        return moved.reshape(rows_here, width)

    arrived = [exchange(x) for x in outgoing]

    local = slabs - me * rows_here
    mask = ((local >= 0) & (local < rows_here)).astype(BF16)
    below = (index[:, None] < index[None, :]).astype(BF16)
    rank = dot(mask, below).astype(jnp.int32)
    order = rank + share * jnp.arange(devices, dtype=jnp.int32)[:, None]
    hits = local.reshape(-1)[None, :] == index[:, None]
    taken = jnp.sum(jnp.where(hits, order.reshape(-1)[None, :], 0), axis=1)
    enter = (taken[:, None] == index[None, :]).astype(BF16)
    hidden = dot(enter, arrived[0])
    upstream = dot(enter, arrived[1])

    segment, position = doc_layout(lengths[0], rows_here)
    inside = (segment[:, None] == segment[None, :]) & (index[:, None] >= index[None, :])
    inverse = ROPE_BASE ** (-(jnp.arange(HD // 2, dtype=F32) * 2.0 / HD))
    angles = position.astype(F32)[:, None] * inverse[None, :]
    layout = (position, inside, (jnp.cos(angles), jnp.sin(angles)))

    matrices = (in_proj, mixer_out, qkv_proj, attn_out, gate_up, down_proj)
    gain_part, conv_part, inner_part = (x.shape[-1] for x in (norm_gains, conv_weight, ssm_gain))
    packed = jnp.concatenate(
        [norm_gains.reshape(LAYERS, -1), conv_weight.reshape(LAYERS, -1), ssm_gain], axis=1
    )
    used = packed.shape[1]
    if own_kernels:
        room = SMALL_ROWS * 128
        padded = jnp.pad(packed, ((0, 0), (0, room - used))).reshape(LAYERS, SMALL_ROWS, 128)
        gathered = gather_all(list(matrices) + [padded], devices)
        weights = [g[:-1] for g in gathered]
        smalls = [g[-1].reshape(devices, room)[:, :used] for g in gathered]
    else:
        weights = [
            [lax.all_gather(x[layer], "dp", axis=0, tiled=True) for x in matrices]
            for layer in range(LAYERS)
        ]
        every = lax.all_gather(packed, "dp", axis=0)
        smalls = [every[:, layer] for layer in range(LAYERS)]

    def spread(piece, count):
        shaped = piece.reshape(devices, count, -1)
        return jnp.swapaxes(shaped, 0, 1).reshape(count, -1).astype(F32)

    def small_of(layer):
        both = smalls[layer]
        mid = 2 * gain_part
        return (
            spread(both[:, :mid], 2),
            spread(both[:, mid : mid + TAPS * conv_part], TAPS),
            spread(both[:, mid + TAPS * conv_part :], 1)[0],
        )

    params = [small_of(layer) for layer in range(LAYERS)]
    heads = [(a_log[layer], d_skip[layer], dt_bias[layer]) for layer in range(LAYERS)]

    kept = [None] * LAYERS
    for layer in range(LAYERS):
        hidden, kept[layer] = layer_forward(
            hidden, weights[layer], params[layer], heads[layer], layout
        )
    leaving = lax.dot_general(
        enter, hidden.astype(BF16), (((0,), (0,)), ((), ())), preferred_element_type=F32
    ).astype(BF16)

    def come_home(rows):
        moved = exchange(rows)
        return lax.dot_general(
            leave, moved, (((0,), (0,)), ((), ())), preferred_element_type=F32
        )

    out_tokens = come_home(leaving).astype(BF16)

    flowing = upstream
    owned = [None] * LAYERS
    for layer in reversed(range(LAYERS)):
        flowing, turned, grads, flat = layer_backward(
            flowing, kept[layer], weights[layer], params[layer], layout
        )
        count = flat.shape[0]
        lines = -(-count // 1024) * 8
        small = jnp.pad(flat, (0, lines * 128 - count)).reshape(lines, 128)
        if own_kernels:
            owned[layer] = scatter_layer(turned, grads, small, devices, layer)
        else:
            owned[layer] = scatter_plain(turned, grads, small)
    sending = lax.dot_general(
        enter, flowing.astype(BF16), (((0,), (0,)), ((), ())), preferred_element_type=F32
    ).astype(BF16)
    in_grad = come_home(sending)

    big = [jnp.stack([owned[layer][k] for layer in range(LAYERS)]) for k in range(6)]
    totals = jnp.stack([owned[layer][6].reshape(-1) for layer in range(LAYERS)])
    model = gain_part * devices
    sizes = (2 * model, TAPS * CONVCH, INNER, HEADS, HEADS, HEADS)
    pieces, at = [], 0
    for size in sizes:
        pieces.append(totals[:, at : at + size])
        at += size

    def mine(piece, count, part):
        shaped = piece.reshape(LAYERS, count, devices * part)
        return lax.dynamic_slice_in_dim(shaped, me * part, part, 2)

    return (
        out_tokens,
        in_grad,
        mine(pieces[0], 2, gain_part),
        big[0],
        mine(pieces[1], TAPS, conv_part),
        mine(pieces[2], 1, inner_part)[:, 0],
        big[1],
        big[2],
        big[3],
        big[4],
        big[5],
        pieces[3],
        pieces[4],
        pieces[5],
    )


def solution(mesh):
    placed = (
        P("dp", None),
        P("dp", None),
        P(),
        P("dp", None),
        P(None, None, "dp"),
        P(None, "dp", None),
        P(None, None, "dp"),
        P(None, "dp"),
        P(None, "dp", None),
        P(None, "dp", None),
        P(None, "dp", None),
        P(None, "dp", None),
        P(None, "dp", None),
        P(),
        P(),
        P(),
    )
    return jax.shard_map(
        shards,
        mesh=mesh,
        in_specs=placed,
        out_specs=(
            P("dp", None),
            P("dp", None),
            P(None, None, "dp"),
            P(None, "dp", None),
            P(None, None, "dp"),
            P(None, "dp"),
            P(None, "dp", None),
            P(None, "dp", None),
            P(None, "dp", None),
            P(None, "dp", None),
            P(None, "dp", None),
            P(),
            P(),
            P(),
        ),
        check_vma=False,
    )
```

time: 2870 us -> 937 us (0.33)
  waiting for transfers between devices: 2160 us -> 15.8 us
  Pallas kernels: 0 us -> 548 us
  blocking collectives: 207 us -> 0 us
  local copies, waits for them, and re-layouts: 159 us -> 81.7 us
    reduce_scatter x12 -> x0, waiting for transfers between devices: 1500 us -> none  [the longest x2 298 us: shards(): lax.psum_scatter(weight_terms[7], 'dp', scatter_dimension=0, tiled=True)]
    pallas_call x0 -> x3, Pallas kernels: none -> 548 us  [the longest x2 304 us: scatter_layer(): pl.pallas_call(functools.partial(scatter_kernel, devices, arrs, nx, ny),...]
    all_gather x12 -> x0, waiting for transfers between devices: 335 us -> none  [the longest x2 75.9 us: gather_layer(): lax.all_gather(gate_up[layer_idx], 'dp', axis=0, tiled=True)]
    unnamed x30 -> x0, waiting for transfers between devices: 302 us -> none
    all_gather x4 -> x0, blocking collectives: 168 us -> none  [the longest x2 87.2 us: gather_layer(): lax.all_gather(norm_gains[layer_idx], 'dp', axis=1, tiled=True)]
    slice x28 -> x18, local copies, waits for them, and re-layouts: 98.6 us -> 12.7 us  [the longest x4 6.56 us: mixer_core(): x_heads = conv_out[:, :INNER].reshape(rows_count, HEADS, HDIM)]
    unnamed x1 -> x0, blocking collectives: 38.9 us -> none
    dot_general x64 -> x58, matrix products: 199 us -> 179 us  [the longest x6 61.4 us: mixer_core(): jnp.einsum('hij,jhp->ihp', decay * affinity[None], scaled, precision=HIGH...]
  transfers between devices with their start and end apart: 31 -> 4, of which waited for: 24 -> 2; matrix products, arithmetic and copies ran while one was open for 10% -> 13% of each run, Pallas kernels for 0% -> 26%
where the time goes in v2:
time: 937 us; the launch traced here: 930 us
  Pallas kernels  548 us (58%)
  matrix products  183 us (20%)
  local copies, waits for them, and re-layouts  81.7 us (9%)
  other arithmetic  78.5 us (8%)
  starting transfers between devices  20 us (2%)
  waiting for transfers between devices  15.8 us (2%)
    pallas_call x2, Pallas kernels, scatter_layer(): pl.pallas_call(functools.partial(scatter_kernel, devices, arrs, nx, ny),...  304 us
    pallas_call x1, Pallas kernels, gather_all(): pl.pallas_call(functools.partial(gather_kernel, devices, chunks, events,...  244 us
    dot_general x6, matrix products, mixer_core(): jnp.einsum('hij,jhp->ihp', decay * affinity[None], scaled, precision=HIGH...  61.4 us
    dot_general x16, matrix products, dot(): return jnp.dot(left, right, preferred_element_type=F32)  39.2 us
    dot_general x12, matrix products, dot_rt(): lax.dot_general(left, right, (((1,), (1,)), ((), ())), preferred_element_...  29.3 us
    unnamed x422, local copies, waits for them, and re-layouts  21 us
    all_to_all x4, starting transfers between devices, exchange(): moved = lax.all_to_all(split, 'dp', split_axis=0, concat_axis=0, tiled=True)  20 us
  transfers between devices with their start and end apart: 4, of which 2 were waited for; matrix products, arithmetic and copies ran while one was open for 13% of the time, Pallas kernels for 26%

profile of v2, /device:TPU:0, one launch (start us, length us, event | category | flops | bytes accessed | tf_op | source)
XLA Modules:
  0.0 930.3 jit_solution(6750698338939644984)
XLA Ops:
  2.9 7.3 all-to-all-start
  11.1 244.4 %gather_all.1 = (bf16[2,2,2,2,2,32,3352]{6,5,4,3,2,1,0:T(8,128)(2,1)}, bf16[2,2,2,2,2,48,1024]{6,5,4,3,2,1,0:T(8,128)(2,1)}, bf16[2,2,2,2,2,32,768]{6,5,4,3,2,1,...) custom-call(bf16[2,32,3352]{2,1,0:T(8,128)(2,1)} %refs_0_.1, ...), custom_call_target="tpu_custom_call" | custom-call | tf_op jit(solution)/shard_map/gather_all/pallas_call | solution.py:142
  270.5 3.8 all-to-all-start.2
  277.2 5.1 fusion.257
  291.8 9.5 %bitcast_add_fusion.1 = f32[256,24,64]{0,2,1:T(8,128)S(1)} fusion(f32[256,24,64]{0,2,1:T(8,128)} %bitcast.404, f32[256,256]{1,0:T(8,128)S(1)} %fusion.174, f32[24,256]{1,0:T(8,128)S(1)} %fusion.155, pred[256,256]{1,0:T(8,128)(4,1)S(1)} %copy-done.115, f32[24]{0:T(128)S(1)} %copy-done.182, f32[256,24]{0,1:T(8,128)S(1)} %copy.191), kind=kOutput, calls=%fused_computation.145 | convolution fusion | flops 1215430656 | bytes 3522656 | tf_op jit(solution)/shard_map/jvp(hij,jhp->ihp)/dot_general | solution.py:382
  312.4 6.2 fusion.234
  325.1 5.2 fusion.259
  337.7 3.1 copy.199
  342.3 10.5 %bitcast_add_fusion = f32[256,24,64]{0,2,1:T(8,128)} fusion(f32[256,24,64]{0,2,1:T(8,128)} %bitcast.407, f32[256,256]{1,0:T(8,128)S(1)} %fusion.167, f32[24,256]{1,0:T(8,128)S(1)} %fusion.153, pred[256,256]{1,0:T(8,128)(4,1)S(1)} %copy-done.116, f32[24]{0:T(128)S(1)} %copy-done.184, f32[256,24]{0,1:T(8,128)S(1)} %copy.201), kind=kOutput, calls=%fused_computation.144 | convolution fusion | flops 1215430656 | bytes 3522656 | tf_op jit(solution)/shard_map/jvp(hij,jhp->ihp)/dot_general | solution.py:382
  355.9 3.6 multiply_reduce_fusion.14
  363.6 3.5 convolution_add_fusion.4
  367.8 8.1 fusion.236
  377.3 6.5 multiply_convert_fusion.3
  383.8 6.5 fusion.240
  396.6 5.2 fusion.110
  401.8 4.2 convolution_bitcast_fusion.3
  413.1 5.0 multiply_reduce_fusion.8
  421.2 12.2 %fusion.114 = (f32[24,256]{1,0:T(8,128)}, f32[24,256]{1,0:T(8,128)}, f32[256,256]{1,0:T(8,128)S(1)}) fusion(f32[24,256]{1,0:T(8,128)S(1)} %copy-done.196, f32[256,256]{1,0:T(8,128)S(1)} %copy-done.83, pred[256,256]{1,0:T(8,128)(4,1)S(1)} %copy-done.117, f32[24,64,256]{2,1,0:T(8,128)} %bitcast.413, f32[256,24,64]{0,2,1:T(8,128)} %bitcast.408, ...), kind=kOutput, calls=%fused_computation.233 | convolution fusion | flops 1231867904 | bytes 3833856 | tf_op jit(solution)/shard_map/transpose(jvp(hij,jhp->ihp))/dot_general | solution.py:382
  436.7 9.2 fusion.80
  476.9 5.2 multiply_reduce_fusion.10
  485.2 12.3 %fusion.116 = (f32[24,256]{1,0:T(8,128)}, f32[24,256]{1,0:T(8,128)}, f32[256,256]{1,0:T(8,128)S(1)}) fusion(f32[24,256]{1,0:T(8,128)S(1)} %copy-done.193, f32[256,256]{1,0:T(8,128)} %copy-done.79, pred[256,256]{1,0:T(8,128)(4,1)S(1)} %copy-done.118, f32[24,64,256]{2,1,0:T(8,128)} %bitcast.410, f32[256,24,64]{0,2,1:T(8,128)} %bitcast.405, ...), kind=kOutput, calls=%fused_computation.235 | convolution fusion | flops 1231867904 | bytes 3833856 | tf_op jit(solution)/shard_map/transpose(jvp(hij,jhp->ihp))/dot_general | solution.py:382
  506.1 3.8 fusion.112
  509.9 3.7 convolution_bitcast_fusion.1
  522.1 7.7 fusion.78
  529.8 3.2 copy.221
  533.0 10.1 %multiply_reduce_fusion.7 = (f32[1792]{0:T(1024)}, f32[1792]{0:T(1024)}, f32[1792]{0:T(1024)}, f32[1792]{0:T(1024)}, f32[1792]{0:T(1024)S(1)}, /*index=5*/f32[17...) fusion(f32[256,1792]{1,0:T(8,128)} %copy-done.20, f32[256]{0:T(256)S(1)} %copy-done.147, ...), kind=kLoop, calls=%fused_computation.119 | loop fusion | flops 15124480 | bytes 14740480 | tf_op jit(solution)/shard_map/transpose(jvp())/reduce_sum | solution.py:361
  577.6 153.9 %scatter_layer.3 = (f32[32,3352]{1,0:T(8,128)}, f32[48,1024]{1,0:T(8,128)}, f32[32,768]{1,0:T(8,128)}, f32[16,1024]{1,0:T(8,128)}, f32[32,4096]{1,0:T(8,128)}, /*index=5*/f32[64,1024]{1,0:T(8,128)}, f32[88,128]{1,0:T(8,128)}) custom-call(bf16[16,2,32,256]{3,2,1,0:T(8,128)(2,1)} %bitcast.400, bf16[16,2,48,256]{3,2,1,0:T(8,128)(2,1)} %bitcast.396, ...), custom_call_target="tpu_custom_call" | custom-call | tf_op jit(solution)/shard_map/scatter_layer/pallas_call | solution.py:324
  732.8 149.7 %scatter_layer.2 = (f32[32,3352]{1,0:T(8,128)}, f32[48,1024]{1,0:T(8,128)}, f32[32,768]{1,0:T(8,128)}, f32[16,1024]{1,0:T(8,128)}, f32[32,4096]{1,0:T(8,128)}, /*index=5*/f32[64,1024]{1,0:T(8,128)}, f32[88,128]{1,0:T(8,128)}) custom-call(bf16[16,2,32,256]{3,2,1,0:T(8,128)(2,1)} %bitcast.403, bf16[16,2,48,256]{3,2,1,0:T(8,128)(2,1)} %bitcast.397, ...), custom_call_target="tpu_custom_call" | custom-call | tf_op jit(solution)/shard_map/scatter_layer/pallas_call | solution.py:324
  888.9 5.8 all-to-all-start.3
  900.4 4.5 fusion.96
  904.9 5.5 all-to-all-done.3
  918.6 10.3 %all-to-all-done.1 = bf16[32,8,1024]{2,1,0:T(8,128)(2,1)S(1)} async-done(((bf16[32,8,1024]{2,1,0:T(8,128)(2,1)}), bf16[32,8,1024]{2,1,0:T(8,128)(2,1)S(1)}, u32[]{:S(2)}, u32[]{:S(2)}) %all-to-all-start.1) | async-done | bytes 524320 | tf_op jit(solution)/shard_map/all_to_all | solution.py:550
  (638 shorter events, 192.0 us)
Async XLA Ops:
  1.8 258.0 %copy-start.157 = (s32[1,256]{1,0:T(1,128)}, s32[1,256]{1,0:T(1,128)S(1)}, u32[]{:S(2)}) copy-start(s32[1,256]{1,0:T(1,128)S(1)} %multiply_add_fusion.5) | copy-start | bytes 3076
  2.9 254.8 %copy-start.181 = (s32[1,4]{1,0:T(1,128)S(1)}, s32[1,4]{1,0:T(1,128)}, u32[]{:S(2)}) copy-start(s32[1,4]{1,0:T(1,128)} %param.20) | copy-start | bytes 52
  2.9 256.3 %copy-start.178 = (f32[2,24]{1,0:T(2,128)S(1)}, f32[2,24]{1,0:T(2,128)}, u32[]{:S(2)}) copy-start(f32[2,24]{1,0:T(2,128)} %param.31) | copy-start | bytes 580
  2.9 256.9 %copy-start.66 = (bf16[256,1024]{1,0:T(8,128)(2,1)S(1)}, bf16[256,1024]{1,0:T(8,128)(2,1)}, u32[]{:S(2)}) copy-start(bf16[256,1024]{1,0:T(8,128)(2,1)} %param.18) | copy-start | bytes 1572868
  2.9 267.6 %all-to-all-start = ((bf16[32,8,1024]{2,1,0:T(8,128)(2,1)}), bf16[32,8,1024]{2,1,0:T(8,128)(2,1)S(1)}, u32[]{:S(2)}, u32[]{:S(2)}) async-start(bf16[32,8,1024]{2,1,0:T(8,128)(2,1)} %fusion.95), calls=%async_computation | async-start | bytes 1048576 | tf_op jit(solution)/shard_map/all_to_all | solution.py:550
  259.0 15.8 %copy-start.86 = (pred[256,256]{0,1:T(8,128)(4,1)}, pred[256,256]{0,1:T(8,128)(4,1)S(1)}, u32[]{:S(2)}) copy-start(pred[256,256]{0,1:T(8,128)(4,1)S(1)} %fusion.140) | copy-start | bytes 196612
  261.7 15.4 %copy-start.73 = (f32[1024]{0:T(1024)}, f32[1024]{0:T(1024)S(1)}, u32[]{:S(2)}) copy-start(f32[1024]{0:T(1024)S(1)} %mul.1068) | copy-start | bytes 12292
  262.5 21.6 %copy-start.101 = (f32[1792]{0:T(1024)}, f32[1792]{0:T(1024)S(1)}, u32[]{:S(2)}) copy-start(f32[1792]{0:T(1024)S(1)} %mul.1074) | copy-start | bytes 21508
  262.6 21.5 %copy-start.103 = (f32[1792]{0:T(1024)}, f32[1792]{0:T(1024)S(1)}, u32[]{:S(2)}) copy-start(f32[1792]{0:T(1024)S(1)} %mul.1082) | copy-start | bytes 21508
  262.7 21.4 %copy-start.104 = (f32[1792]{0:T(1024)}, f32[1792]{0:T(1024)S(1)}, u32[]{:S(2)}) copy-start(f32[1792]{0:T(1024)S(1)} %mul.1087) | copy-start | bytes 21508
  270.5 105.4 %all-to-all-start.2 = ((bf16[32,8,1024]{2,1,0:T(8,128)(2,1)}), bf16[32,8,1024]{2,1,0:T(8,128)(2,1)}, u32[]{:S(2)}, u32[]{:S(2)}) async-start(bf16[32,8,1024]{2,1,0:T(8,128)(2,1)} %fusion.97), calls=%async_computation.2 | async-start | bytes 1048576 | tf_op jit(solution)/shard_map/all_to_all | solution.py:550
  288.4 19.3 %copy-start.77 = (bf16[256,128]{0,1:T(8,128)(2,1)}, bf16[256,128]{0,1:T(8,128)(2,1)S(1)}, u32[]{:S(2)}) copy-start(bf16[256,128]{0,1:T(8,128)(2,1)S(1)} %copy.195) | copy-start | bytes 196612
  325.0 36.6 %copy-start.84 = (bf16[256,8,64]{0,2,1:T(8,128)(2,1)}, bf16[256,8,64]{0,2,1:T(8,128)(2,1)S(1)}, u32[]{:S(2)}) copy-start(bf16[256,8,64]{0,2,1:T(8,128)(2,1)S(1)} %pad_maximum_fusion.12) | copy-start | bytes 786436
  325.0 34.4 %copy-start.123 = (bf16[256,2,64,1]{0,2,3,1:T(8,128)(2,1)}, bf16[256,2,64,1]{0,2,3,1:T(8,128)(2,1)S(1)}, u32[]{:S(2)}) copy-start(bf16[256,2,64,1]{0,2,3,1:T(8,128)(2,1)S(1)} %maximum_bitcast_fusion) | copy-start | bytes 196612
  367.6 24.4 %copy-start.9 = (f32[256,1024]{1,0:T(8,128)}, f32[256,1024]{1,0:T(8,128)S(1)}, u32[]{:S(2)}) copy-start(f32[256,1024]{1,0:T(8,128)S(1)} %get-tuple-element.209) | copy-start | bytes 3145732
  421.1 15.1 %copy-start.64 = (f32[256,32]{0,1:T(8,128)S(1)}, f32[256,32]{0,1:T(8,128)}, u32[]{:S(2)}) copy-start(f32[256,32]{0,1:T(8,128)} %copy-done.63) | copy-start | bytes 98308
  421.1 15.1 %copy-start.67 = (f32[2,64,4,256]{3,1,2,0:T(8,128)S(1)}, f32[2,64,4,256]{3,1,2,0:T(8,128)}, u32[]{:S(2)}) copy-start(f32[2,64,4,256]{3,1,2,0:T(8,128)} %fusion.110) | copy-start | bytes 1572868
  421.2 15.1 %copy-start.75 = (f32[256,32]{0,1:T(8,128)S(1)}, f32[256,32]{0,1:T(8,128)}, u32[]{:S(2)}) copy-start(f32[256,32]{0,1:T(8,128)} %get-tuple-element.182) | copy-start | bytes 98308
  472.1 32.8 %copy-start.28 = (bf16[256,1024]{1,0:T(8,128)(2,1)}, bf16[256,1024]{1,0:T(8,128)(2,1)S(1)}, u32[]{:S(2)}) copy-start(bf16[256,1024]{1,0:T(8,128)(2,1)S(1)} %get-tuple-element.131.refs_7_) | copy-start | bytes 1572868
  485.2 16.4 %copy-start.56 = (bf16[256,2048]{1,0:T(8,128)(2,1)S(1)}, bf16[256,2048]{1,0:T(8,128)(2,1)}, u32[]{:S(2)}) copy-start(bf16[256,2048]{1,0:T(8,128)(2,1)} %copy-done.55) | copy-start | bytes 3145732
  485.2 16.4 %copy-start.58 = (bf16[256,2048]{1,0:T(8,128)(2,1)S(1)}, bf16[256,2048]{1,0:T(8,128)(2,1)}, u32[]{:S(2)}) copy-start(bf16[256,2048]{1,0:T(8,128)(2,1)} %copy-done.57) | copy-start | bytes 3145732
  533.0 15.2 %copy-start.148 = (f32[1536]{0:T(1024)S(1)}, f32[1536]{0:T(1024)}, u32[]{:S(2)}) copy-start(f32[1536]{0:T(1024)} %get-tuple-element.90) | copy-start | bytes 18436
  533.0 15.2 %copy-start.167 = (f32[1024]{0:T(1024)S(1)}, f32[1024]{0:T(1024)}, u32[]{:S(2)}) copy-start(f32[1024]{0:T(1024)} %get-tuple-element.94) | copy-start | bytes 12292
  533.0 16.6 %copy-start.48 = (bf16[1024,256]{0,1:T(8,128)(2,1)S(1)}, bf16[1024,256]{0,1:T(8,128)(2,1)}, u32[]{:S(2)}) copy-start(bf16[1024,256]{0,1:T(8,128)(2,1)} %fusion.341) | copy-start | bytes 1572868
  732.8 149.8 %copy-start.65 = (f32[88,128]{1,0:T(8,128)S(1)}, f32[88,128]{1,0:T(8,128)}, u32[]{:S(2)}) copy-start(f32[88,128]{1,0:T(8,128)} %get-tuple-element.65) | copy-start | bytes 135172
  732.8 154.7 %copy-start.172 = (f32[256]{0:T(256)S(1)}, f32[256]{0:T(256)}, u32[]{:S(2)}) copy-start(f32[256]{0:T(256)} %get-tuple-element.101) | copy-start | bytes 3076
  732.8 154.7 %copy-start.37 = (f32[256,1024]{1,0:T(8,128)S(1)}, f32[256,1024]{1,0:T(8,128)}, u32[]{:S(2)}) copy-start(f32[256,1024]{1,0:T(8,128)} %get-tuple-element.132) | copy-start | bytes 3145732
  732.8 154.7 %copy-start.166 = (s32[256]{0:T(256)S(1)}, s32[256]{0:T(256)}, u32[]{:S(2)}) copy-start(s32[256]{0:T(256)} %copy-done.164) | copy-start | bytes 3076
  888.9 21.5 %all-to-all-start.3 = ((bf16[32,8,1024]{2,1,0:T(8,128)(2,1)}), bf16[32,8,1024]{2,1,0:T(8,128)(2,1)S(1)}, u32[]{:S(2)}, u32[]{:S(2)}) async-start(bf16[32,8,1024]{2,1,0:T(8,128)(2,1)} %fusion.98), calls=%async_computation.3 | async-start | bytes 1048576 | tf_op jit(solution)/shard_map/all_to_all | solution.py:550
  900.3 14.3 %copy-start.95 = (f32[48,1024]{1,0:T(8,128)S(1)}, f32[48,1024]{1,0:T(8,128)}, u32[]{:S(2)}) copy-start(f32[48,1024]{1,0:T(8,128)} %get-tuple-element.69) | copy-start | bytes 589828
  900.4 14.3 %copy-start.96 = (f32[48,1024]{1,0:T(8,128)S(1)}, f32[48,1024]{1,0:T(8,128)}, u32[]{:S(2)}) copy-start(f32[48,1024]{1,0:T(8,128)} %get-tuple-element.68) | copy-start | bytes 589828
  910.3 18.6 %all-to-all-start.1 = ((bf16[32,8,1024]{2,1,0:T(8,128)(2,1)}), bf16[32,8,1024]{2,1,0:T(8,128)(2,1)S(1)}, u32[]{:S(2)}, u32[]{:S(2)}) async-start(bf16[32,8,1024]{2,1,0:T(8,128)(2,1)} %fusion.96), calls=%async_computation.1 | async-start | bytes 1048576 | tf_op jit(solution)/shard_map/all_to_all | solution.py:550
  (181 other events, 703.7 us)

commit v3 on v2

--- a/solution.py
+++ b/solution.py
@@ -26,12 +26,13 @@
 BF16 = jnp.bfloat16
 MESH = pl.DeviceIdType.MESH
 
-AG_CHUNKS = [(1, 3, (4, 3, 1, 2)), (0, 2, (1, 4, 3, 2)), (0, 3, (4, 3, 2, 1)), (0, 5, (2, 4, 3, 1)), (0, 0, (4, 3, 2, 1)), (1, 2, (1, 4, 3, 2)), (1, 1, (4, 3, 1, 2)), (1, 5, (4, 3, 1, 2)), (0, 4, (2, 1, 4, 3)), (1, 4, (4, 3, 1, 2)), (0, 1, (2, 1, 4, 3)), (1, 0, (4, 3, 2, 1))]
-AG_EVENTS = [(1, 0), (0, 0), (5, 0), (2, 0), (3, 0), (8, 0), (10, 0), (4, 0), (6, 0), (7, 0), (8, 1), (0, 1), (10, 1), (2, 1), (0, 2), (9, 0), (2, 2), (0, 3), (2, 3), (11, 0), (4, 1), (1, 1), (6, 1), (5, 1), (7, 1), (6, 2), (3, 1), (4, 2), (7, 2), (6, 3), (9, 1), (7, 3), (11, 1), (4, 3), (8, 2), (1, 2), (5, 2), (10, 2), (3, 2), (11, 2), (9, 2), (1, 3), (5, 3), (3, 3), (8, 3), (10, 3), (9, 3), (11, 3)]
-RS_CHUNKS = [(0, 0, 1792, (1, 2, 3, 4)), (1, 0, 512, (2, 3, 4, 1)), (2, 384, 768, (2, 3, 4, 1)), (0, 1792, 3352, (3, 4, 1, 2)), (4, 2048, 4096, (1, 2, 3, 4)), (5, 0, 512, (1, 2, 3, 4)), (5, 512, 1024, (1, 2, 3, 4)), (4, 0, 2048, (2, 3, 4, 1)), (3, 512, 1024, (3, 4, 1, 2)), (1, 512, 1024, (1, 2, 3, 4)), (2, 0, 384, (2, 1, 3, 4)), (3, 0, 512, (1, 2, 3, 4))]
-RS_EVENTS = [(0, -1), (1, -1), (2, -1), (3, -1), (4, -1), (5, -1), (6, -1), (7, -1), (8, -1), (9, -1), (10, -1), (11, -1), (1, 0), (2, 0), (0, 0), (3, 0), (8, 0), (1, 1), (2, 1), (7, 0), (10, 0), (3, 1), (4, 0), (8, 1), (1, 2), (2, 2), (0, 1), (5, 0), (7, 1), (0, 2), (4, 1), (6, 0), (5, 1), (7, 2), (4, 2), (0, 3), (9, 0), (6, 1), (5, 2), (11, 0), (10, 1), (9, 1), (4, 3), (6, 2), (11, 1), (3, 2), (8, 2), (10, 2), (5, 3), (1, 3), (2, 3), (9, 2), (6, 3), (3, 3), (10, 3), (11, 2), (7, 3), (8, 3), (9, 3), (11, 3)]
+AG_CHUNKS = [(0, 6, (4, 3, 2, 1)), (1, 6, (4, 3, 2, 1)), (0, 1, (4, 3, 2, 1)), (1, 3, (4, 3, 1, 2)), (0, 2, (2, 4, 3, 1)), (1, 2, (4, 3, 1, 2)), (0, 5, (4, 3, 2, 1)), (1, 5, (1, 4, 3, 2)), (0, 3, (1, 2, 4, 3)), (0, 0, (1, 4, 3, 2)), (1, 1, (4, 3, 1, 2)), (1, 4, (1, 2, 4, 3)), (1, 0, (4, 3, 2, 1)), (0, 4, (4, 3, 2, 1))]
+AG_EVENTS = [(0, 0), (1, 0), (4, 0), (7, 0), (8, 0), (2, 0), (3, 0), (8, 1), (5, 0), (9, 0), (6, 0), (11, 0), (10, 0), (0, 1), (1, 1), (12, 0), (11, 1), (0, 2), (1, 2), (2, 1), (3, 1), (0, 3), (1, 3), (5, 1), (3, 2), (13, 0), (2, 2), (4, 1), (5, 2), (3, 3), (6, 1), (7, 1), (10, 1), (5, 3), (8, 2), (2, 3), (12, 1), (6, 2), (10, 2), (9, 1), (12, 2), (6, 3), (13, 1), (4, 2), (10, 3), (7, 2), (8, 3), (11, 2), (13, 2), (12, 3), (4, 3), (9, 2), (7, 3), (13, 3), (11, 3), (9, 3)]
+RS_CHUNKS = [(3, 512, 1024, (2, 1, 3, 4)), (4, 2048, 4096, (3, 4, 1, 2)), (5, 512, 1024, (2, 3, 4, 1)), (4, 0, 2048, (1, 2, 3, 4)), (1, 512, 1024, (2, 1, 3, 4)), (0, 0, 1792, (1, 2, 3, 4)), (0, 1792, 3352, (1, 2, 3, 4)), (3, 0, 512, (2, 1, 3, 4)), (1, 0, 512, (1, 2, 3, 4)), (5, 0, 512, (2, 3, 4, 1)), (2, 384, 768, (1, 2, 3, 4)), (2, 0, 384, (2, 3, 4, 1))]
+RS_EVENTS = [(0, -1), (1, -1), (2, -1), (3, -1), (4, -1), (5, -1), (6, -1), (7, -1), (8, -1), (9, -1), (10, -1), (11, -1), (-1, 0), (0, 0), (-2, 0), (2, 0), (4, 0), (1, 0), (7, 0), (3, 0), (2, 1), (9, 0), (11, 0), (-2, 1), (5, 0), (9, 1), (11, 1), (1, 1), (-2, 2), (2, 2), (3, 1), (9, 2), (6, 0), (11, 2), (5, 1), (3, 2), (8, 0), (-2, 3), (6, 1), (10, 0), (5, 2), (-2, 4), (-1, 1), (0, 1), (8, 1), (3, 3), (10, 1), (4, 1), (-1, 2), (6, 2), (7, 1), (5, 3), (0, 2), (8, 2), (1, 2), (10, 2), (2, 3), (4, 2), (6, 3), (9, 3), (0, 3), (-1, 3), (11, 3), (8, 3), (7, 2), (1, 3), (10, 3), (4, 3), (-1, 4), (7, 3)]
 
 SMALL_ROWS = 16
+ROW_BITS = (1, 2, 3, 4, 0)
 
 
 def dot(left, right):
@@ -125,22 +126,14 @@
 def gather_all(shards, devices):
     bits = devices.bit_length() - 1
     layers = shards[0].shape[0]
-    chunks = list(AG_CHUNKS)
-    events = list(AG_EVENTS)
-    extra = len(shards) - 1
-    for layer in range(layers):
-        c = len(chunks)
-        chunks.append((layer, extra, (4, 3, 2, 1)))
-        for s in range(bits - 1):
-            events.insert(3 + layer + 6 * s, (c, s))
-    n = len(chunks)
+    n = len(AG_CHUNKS)
     outs = [
         jax.ShapeDtypeStruct((2,) * bits + s.shape[1:], s.dtype)
         for _ in range(layers)
         for s in shards
     ]
     res = pl.pallas_call(
-        functools.partial(gather_kernel, devices, chunks, events, layers, len(shards)),
+        functools.partial(gather_kernel, devices, AG_CHUNKS, AG_EVENTS, layers, len(shards)),
         out_shape=outs,
         in_specs=[pl.BlockSpec(memory_space=pltpu.VMEM)] * len(shards),
         out_specs=[pl.BlockSpec(memory_space=pl.ANY)] * len(outs),
@@ -163,12 +156,13 @@
     half = devices // 2
     na, nc = len(arrs), len(chunks)
     groups, at = [], 0
-    for size in (nx, ny, 1, na, 1, nx, ny, nc, nc * (bits - 1), bits - 1, bits):
+    for size in (nx, ny, 2, na, 2, nx, ny, nc, nc * (bits - 1), bits - 1, bits, bits):
         groups.append(refs[at : at + size])
         at += size
-    xs, ys, small, outs, small_out, xr, yr, sums, parts, small_mid, small_got = groups
-    small, small_out = small[0], small_out[0]
-    xs_s, xs_r, ys_s, ys_r, st_s, st_r, sm_s, sm_r = refs[at:]
+    xs, ys, extra, outs, extra_out, xr, yr, sums, parts, small_mid, small_got, rows_got = groups
+    small, rows_in = extra
+    small_out, rows_out = extra_out
+    xs_s, xs_r, ys_s, ys_r, st_s, st_r, sm_s, sm_r, ro_s, ro_r = refs[at:]
     me = lax.axis_index("dp")
     mine = [(me // (1 << b)) % 2 for b in range(bits)]
     greet(me, bits)
@@ -202,6 +196,36 @@
             small_send(s + 1)
         else:
             small_out[...] = total
+
+    def rows_index(s, j):
+        index, pos = [], bits - 1
+        for q in reversed(range(bits)):
+            if q == ROW_BITS[s]:
+                index.append(1 - mine[q])
+            else:
+                pos -= 1
+                index.append((j // (1 << pos)) % 2)
+        return tuple(index)
+
+    def rows_send(s):
+        bit = ROW_BITS[s]
+        index = tuple(1 - mine[q] if q == bit else slice(None) for q in reversed(range(bits)))
+        copy = remote(me, rows_out.at[index], rows_got[s], ro_s.at[s], ro_r.at[s], bit)
+        copy.start()
+        pending["rows"] = copy
+
+    def rows_receive(s):
+        pending["rows"].wait_send()
+        pending["rows"].wait_recv()
+
+        @pl.loop(0, 1 << (bits - 1))
+        def _(j):
+            index = rows_index(s, j)
+            there = tuple(index[k] for k in range(bits) if k != bits - 1 - ROW_BITS[s])
+            rows_out[index] = rows_got[s][there]
+
+        if s + 1 < bits:
+            rows_send(s + 1)
 
     def send(c, s):
         order = chunks[c][3]
@@ -288,21 +312,24 @@
             send(c, s + 1)
 
     small_send(0)
-    taken = 0
-    for at, (c, s) in enumerate(events):
-        if s < 0:
+    rows_out[...] = rows_in[...]
+    rows_send(0)
+    for c, s in events:
+        if c == -1:
+            small_receive(s)
+        elif c == -2:
+            rows_receive(s)
+        elif s < 0:
             compute(c)
         else:
             receive(c, s)
-            if taken < bits and at % 4 == 0:
-                small_receive(taken)
-                taken += 1
     for copy in list(swaps_x.values()) + list(swaps_y.values()) + sends:
         copy.wait_send()
 
 
-def scatter_layer(turned, grads, small, devices, layer):
+def scatter_layer(turned, grads, small, rows, devices):
     bits = devices.bit_length() - 1
+    moved = rows.reshape((2,) * bits + (rows.shape[0] // devices, rows.shape[1]))
     nx, ny = len(turned), len(grads)
     half = devices // 2
     split = [x.reshape(half, 2, x.shape[0] // devices, x.shape[1]) for x in turned]
@@ -315,23 +342,26 @@
         for s in range(bits - 1):
             scratch.append(pltpu.VMEM((2,) * (bits - 2 - s) + (arrs[a][0], end - first), BF16))
     scratch += [pltpu.VMEM(small.shape, F32)] * (2 * bits - 1)
+    scratch += [pltpu.VMEM(moved.shape[1:], BF16)] * bits
     dma = pltpu.SemaphoreType.DMA
     scratch += [dma((nx,))] * 2 + [dma((ny,))] * 2 + [dma((len(RS_CHUNKS), bits - 1))] * 2
-    scratch += [dma((bits,))] * 2
+    scratch += [dma((bits,))] * 4
     vmem = pl.BlockSpec(memory_space=pltpu.VMEM)
     outs = [jax.ShapeDtypeStruct(shape, F32) for shape in arrs]
     outs.append(jax.ShapeDtypeStruct(small.shape, F32))
-    return pl.pallas_call(
+    outs.append(jax.ShapeDtypeStruct(moved.shape, BF16))
+    *owned, back = pl.pallas_call(
         functools.partial(scatter_kernel, devices, arrs, nx, ny),
         out_shape=outs,
-        in_specs=[vmem] * (nx + ny + 1),
+        in_specs=[vmem] * (nx + ny + 2),
         out_specs=[vmem] * len(outs),
         scratch_shapes=scratch,
         compiler_params=pltpu.CompilerParams(
             collective_id=1, has_side_effects=True, vmem_limit_bytes=60 * 1024 * 1024
         ),
         name="scatter_layer",
-    )(*split, *grads, small)
+    )(*split, *grads, small, moved)
+    return owned, back.reshape(rows.shape)
 
 
 def scatter_plain(turned, grads, small):
@@ -353,73 +383,393 @@
     return (segment, position)
 
 
-def causal_conv(channels, kernel, position):
-    summed = channels * kernel[TAPS - 1]
+PAIRS_OF_HEADS = HEADS // 2
+LANES = 128
+VMEM = pl.BlockSpec(memory_space=pltpu.VMEM)
+BIG = pltpu.CompilerParams(vmem_limit_bytes=56 * 1024 * 1024)
+
+
+def dot_exact(left, right):
+    return jnp.dot(left, right, preferred_element_type=F32, precision=HIGHEST)
+
+
+def dot_rt_exact(left, right):
+    return lax.dot_general(
+        left, right, (((1,), (1,)), ((), ())), preferred_element_type=F32, precision=HIGHEST
+    )
+
+
+def sigmoid(x):
+    return 1.0 / (1.0 + jnp.exp(-x))
+
+
+def column_index(shape):
+    return lax.broadcasted_iota(jnp.int32, shape, len(shape) - 1)
+
+
+def shifted_down(values, offset, position):
+    return jnp.where(position >= offset, pltpu.roll(values, offset, 0), 0.0)
+
+
+def conv_before(conv_in, taps, position):
+    total = conv_in * taps[TAPS - 1 : TAPS]
     for offset in range(1, TAPS):
-        shifted = jnp.pad(channels, ((offset, 0), (0, 0)))[: channels.shape[0]]
-        valid = (position >= offset).astype(channels.dtype)
-        summed = summed + shifted * kernel[TAPS - 1 - offset] * valid[:, None]
-    return summed
-
-
-def mixer_core(inner, kernel, head_params, position, inside):
-    log_rates, skip_coef, step_bias = head_params
-    rows_count = inner.shape[0]
-    gate_z = inner[:, :INNER]
-    conv_in = inner[:, INNER : INNER + CONVCH]
-    step_raw = inner[:, INNER + CONVCH :]
-    conv_out = jax.nn.silu(causal_conv(conv_in, kernel, position))
-    x_heads = conv_out[:, :INNER].reshape(rows_count, HEADS, HDIM)
-    b_all = conv_out[:, INNER : INNER + STATE]
-    c_all = conv_out[:, INNER + STATE :]
-    dt_all = jax.nn.softplus(step_raw + step_bias[None, :])
-    rates = -jnp.exp(log_rates)
-    cumul = jnp.dot(inside.astype(F32), dt_all * rates[None, :], precision=HIGHEST).T
-    gaps = cumul[:, :, None] - cumul[:, None, :]
-    decay = jnp.exp(jnp.where(inside[None], jnp.minimum(gaps, 0.0), -1e30))
-    affinity = jnp.dot(c_all, b_all.T, precision=HIGHEST)
-    scaled = x_heads * dt_all[:, :, None]
-    scanned = jnp.einsum("hij,jhp->ihp", decay * affinity[None], scaled, precision=HIGHEST)
-    scanned = scanned + skip_coef[None, :, None] * x_heads
-    return scanned.reshape(rows_count, INNER) * jax.nn.silu(gate_z)
-
-
-def rotate(values, cosine, sine):
-    front, rear = values[..., : HD // 2], values[..., HD // 2 :]
-    return jnp.concatenate([front * cosine - rear * sine, rear * cosine + front * sine], axis=-1)
-
-
-def attention_forward(packed, tables, inside):
-    rows = packed.shape[0]
-    cosine, sine = tables
-    heads = packed[:, : (QH + KVH) * HD].reshape(rows, QH + KVH, HD)
-    turned = rotate(heads, cosine[:, None], sine[:, None]).astype(BF16)
-    query = turned[:, :QH].reshape(rows, KVH, QH // KVH, HD)
-    key = turned[:, QH:]
-    value = packed[:, (QH + KVH) * HD :].astype(BF16).reshape(rows, KVH, HD)
-    scores = jnp.einsum("skgd,tkd->kgst", query, key, preferred_element_type=F32) * SCORE_SCALE
-    scores = jnp.where(inside[None, None], scores, -1e30)
-    expo = jnp.exp(scores - jnp.max(scores, axis=-1, keepdims=True))
-    probs = expo / jnp.sum(expo, axis=-1, keepdims=True)
-    low = probs.astype(BF16)
-    context = jnp.einsum("kgst,tkd->skgd", low, value, preferred_element_type=F32)
-    return context.reshape(rows, QH * HD).astype(BF16), (query, key, value, probs, low)
-
-
-def attention_backward(dcontext, kept, tables):
-    query, key, value, probs, low = kept
-    rows = dcontext.shape[0]
-    cosine, sine = tables
-    grad = dcontext.reshape(rows, KVH, QH // KVH, HD)
-    dvalue = jnp.einsum("kgst,skgd->tkd", low, grad, preferred_element_type=F32)
-    dprobs = jnp.einsum("skgd,tkd->kgst", grad, value, preferred_element_type=F32)
-    dscores = probs * (dprobs - jnp.sum(probs * dprobs, axis=-1, keepdims=True))
-    dscores = (dscores * SCORE_SCALE).astype(BF16)
-    dquery = jnp.einsum("kgst,tkd->skgd", dscores, key, preferred_element_type=F32)
-    dkey = jnp.einsum("kgst,skgd->tkd", dscores, query, preferred_element_type=F32)
-    both = jnp.concatenate([dquery.reshape(rows, QH, HD), dkey], axis=1)
-    both = rotate(both, cosine[:, None], -sine[:, None]).reshape(rows, (QH + KVH) * HD)
-    return jnp.concatenate([both, dvalue.reshape(rows, KVH * HD)], axis=1).astype(BF16)
+        total = total + shifted_down(conv_in, offset, position) * taps[
+            TAPS - 1 - offset : TAPS - offset
+        ]
+    return total
+
+
+def mixer_setup(inner_ref, taps_ref, heads_ref, position, inside, x_ref, qcol, qrow, dtpair):
+    rows = inner_ref.shape[0]
+
+    @pl.loop(0, CONVCH // LANES)
+    def _(k):
+        at = pl.multiple_of(k * LANES, LANES)
+        before = conv_before(
+            inner_ref[:, pl.ds(pl.multiple_of(INNER + at, LANES), LANES)],
+            taps_ref[:, pl.ds(at, LANES)],
+            position,
+        )
+        x_ref[:, pl.ds(at, LANES)] = before * sigmoid(before)
+
+    raw = inner_ref[:, INNER + CONVCH :] + heads_ref[2:3, :HEADS]
+    step = jnp.maximum(raw, 0.0) + jnp.log1p(jnp.exp(-jnp.abs(raw)))
+    rates = -jnp.exp(heads_ref[0:1, :HEADS])
+    sums = dot_exact(inside, step * rates)
+    wide = jnp.concatenate([sums, jnp.zeros((rows, LANES - HEADS), F32)], axis=1)
+    qrow[...] = wide.T[: qrow.shape[0]]
+    first = column_index((rows, LANES)) < HDIM
+    for p in range(PAIRS_OF_HEADS):
+        both = []
+        for h in (2 * p, 2 * p + 1):
+            qcol[h] = jnp.broadcast_to(sums[:, h : h + 1], (rows, LANES))
+            both.append(jnp.broadcast_to(step[:, h : h + 1], (rows, LANES)))
+        dtpair[p] = jnp.where(first, both[0], both[1])
+    return raw, step, rates
+
+
+def mixer_forward_kernel(
+    inner_ref, taps_ref, heads_ref, skip_ref, gain_ref, position_ref, inside_ref,
+    mixed_ref, turned_ref, y_ref, x_ref, qcol, qrow, dtpair, aff_ref,
+):
+    rows = inner_ref.shape[0]
+    position = position_ref[...]
+    inside = inside_ref[...]
+    mixer_setup(inner_ref, taps_ref, heads_ref, position, inside, x_ref, qcol, qrow, dtpair)
+    b_all = x_ref[:, INNER : INNER + STATE]
+    c_all = x_ref[:, INNER + STATE :]
+    aff_ref[...] = dot_rt_exact(c_all, b_all) * inside
+    first = column_index((rows, LANES)) < HDIM
+
+    def pair(p, total):
+        at = pl.multiple_of(p * LANES, LANES)
+        x = x_ref[:, pl.ds(at, LANES)]
+        scaled = (x * dtpair[p]).astype(BF16)
+        outs = []
+        for k in (0, 1):
+            h = 2 * p + k
+            column = qcol[h]
+            gaps = jnp.concatenate([column, column], axis=1) - qrow[pl.ds(h, 1), :]
+            prod = jnp.exp(jnp.minimum(gaps, 0.0)) * aff_ref[...]
+            outs.append(dot(prod.astype(BF16), scaled))
+        y = jnp.where(first, outs[0], outs[1]) + x * skip_ref[:, pl.ds(at, LANES)]
+        y_ref[:, pl.ds(at, LANES)] = y
+        z = inner_ref[:, pl.ds(at, LANES)]
+        w = y * (z * sigmoid(z))
+        return total + jnp.sum(w * w, axis=1, keepdims=True)
+
+    total = lax.fori_loop(0, PAIRS_OF_HEADS, pair, jnp.zeros((rows, 1), F32))
+    scale = lax.rsqrt(total / INNER + EPSILON)
+
+    @pl.loop(0, PAIRS_OF_HEADS)
+    def _(p):
+        at = pl.multiple_of(p * LANES, LANES)
+        z = inner_ref[:, pl.ds(at, LANES)]
+        w = y_ref[:, pl.ds(at, LANES)] * (z * sigmoid(z))
+        mixed = w * scale * gain_ref[:, pl.ds(at, LANES)]
+        mixed_ref[:, pl.ds(at, LANES)] = mixed.astype(BF16)
+        turned_ref[pl.ds(at, LANES), :] = mixed.T.astype(BF16)
+
+
+def mixer_scratch(rows):
+    return [
+        pltpu.VMEM((rows, CONVCH), F32),
+        pltpu.VMEM((HEADS, rows, LANES), F32),
+        pltpu.VMEM((HEADS, rows), F32),
+        pltpu.VMEM((PAIRS_OF_HEADS, rows, LANES), F32),
+        pltpu.VMEM((rows, rows), F32),
+    ]
+
+
+def mixer_forward(inner, taps, heads, skip, gain, position, inside):
+    rows = inner.shape[0]
+    shape = jax.ShapeDtypeStruct
+    return pl.pallas_call(
+        mixer_forward_kernel,
+        out_shape=[
+            shape((rows, INNER), BF16),
+            shape((INNER, rows), BF16),
+            shape((rows, INNER), F32),
+        ],
+        in_specs=[VMEM] * 7,
+        out_specs=[VMEM] * 3,
+        scratch_shapes=mixer_scratch(rows),
+        compiler_params=BIG,
+        name="mixer_forward",
+    )(inner, taps, heads, skip, gain, position, inside)
+
+
+def mixer_backward_kernel(
+    inner_ref, taps_ref, heads_ref, skip_ref, gain_ref, position_ref, inside_ref, y_ref, dmixed_ref,
+    dinner_ref, dtaps_ref, dgain_ref, dskip_ref, dheads_ref,
+    x_ref, qcol, qrow, dtpair, aff_ref, dx_ref, daff_ref, rowsum, stepgrad, colsum,
+):
+    rows = inner_ref.shape[0]
+    position = position_ref[...]
+    inside = inside_ref[...]
+    raw, step, rates = mixer_setup(
+        inner_ref, taps_ref, heads_ref, position, inside, x_ref, qcol, qrow, dtpair
+    )
+    turned_inside = inside.T
+    aff_ref[...] = (
+        dot_rt_exact(x_ref[:, INNER : INNER + STATE], x_ref[:, INNER + STATE :]) * turned_inside
+    )
+    daff_ref[...] = jnp.zeros_like(daff_ref)
+    stepgrad[...] = jnp.zeros_like(stepgrad)
+    colsum[...] = jnp.zeros_like(colsum)
+    lane = column_index((rows, LANES))
+    first = lane < HDIM
+
+    def sums(p, carry):
+        squares, product = carry
+        at = pl.multiple_of(p * LANES, LANES)
+        z = inner_ref[:, pl.ds(at, LANES)]
+        w = y_ref[:, pl.ds(at, LANES)] * (z * sigmoid(z))
+        g = dmixed_ref[:, pl.ds(at, LANES)] * gain_ref[:, pl.ds(at, LANES)]
+        return (
+            squares + jnp.sum(w * w, axis=1, keepdims=True),
+            product + jnp.sum(w * g, axis=1, keepdims=True),
+        )
+
+    zero = jnp.zeros((rows, 1), F32)
+    squares, product = lax.fori_loop(0, PAIRS_OF_HEADS, sums, (zero, zero))
+    scale = lax.rsqrt(squares / INNER + EPSILON)
+    pull = scale * scale * scale * product / INNER
+
+    @pl.loop(0, PAIRS_OF_HEADS)
+    def _(p):
+        at = pl.multiple_of(p * LANES, LANES)
+        here = pl.ds(at, LANES)
+        z = inner_ref[:, here]
+        y = y_ref[:, here]
+        sig = sigmoid(z)
+        silu = z * sig
+        w = y * silu
+        g = dmixed_ref[:, here]
+        dgain_ref[:, here] = jnp.sum(g * w * scale, axis=0, keepdims=True)
+        dw = scale * (g * gain_ref[:, here]) - w * pull
+        dinner_ref[:, here] = (dw * y * (sig * (1.0 + z * (1.0 - sig)))).astype(BF16)
+        dy = dw * silu
+        x = x_ref[:, here]
+        dskip_ref[:, here] = jnp.sum(dy * x, axis=0, keepdims=True)
+        steps = dtpair[p]
+        scaled = x * steps
+        low = dy.astype(BF16)
+        outs = []
+        for k in (0, 1):
+            h = 2 * p + k
+            column = qcol[h]
+            gaps = qrow[pl.ds(h, 1), :] - jnp.concatenate([column, column], axis=1)
+            decay = jnp.exp(jnp.minimum(gaps, 0.0))
+            prod = decay * aff_ref[...]
+            own = first if k == 0 else jnp.logical_not(first)
+            dprod = dot_rt(jnp.where(own, scaled, 0.0).astype(BF16), low)
+            daff_ref[...] += dprod * decay
+            both = dprod * prod
+            rowsum[pl.ds(h, 1), :] = jnp.sum(both, axis=0, keepdims=True)
+            away = jnp.sum(both, axis=1, keepdims=True)
+            colsum[...] += jnp.where(lane == h, away, 0.0)
+            outs.append(dot(prod.astype(BF16), low))
+        dscaled = jnp.where(first, outs[0], outs[1])
+        dx_ref[:, here] = dscaled * steps + dy * skip_ref[:, here]
+        gain_step = dscaled * x
+        left = jnp.sum(jnp.where(first, gain_step, 0.0), axis=1, keepdims=True)
+        right = jnp.sum(jnp.where(first, 0.0, gain_step), axis=1, keepdims=True)
+        stepgrad[...] += jnp.where(lane == 2 * p, left, 0.0) + jnp.where(
+            lane == 2 * p + 1, right, 0.0
+        )
+
+    daff = daff_ref[...] * turned_inside
+    dx_ref[:, INNER : INNER + STATE] = dot_exact(daff, x_ref[:, INNER + STATE :])
+    dx_ref[:, INNER + STATE :] = dot_exact(daff.T, x_ref[:, INNER : INNER + STATE])
+    pad = jnp.zeros((LANES - HEADS, rows), F32)
+    dsums = jnp.concatenate([rowsum[...], pad], axis=0).T - colsum[...]
+    dlog = dot_exact(turned_inside, dsums)[:, :HEADS]
+    dstep = stepgrad[:, :HEADS] + dlog * rates
+    draw = dstep * sigmoid(raw)
+    dinner_ref[:, INNER + CONVCH :] = draw.astype(BF16)
+    dheads_ref[0:1, :HEADS] = jnp.sum(dlog * step, axis=0, keepdims=True) * rates
+    dheads_ref[1:2, :HEADS] = jnp.sum(draw, axis=0, keepdims=True)
+
+    @pl.loop(0, CONVCH // LANES)
+    def _(k):
+        here = pl.ds(pl.multiple_of(k * LANES, LANES), LANES)
+        there = pl.ds(pl.multiple_of(INNER + k * LANES, LANES), LANES)
+        conv_in = inner_ref[:, there]
+        taps = taps_ref[:, here]
+        before = conv_before(conv_in, taps, position)
+        sig = sigmoid(before)
+        grad = dx_ref[:, here] * (sig * (1.0 + before * (1.0 - sig)))
+        back = grad * taps[TAPS - 1 : TAPS]
+        dtaps_ref[TAPS - 1 : TAPS, here] = jnp.sum(grad * conv_in, axis=0, keepdims=True)
+        for offset in range(1, TAPS):
+            t = TAPS - 1 - offset
+            valid = jnp.where(position >= offset, grad, 0.0)
+            dtaps_ref[t : t + 1, here] = jnp.sum(
+                valid * pltpu.roll(conv_in, offset, 0), axis=0, keepdims=True
+            )
+            back = back + pltpu.roll(valid, rows - offset, 0) * taps[t : t + 1]
+        dinner_ref[:, there] = back.astype(BF16)
+
+
+def mixer_backward(inner, taps, heads, skip, gain, position, inside, y, dmixed):
+    rows = inner.shape[0]
+    shape = jax.ShapeDtypeStruct
+    return pl.pallas_call(
+        mixer_backward_kernel,
+        out_shape=[
+            shape(inner.shape, BF16),
+            shape(taps.shape, F32),
+            shape((1, INNER), F32),
+            shape((1, INNER), F32),
+            shape((8, LANES), F32),
+        ],
+        in_specs=[VMEM] * 9,
+        out_specs=[VMEM] * 5,
+        scratch_shapes=mixer_scratch(rows)
+        + [
+            pltpu.VMEM((rows, CONVCH), F32),
+            pltpu.VMEM((rows, rows), F32),
+            pltpu.VMEM((HEADS, rows), F32),
+            pltpu.VMEM((rows, LANES), F32),
+            pltpu.VMEM((rows, LANES), F32),
+        ],
+        compiler_params=BIG,
+        name="mixer_backward",
+    )(inner, taps, heads, skip, gain, position, inside, y, dmixed)
+
+
+def rotate_rows(front, rear, cosine, sine):
+    return front * cosine - rear * sine, rear * cosine + front * sine
+
+
+def attention_setup(packed_ref, cosine_ref, sine_ref, query, key_rows):
+    half = HD // 2
+    for h in range(QH + KVH):
+        at = h * HD
+        turned = rotate_rows(
+            packed_ref[at : at + half], packed_ref[at + half : at + HD],
+            cosine_ref[...], sine_ref[...],
+        )
+        both = jnp.concatenate(turned, axis=0)
+        if h < QH:
+            query[at : at + HD] = both.astype(BF16)
+        else:
+            key_rows[at - QH * HD : at - (QH - 1) * HD] = both
+
+
+def turned_probs(keys, query, outside):
+    scores = dot(keys, query) * SCORE_SCALE + outside
+    expo = jnp.exp(scores - jnp.max(scores, axis=0, keepdims=True))
+    return expo / jnp.sum(expo, axis=0, keepdims=True)
+
+
+def attention_forward_kernel(
+    packed_ref, cosine_ref, sine_ref, outside_ref, context_ref, turned_ref, query, key_rows
+):
+    attention_setup(packed_ref, cosine_ref, sine_ref, query, key_rows)
+    keys = key_rows[...].T.astype(BF16)
+    values = packed_ref[(QH + KVH) * HD :].astype(BF16)
+    for h in range(QH):
+        kv = h * KVH // QH
+        probs = turned_probs(
+            keys[:, kv * HD : (kv + 1) * HD], query[h * HD : (h + 1) * HD], outside_ref[...]
+        )
+        turned = dot(values[kv * HD : (kv + 1) * HD], probs.astype(BF16))
+        turned_ref[h * HD : (h + 1) * HD] = turned.astype(BF16)
+    for k in range(QH * HD // LANES):
+        here = slice(k * LANES, (k + 1) * LANES)
+        context_ref[:, here] = turned_ref[here].astype(F32).T.astype(BF16)
+
+
+def attention_forward(packed, cosine, sine, outside):
+    rows = packed.shape[1]
+    shape = jax.ShapeDtypeStruct
+    return pl.pallas_call(
+        attention_forward_kernel,
+        out_shape=[shape((rows, QH * HD), BF16), shape((QH * HD, rows), BF16)],
+        in_specs=[VMEM] * 4,
+        out_specs=[VMEM] * 2,
+        scratch_shapes=[pltpu.VMEM((QH * HD, rows), BF16), pltpu.VMEM((KVH * HD, rows), F32)],
+        compiler_params=BIG,
+        name="attention_forward",
+    )(packed, cosine, sine, outside)
+
+
+def attention_backward_kernel(
+    packed_ref, cosine_ref, sine_ref, outside_ref, dcontext_ref, dpacked_ref,
+    query, key_rows, grad_rows,
+):
+    half = HD // 2
+    attention_setup(packed_ref, cosine_ref, sine_ref, query, key_rows)
+    low_rows = key_rows[...].astype(BF16)
+    keys = key_rows[...].T.astype(BF16)
+    values = packed_ref[(QH + KVH) * HD :].T.astype(BF16)
+    for k in range(QH * HD // LANES):
+        here = slice(k * LANES, (k + 1) * LANES)
+        grad_rows[here] = dcontext_ref[:, here].T
+    for kv in range(KVH):
+        of_kv = slice(kv * HD, (kv + 1) * HD)
+        dkey = jnp.zeros((HD, keys.shape[0]), F32)
+        dvalue = jnp.zeros((HD, keys.shape[0]), F32)
+        for h in range(kv * QH // KVH, (kv + 1) * QH // KVH):
+            here = slice(h * HD, (h + 1) * HD)
+            probs = turned_probs(keys[:, of_kv], query[here], outside_ref[...])
+            grad = grad_rows[here].astype(BF16)
+            dprobs = dot(values[:, of_kv], grad)
+            dvalue = dvalue + dot_rt(grad, probs.astype(BF16))
+            inner = jnp.sum(probs * dprobs, axis=0, keepdims=True)
+            dscores = (probs * (dprobs - inner) * SCORE_SCALE).astype(BF16)
+            dquery = dot(low_rows[of_kv], dscores)
+            dkey = dkey + dot_rt(query[here], dscores)
+            turned = rotate_rows(dquery[:half], dquery[half:], cosine_ref[...], -sine_ref[...])
+            grad_rows[here] = jnp.concatenate(turned, axis=0)
+        turned = rotate_rows(dkey[:half], dkey[half:], cosine_ref[...], -sine_ref[...])
+        at = QH * HD + kv * HD
+        grad_rows[at : at + HD] = jnp.concatenate(turned, axis=0)
+        at = (QH + KVH) * HD + kv * HD
+        grad_rows[at : at + HD] = dvalue
+    for k in range((QH + 2 * KVH) * HD // LANES):
+        here = slice(k * LANES, (k + 1) * LANES)
+        dpacked_ref[:, here] = grad_rows[here].T.astype(BF16)
+
+
+def attention_backward(packed, cosine, sine, outside, dcontext):
+    width, rows = packed.shape
+    return pl.pallas_call(
+        attention_backward_kernel,
+        out_shape=jax.ShapeDtypeStruct((rows, width), BF16),
+        in_specs=[VMEM] * 5,
+        out_specs=VMEM,
+        scratch_shapes=[
+            pltpu.VMEM((QH * HD, rows), BF16),
+            pltpu.VMEM((KVH * HD, rows), F32),
+            pltpu.VMEM((width, rows), F32),
+        ],
+        compiler_params=BIG,
+        name="attention_backward",
+    )(packed, cosine, sine, outside, dcontext)
 
 
 def inverse_rms(values):
@@ -433,64 +783,33 @@
     return scale * (inner - normed * jnp.mean(inner * normed, axis=-1, keepdims=True)), grad_gain
 
 
-def layer_forward(hidden, weights, small, heads, layout):
+def layer_forward(hidden, weights, small, layout):
     w_in, w_mix, w_qkv, w_attn, w_gate_up, w_down = weights
-    gains, kernel, gain_inner = small
-    position, inside, tables = layout
+    gains, taps, gain_inner, heads, skip = small
+    position, inside, outside, cosine, sine = layout
     scale = inverse_rms(hidden)
     normed = (hidden * scale * gains[0]).astype(BF16)
     inner = dot(normed, w_in)
-    packed = dot(normed, w_qkv)
-    core = functools.partial(mixer_core, position=position, inside=inside)
-    gated, pull_core = jax.vjp(core, inner, kernel, heads)
-    scale_inner = inverse_rms(gated)
-    mixed = (gated * scale_inner * gain_inner).astype(BF16)
-    context, kept_attn = attention_forward(packed, tables, inside)
+    packed = lax.dot_general(
+        w_qkv, normed, (((0,), (1,)), ((), ())), preferred_element_type=F32
+    )
+    mixed, mixed_rows, y = mixer_forward(inner, taps, heads, skip, gain_inner, position, inside)
+    context, context_rows = attention_forward(packed, cosine, sine, outside)
     middle = hidden + dot(mixed, w_mix) + dot(context, w_attn)
     scale_two = inverse_rms(middle)
     normed_two = (middle * scale_two * gains[1]).astype(BF16)
     both = dot(normed_two, w_gate_up)
     active = (jax.nn.silu(both[:, :FF]) * both[:, FF:]).astype(BF16)
     out = middle + dot(active, w_down)
-    kept = (
-        hidden,
-        scale,
-        normed,
-        pull_core,
-        gated,
-        scale_inner,
-        mixed,
-        context,
-        kept_attn,
-        middle,
-        scale_two,
-        normed_two,
-        both,
-        active,
-    )
-    return out, kept
+    turned = [normed.T, mixed_rows, context_rows, normed_two.T, active.T]
+    return out, (hidden, scale, inner, packed, y, middle, scale_two, both, turned)
 
 
 def layer_backward(grad, kept, weights, small, layout):
     w_in, w_mix, w_qkv, w_attn, w_gate_up, w_down = weights
-    gains, kernel, gain_inner = small
-    position, inside, tables = layout
-    (
-        hidden,
-        scale,
-        normed,
-        pull_core,
-        gated,
-        scale_inner,
-        mixed,
-        context,
-        kept_attn,
-        middle,
-        scale_two,
-        normed_two,
-        both,
-        active,
-    ) = kept
+    gains, taps, gain_inner, heads, skip = small
+    position, inside, outside, cosine, sine = layout
+    hidden, scale, inner, packed, y, middle, scale_two, both, turned = kept
     ddown = grad.astype(BF16)
     dactive = dot_rt(ddown, w_down)
     gate, up = both[:, :FF], both[:, FF:]
@@ -500,16 +819,17 @@
     dmiddle, dgain_two = norm_backward(dot_rt(dboth, w_gate_up), middle, scale_two, gains[1])
     dmiddle = grad + dmiddle
     dbranch = dmiddle.astype(BF16)
-    dgated, dgain_inner = norm_backward(dot_rt(dbranch, w_mix), gated, scale_inner, gain_inner)
-    dcontext = dot_rt(dbranch, w_attn).astype(BF16)
-    dpacked = attention_backward(dcontext, kept_attn, tables)
-    dinner, dkernel, dheads = pull_core(dgated)
-    dinner = dinner.astype(BF16)
+    dmixed = dot_rt(dbranch, w_mix)
+    dcontext = dot_rt(dbranch, w_attn).astype(BF16).astype(F32)
+    dpacked = attention_backward(packed, cosine, sine, outside, dcontext)
+    dinner, dtaps, dgain_inner, dskip, dheads = mixer_backward(
+        inner, taps, heads, skip, gain_inner, position, inside, y, dmixed
+    )
     dnormed = dot_rt(dinner, w_in) + dot_rt(dpacked, w_qkv)
     dhidden, dgain = norm_backward(dnormed, hidden, scale, gains[0])
-    turned = [x.T for x in (normed, mixed, context, normed_two, active)]
     grads = [dinner, dpacked, dbranch, dboth, ddown]
-    flat = [dgain, dgain_two, dkernel.reshape(-1), dgain_inner] + list(dheads)
+    flat = [dgain, dgain_two, dtaps.reshape(-1), dgain_inner[0], dheads[0, :HEADS]]
+    flat += [jnp.sum(dskip.reshape(HEADS, HDIM), axis=1), dheads[1, :HEADS]]
     return dmiddle + dhidden, turned, grads, jnp.concatenate(flat)
 
 
@@ -567,7 +887,8 @@
     inside = (segment[:, None] == segment[None, :]) & (index[:, None] >= index[None, :])
     inverse = ROPE_BASE ** (-(jnp.arange(HD // 2, dtype=F32) * 2.0 / HD))
     angles = position.astype(F32)[:, None] * inverse[None, :]
-    layout = (position, inside, (jnp.cos(angles), jnp.sin(angles)))
+    outside = jnp.where(inside.T, 0.0, -1e30)
+    layout = (position[:, None], inside.astype(F32), outside, jnp.cos(angles).T, jnp.sin(angles).T)
 
     matrices = (in_proj, mixer_out, qkv_proj, attn_out, gate_up, down_proj)
     gain_part, conv_part, inner_part = (x.shape[-1] for x in (norm_gains, conv_weight, ssm_gain))
@@ -596,34 +917,29 @@
     def small_of(layer):
         both = smalls[layer]
         mid = 2 * gain_part
+        heads = jnp.stack([a_log[layer], d_skip[layer], dt_bias[layer]])
         return (
             spread(both[:, :mid], 2),
             spread(both[:, mid : mid + TAPS * conv_part], TAPS),
-            spread(both[:, mid + TAPS * conv_part :], 1)[0],
+            spread(both[:, mid + TAPS * conv_part :], 1),
+            jnp.pad(heads, ((0, 5), (0, LANES - HEADS))),
+            jnp.repeat(d_skip[layer], HDIM)[None],
         )
 
     params = [small_of(layer) for layer in range(LAYERS)]
-    heads = [(a_log[layer], d_skip[layer], dt_bias[layer]) for layer in range(LAYERS)]
 
     kept = [None] * LAYERS
     for layer in range(LAYERS):
-        hidden, kept[layer] = layer_forward(
-            hidden, weights[layer], params[layer], heads[layer], layout
+        hidden, kept[layer] = layer_forward(hidden, weights[layer], params[layer], layout)
+
+    def permute_back(choice, rows):
+        return lax.dot_general(
+            choice, rows.astype(BF16), (((0,), (0,)), ((), ())), preferred_element_type=F32
         )
-    leaving = lax.dot_general(
-        enter, hidden.astype(BF16), (((0,), (0,)), ((), ())), preferred_element_type=F32
-    ).astype(BF16)
-
-    def come_home(rows):
-        moved = exchange(rows)
-        return lax.dot_general(
-            leave, moved, (((0,), (0,)), ((), ())), preferred_element_type=F32
-        )
-
-    out_tokens = come_home(leaving).astype(BF16)
 
     flowing = upstream
     owned = [None] * LAYERS
+    back = [None] * LAYERS
     for layer in reversed(range(LAYERS)):
         flowing, turned, grads, flat = layer_backward(
             flowing, kept[layer], weights[layer], params[layer], layout
@@ -631,14 +947,14 @@
         count = flat.shape[0]
         lines = -(-count // 1024) * 8
         small = jnp.pad(flat, (0, lines * 128 - count)).reshape(lines, 128)
+        home = flowing if layer == 0 else hidden
+        home = permute_back(enter, home).astype(BF16)
         if own_kernels:
-            owned[layer] = scatter_layer(turned, grads, small, devices, layer)
+            owned[layer], back[layer] = scatter_layer(turned, grads, small, home, devices)
         else:
-            owned[layer] = scatter_plain(turned, grads, small)
-    sending = lax.dot_general(
-        enter, flowing.astype(BF16), (((0,), (0,)), ((), ())), preferred_element_type=F32
-    ).astype(BF16)
-    in_grad = come_home(sending)
+            owned[layer], back[layer] = scatter_plain(turned, grads, small), exchange(home)
+    out_tokens = permute_back(leave, back[LAYERS - 1]).astype(BF16)
+    in_grad = permute_back(leave, back[0])
 
     big = [jnp.stack([owned[layer][k] for layer in range(LAYERS)]) for k in range(6)]
     totals = jnp.stack([owned[layer][6].reshape(-1) for layer in range(LAYERS)])

time: 937 us -> 742 us (0.79)
  matrix products: 183 us -> 83.9 us
  other arithmetic: 78.5 us -> 23.1 us
  local copies, waits for them, and re-layouts: 81.7 us -> 33.4 us
  Pallas kernels: 548 us -> 581 us
  waiting for transfers between devices: 15.8 us -> 0.01 us
  starting transfers between devices: 20 us -> 10.2 us
    dot_general x30 -> x6, matrix products: 110 us -> 13.1 us  [the longest x4 9.9 us: permute_back(): lax.dot_general(choice, rows.astype(BF16), (((0,), (0,)), ((), ())), pref...]
    pallas_call x1 -> x9, Pallas kernels: 244 us -> 327 us  [the longest x1 230 us: gather_all(): pl.pallas_call(functools.partial(gather_kernel, devices, AG_CHUNKS, AG_EV...]
    pallas_call x2, Pallas kernels: 304 us -> 254 us  [scatter_layer(): pl.pallas_call(functools.partial(scatter_kernel, devices, arrs, nx, ny),...]
    reduce_sum x11 -> x2, other arithmetic: 33.9 us -> 0.23 us  [layer_backward(): flat += [jnp.sum(dskip.reshape(HEADS, HDIM), axis=1), dheads[1, :HEADS]]]
    all_to_all x4 -> x2, waiting for transfers between devices: 15.8 us -> 0.01 us  [exchange(): moved = lax.all_to_all(split, 'dp', split_axis=0, concat_axis=0, tiled=True)]
    reshape x18 -> x4, local copies, waits for them, and re-layouts: 14 us -> 0.17 us  [the longest x2 0.14 us: layer_backward(): flat += [jnp.sum(dskip.reshape(HEADS, HDIM), axis=1), dheads[1, :HEADS]]]
    mul x7 -> x0, other arithmetic: 11.3 us -> none  [the longest x2 4.94 us: mixer_core(): conv_out = jax.nn.silu(causal_conv(conv_in, kernel, position))]
    mul x11 -> x0, local copies, waits for them, and re-layouts: 10.4 us -> none  [the longest x2 6.13 us: mixer_core(): return scanned.reshape(rows_count, INNER) * jax.nn.silu(gate_z)]
  transfers between devices with their start and end apart: 4 -> 2, of which waited for: 2 -> 0; matrix products, arithmetic and copies ran while one was open for 13% -> 7% of each run, Pallas kernels for 26% -> 37%
where the time goes in v3:
time: 742 us; the launch traced here: 733 us
  Pallas kernels  581 us (78%)
  matrix products  83.9 us (11%)
  local copies, waits for them, and re-layouts  33.4 us (5%)
  other arithmetic  23.1 us (3%)
  starting transfers between devices  10.2 us (1%)
    pallas_call x2, Pallas kernels, scatter_layer(): pl.pallas_call(functools.partial(scatter_kernel, devices, arrs, nx, ny),...  254 us
    pallas_call x1, Pallas kernels, gather_all(): pl.pallas_call(functools.partial(gather_kernel, devices, AG_CHUNKS, AG_EV...  230 us
    pallas_call x2, Pallas kernels, mixer_backward(): pl.pallas_call(mixer_backward_kernel, out_shape=[shape(inner.shape, BF16)...  47 us
    dot_general x12, matrix products, dot_rt(): lax.dot_general(left, right, (((1,), (1,)), ((), ())), preferred_element_...  37.2 us
    dot_general x14, matrix products, dot(): return jnp.dot(left, right, preferred_element_type=F32)  33.6 us
    pallas_call x2, Pallas kernels, mixer_forward(): pl.pallas_call(mixer_forward_kernel, out_shape=[shape((rows, INNER), BF16...  29.5 us
  transfers between devices with their start and end apart: 2, of which 0 were waited for; matrix products, arithmetic and copies ran while one was open for 7% of the time, Pallas kernels for 37%

profile of v3, /device:TPU:0, one launch (start us, length us, event | category | flops | bytes accessed | tf_op | source)
XLA Modules:
  0.0 733.0 jit_solution(2829884184879772416)
XLA Ops:
  2.9 7.3 %all-to-all-start = ((bf16[32,8,1024]{2,1,0:T(8,128)(2,1)}), bf16[32,8,1024]{2,1,0:T(8,128)(2,1)S(1)}, u32[]{:S(2)}, u32[]{:S(2)}) async-start(bf16[32,8,1024]{2,1,0:T(8,128)(2,1)} %fusion.3), calls=%async_computation | async-start | bytes 1048576 | tf_op jit(solution)/shard_map/all_to_all | solution.py:870
  11.1 230.1 %gather_all.1 = (bf16[2,2,2,2,2,32,3352]{6,5,4,3,2,1,0:T(8,128)(2,1)}, bf16[2,2,2,2,2,48,1024]{6,5,4,3,2,1,0:T(8,128)(2,1)}, bf16[2,2,2,2,2,32,768]{6,5,4,3,2,1,...) custom-call(bf16[2,32,3352]{2,1,0:T(8,128)(2,1)} %refs_0_.1, ...), custom_call_target="tpu_custom_call" | custom-call | tf_op jit(solution)/shard_map/gather_all/pallas_call | solution.py:135
  255.5 2.9 all-to-all-start.1
  258.8 7.0 fusion.62.inner_ref
  267.4 14.9 %mixer_forward.2 = (bf16[256,1536]{1,0:T(8,128)(2,1)}, bf16[1536,256]{1,0:T(8,128)(2,1)}, f32[256,1536]{1,0:T(8,128)}) custom-call(f32[256,3352]{1,0:T(8,128)} %fusion.62.inner_ref, f32[4,1792]{1,0:T(4,128)} %reshape.394.taps_ref, f32[8,128]{1,0:T(8,128)} %get-tuple-element.177.heads_ref, f32[1,1536]{1,0:T(1,128)} %broadcast_in_dim_reshape.8.skip_ref, ...), custom_call_target="tpu_custom_call" | custom-call | tf_op jit(solution)/shard_map/mixer_forward/pallas_call | solution.py:508
  282.3 2.2 convolution_add_fusion.5
  284.5 4.7 attention_forward.2
  290.7 6.2 fusion.51
  300.3 3.9 fusion.64.inner_ref
  305.8 4.7 attention_forward.3
  310.5 14.6 %mixer_forward.3 = (bf16[256,1536]{1,0:T(8,128)(2,1)}, bf16[1536,256]{1,0:T(8,128)(2,1)}, f32[256,1536]{1,0:T(8,128)}) custom-call(f32[256,3352]{1,0:T(8,128)} %fusion.64.inner_ref, f32[4,1792]{1,0:T(4,128)} %reshape.396.taps_ref, f32[8,128]{1,0:T(8,128)} %get-tuple-element.176.heads_ref, f32[1,1536]{1,0:T(1,128)} %broadcast_in_dim_reshape.9.skip_ref, ...), custom_call_target="tpu_custom_call" | custom-call | tf_op jit(solution)/shard_map/mixer_forward/pallas_call | solution.py:508
  325.2 3.3 convolution_add_fusion.4
  330.0 4.5 fusion.52
  334.9 6.7 multiply_convert_fusion.3
  341.6 2.7 multiply_reduce_fusion.5
  346.4 2.3 fusion.66.dmixed_ref
  350.0 23.5 %mixer_backward.2 = (bf16[256,3352]{1,0:T(8,128)(2,1)}, f32[4,1792]{1,0:T(4,128)}, f32[1,1536]{1,0:T(1,128)}, f32[1,1536]{1,0:T(1,128)}, f32[8,128]{1,0:T(8,128)}) custom-call(f32[256,3352]{1,0:T(8,128)} %fusion.64.inner_ref, f32[4,1792]{1,0:T(4,128)} %reshape.396.taps_ref, f32[8,128]{1,0:T(8,128)} %get-tuple-element.176.heads_ref, ...), custom_call_target="tpu_custom_call" | custom-call | tf_op jit(solution)/shard_map/mixer_backward/pallas_call | solution.py:639
  373.5 5.6 fusion.67
  379.2 5.3 attention_backward.2.refs_6_
  391.7 2.6 multiply_reduce_fusion.1
  396.7 2.3 fusion.68.dmixed_ref
  406.5 23.5 %mixer_backward.3 = (bf16[256,3352]{1,0:T(8,128)(2,1)}, f32[4,1792]{1,0:T(4,128)}, f32[1,1536]{1,0:T(1,128)}, f32[1,1536]{1,0:T(1,128)}, f32[8,128]{1,0:T(8,128)}) custom-call(f32[256,3352]{1,0:T(8,128)} %fusion.62.inner_ref, f32[4,1792]{1,0:T(4,128)} %reshape.394.taps_ref, f32[8,128]{1,0:T(8,128)} %get-tuple-element.177.heads_ref, ...), custom_call_target="tpu_custom_call" | custom-call | tf_op jit(solution)/shard_map/mixer_backward/pallas_call | solution.py:639
  430.1 5.6 fusion.69
  435.7 5.3 attention_backward.3.refs_6_
  441.1 2.7 multiply_reduce_fusion
  445.5 2.1 copy.65
  447.7 2.3 copy.66
  451.0 4.9 convolution_convert_fusion.2
  458.7 2.4 copy.62
  462.1 2.6 convolution_convert_fusion
  464.7 127.8 %scatter_layer.3 = (f32[32,3352]{1,0:T(8,128)}, f32[48,1024]{1,0:T(8,128)}, f32[32,768]{1,0:T(8,128)}, f32[16,1024]{1,0:T(8,128)}, f32[32,4096]{1,0:T(8,128)}, /...) custom-call(bf16[16,2,32,256]{3,2,1,0:T(8,128)(2,1)} %bitcast.194, ...), custom_call_target="tpu_custom_call" | custom-call | tf_op jit(solution)/shard_map/scatter_layer/pallas_call | solution.py:353
  593.2 126.2 %scatter_layer.2 = (f32[32,3352]{1,0:T(8,128)}, f32[48,1024]{1,0:T(8,128)}, f32[32,768]{1,0:T(8,128)}, f32[16,1024]{1,0:T(8,128)}, f32[32,4096]{1,0:T(8,128)}, /...) custom-call(bf16[16,2,32,256]{3,2,1,0:T(8,128)(2,1)} %bitcast.196, ...), custom_call_target="tpu_custom_call" | custom-call | tf_op jit(solution)/shard_map/scatter_layer/pallas_call | solution.py:353
  (264 shorter events, 68.4 us)
Async XLA Ops:
  0.7 9.6 %copy-start.52 = (bf16[2,4,56]{2,1,0:T(4,128)(2,1)S(1)}, bf16[2,4,56]{2,1,0:T(4,128)(2,1)}, u32[]{:S(2)}) copy-start(bf16[2,4,56]{2,1,0:T(4,128)(2,1)} %param.22) | copy-start | bytes 2692
  0.7 9.7 %copy-start.60 = (bf16[2,2,32]{2,1,0:T(2,128)(2,1)S(1)}, bf16[2,2,32]{2,1,0:T(2,128)(2,1)}, u32[]{:S(2)}) copy-start(bf16[2,2,32]{2,1,0:T(2,128)(2,1)} %param.20) | copy-start | bytes 772
  0.7 9.8 %copy-start.56 = (bf16[2,48]{1,0:T(2,128)(2,1)S(1)}, bf16[2,48]{1,0:T(2,128)(2,1)}, u32[]{:S(2)}) copy-start(bf16[2,48]{1,0:T(2,128)(2,1)} %param.23) | copy-start | bytes 580
  1.8 241.7 %copy-start.41 = (s32[8192]{0:T(1024)S(1)}, s32[8192]{0:T(1024)}, u32[]{:S(2)}) copy-start(s32[8192]{0:T(1024)} %param.18) | copy-start | bytes 98308
  2.9 240.9 %copy-start.53 = (f32[2,24]{1,0:T(2,128)S(1)}, f32[2,24]{1,0:T(2,128)}, u32[]{:S(2)}) copy-start(f32[2,24]{1,0:T(2,128)} %param.30) | copy-start | bytes 580
  2.9 241.0 %copy-start.54 = (f32[2,24]{1,0:T(2,128)S(1)}, f32[2,24]{1,0:T(2,128)}, u32[]{:S(2)}) copy-start(f32[2,24]{1,0:T(2,128)} %param.29) | copy-start | bytes 580
  2.9 241.0 %copy-start.55 = (f32[2,24]{1,0:T(2,128)S(1)}, f32[2,24]{1,0:T(2,128)}, u32[]{:S(2)}) copy-start(f32[2,24]{1,0:T(2,128)} %param.31) | copy-start | bytes 580
  2.9 241.0 %copy-start.57 = (s32[1,4]{1,0:T(1,128)S(1)}, s32[1,4]{1,0:T(1,128)}, u32[]{:S(2)}) copy-start(s32[1,4]{1,0:T(1,128)} %param.19) | copy-start | bytes 52
  2.9 241.3 %copy-start.29 = (bf16[256,1024]{1,0:T(8,128)(2,1)S(1)}, bf16[256,1024]{1,0:T(8,128)(2,1)}, u32[]{:S(2)}) copy-start(bf16[256,1024]{1,0:T(8,128)(2,1)} %param.17) | copy-start | bytes 1572868
  2.9 252.6 %all-to-all-start = ((bf16[32,8,1024]{2,1,0:T(8,128)(2,1)}), bf16[32,8,1024]{2,1,0:T(8,128)(2,1)S(1)}, u32[]{:S(2)}, u32[]{:S(2)}) async-start(bf16[32,8,1024]{2,1,0:T(8,128)(2,1)} %fusion.3), calls=%async_computation | async-start | bytes 1048576 | tf_op jit(solution)/shard_map/all_to_all | solution.py:870
  255.5 79.0 %all-to-all-start.1 = ((bf16[32,8,1024]{2,1,0:T(8,128)(2,1)}), bf16[32,8,1024]{2,1,0:T(8,128)(2,1)S(1)}, u32[]{:S(2)}, u32[]{:S(2)}) async-start(bf16[32,8,1024]{2,1,0:T(8,128)(2,1)} %fusion.4), calls=%async_computation.1 | async-start | bytes 1048576 | tf_op jit(solution)/shard_map/all_to_all | solution.py:870
  258.8 7.0 copy-start.14
  267.4 14.9 %copy-start.4 = (bf16[2,2,2,2,2,48,1024]{6,5,4,3,2,1,0:T(8,128)(2,1)S(1)}, bf16[2,2,2,2,2,48,1024]{6,5,4,3,2,1,0:T(8,128)(2,1)}, u32[]{:S(2)}) copy-start(bf16[2,2,2,2,2,48,1024]{6,5,4,3,2,1,0:T(8,128)(2,1)} %get-tuple-element.67) | copy-start | bytes 9437188
  282.3 6.9 copy-start.18
  290.7 6.2 copy-start.10
  290.7 6.2 copy-start.58
  290.7 8.3 %slice-start.6 = ((s8[7077888]{0:T(1024)(128)(4,1)}), s8[4194304]{0:T(1024)(128)(4,1)S(1)}, s32[]{:S(2)}) async-start(s8[7077888]{0:T(1024)(128)(4,1)} %bitcast.180), calls=%async_computation.8 | async-start | bytes 8388608
  304.2 25.7 %slice-start.2 = ((s8[8388608]{0:T(1024)(128)(4,1)}), s8[4194304]{0:T(1024)(128)(4,1)S(1)}, s32[]{:S(2)}) async-start(s8[8388608]{0:T(1024)(128)(4,1)} %bitcast.167), calls=%async_computation.4 | async-start | bytes 8388608
  334.5 7.1 slice-start.4
  334.8 6.7 copy-start.24
  334.8 6.7 slice-start.5
  334.8 6.7 copy-start.8
  435.7 5.3 copy-start.15
  445.5 5.5 copy-start.9
  451.0 6.6 copy-start.25
  593.2 126.2 %copy-start.28 = (f32[88,128]{1,0:T(8,128)S(1)}, f32[88,128]{1,0:T(8,128)}, u32[]{:S(2)}) copy-start(f32[88,128]{1,0:T(8,128)} %get-tuple-element.100) | copy-start | bytes 135172
  593.2 130.1 %copy-start.32 = (bf16[2,2,2,2,2,8,1024]{6,5,4,3,2,1,0:T(8,128)(2,1)S(1)}, bf16[2,2,2,2,2,8,1024]{6,5,4,3,2,1,0:T(8,128)(2,1)}, u32[]{:S(2)}) copy-start(bf16[2,2,2,2,2,8,1024]{6,5,4,3,2,1,0:T(8,128)(2,1)} %get-tuple-element.99) | copy-start | bytes 1572868
  719.4 6.4 copy-start.37
  719.4 6.4 copy-start.38
  720.9 5.8 copy-start.31
  720.9 5.8 copy-start.33
  726.7 6.1 copy-start.1
  (39 other events, 129.2 us)

commit v4 on v2

v4 whole, which is shorter than its diff:
```python
import functools

import jax
import jax.numpy as jnp
from jax import lax
from jax.experimental import pallas as pl
from jax.experimental.pallas import tpu as pltpu
from jax.sharding import PartitionSpec as P

FF = 2048
HEADS = 24
HDIM = 64
STATE = 128
QH = 8
KVH = 2
HD = 64
LAYERS = 2
INNER = 1536
CONVCH = 1792
TAPS = 4
EPSILON = 1e-05
ROPE_BASE = 100000000000.0
SCORE_SCALE = 0.125
HIGHEST = lax.Precision.HIGHEST
F32 = jnp.float32
BF16 = jnp.bfloat16
MESH = pl.DeviceIdType.MESH

AG_CHUNKS = [(0, 6, (4, 3, 2, 1)), (1, 6, (4, 3, 2, 1)), (1, 0, (4, 3, 1, 2)), (1, 3, (4, 3, 2, 1)), (1, 2, (4, 3, 2, 1)), (0, 2, (4, 3, 2, 1)), (1, 5, (4, 3, 2, 1)), (0, 0, (4, 3, 1, 2)), (0, 3, (1, 4, 3, 2)), (0, 5, (4, 3, 2, 1)), (0, 4, (1, 2, 4, 3)), (0, 1, (1, 2, 4, 3)), (1, 1, (4, 3, 2, 1))]
AG_EVENTS = [(0, 0), (1, 0), (8, 0), (10, 0), (11, 0), (2, 0), (3, 0), (4, 0), (5, 0), (0, 1), (1, 1), (6, 0), (10, 1), (11, 1), (0, 2), (1, 2), (0, 3), (1, 3), (7, 0), (2, 1), (3, 1), (4, 1), (9, 0), (5, 1), (3, 2), (12, 0), (6, 1), (4, 2), (8, 1), (5, 2), (2, 2), (6, 2), (3, 3), (4, 3), (5, 3), (7, 1), (9, 1), (10, 2), (12, 1), (2, 3), (8, 2), (6, 3), (11, 2), (9, 2), (12, 2), (7, 2), (8, 3), (9, 3), (10, 3), (12, 3), (7, 3), (11, 3)]
PLAN_A = ([(1, 0, 256, (2, 1, 3, 4)), (1, 768, 1024, (3, 4, 1, 2)), (0, 0, 1024, (1, 2, 3, 4)), (0, 2048, 3072, (2, 3, 4, 1)), (0, 3072, 4096, (3, 4, 1, 2)), (0, 1024, 2048, (1, 2, 3, 4)), (1, 256, 512, (1, 2, 3, 4)), (1, 512, 768, (2, 1, 3, 4))], [(0, -1), (1, -1), (2, -1), (3, -1), (4, -1), (5, -1), (6, -1), (7, -1), (-3, 0), (0, 0), (1, 0), (-3, 0), (-3, 0), (-3, 0), (-3, 0), (-3, 0), (-3, 0), (-3, 0), (2, 0), (-3, 0), (1, 1), (3, 0), (4, 0), (-3, 0), (-3, 0), (7, 0), (-3, 0), (5, 0), (3, 1), (-3, 0), (2, 1), (-3, 0), (6, 0), (-3, 0), (-3, 0), (0, 1), (4, 1), (-3, 0), (5, 1), (1, 2), (-3, 0), (-3, 0), (7, 1), (6, 1), (2, 2), (-3, 0), (0, 2), (3, 2), (-3, 0), (1, 3), (-3, 0), (4, 2), (-3, 0), (-3, 0), (5, 2), (-3, 0), (-3, 0), (7, 2), (-3, 0), (-3, 0), (3, 3), (-3, 0), (6, 2), (2, 3), (-3, 0), (4, 3), (0, 3), (5, 3), (7, 3), (6, 3)], (1, 2, 3, 4, 0))
PLAN_B = ([(1, 512, 1024, (1, 2, 3, 4)), (4, 2688, 4096, (2, 1, 3, 4)), (0, 0, 1664, (3, 4, 2, 1)), (2, 0, 768, (3, 4, 2, 1)), (3, 0, 1024, (2, 1, 3, 4)), (4, 1408, 2688, (1, 3, 4, 2)), (0, 1664, 3352, (2, 1, 3, 4)), (4, 0, 1408, (1, 2, 3, 4)), (5, 512, 1024, (1, 3, 4, 2)), (5, 0, 512, (2, 1, 3, 4)), (1, 0, 512, (2, 1, 3, 4))], [(0, -1), (1, -1), (2, -1), (3, -1), (4, -1), (5, -1), (6, -1), (7, -1), (8, -1), (9, -1), (10, -1), (-1, 0), (0, 0), (-2, 0), (-3, 0), (-2, 1), (-3, 0), (-3, 0), (-3, 0), (-3, 0), (1, 0), (-3, 0), (-3, 0), (-3, 0), (-3, 0), (5, 0), (4, 0), (2, 0), (-3, 0), (-3, 0), (-3, 0), (3, 0), (-3, 0), (-3, 0), (-3, 0), (-3, 0), (7, 0), (5, 1), (-3, 0), (-3, 0), (-3, 0), (6, 0), (-3, 0), (-3, 0), (-3, 0), (-3, 0), (-3, 0), (-3, 0), (-3, 0), (-3, 0), (-3, 0), (2, 1), (-3, 0), (-3, 0), (8, 0), (-1, 1), (9, 0), (3, 1), (1, 1), (4, 1), (8, 1), (10, 0), (5, 2), (0, 1), (1, 2), (4, 2), (6, 1), (-2, 2), (8, 2), (0, 2), (1, 3), (9, 1), (4, 3), (0, 3), (7, 1), (6, 2), (10, 1), (9, 2), (2, 2), (-1, 2), (-2, 3), (3, 2), (7, 2), (6, 3), (5, 3), (2, 3), (8, 3), (3, 3), (9, 3), (10, 2), (-1, 3), (7, 3), (10, 3), (-2, 4), (-1, 4)], (4, 0, 2, 1, 3))
PLAN_C = ([(3, 512, 1024, (2, 1, 3, 4)), (1, 0, 512, (1, 2, 3, 4)), (0, 2560, 3352, (3, 4, 1, 2)), (2, 384, 768, (2, 3, 4, 1)), (0, 0, 896, (2, 1, 3, 4)), (0, 896, 1664, (3, 4, 2, 1)), (0, 1664, 2560, (2, 1, 3, 4)), (1, 512, 1024, (1, 2, 3, 4)), (2, 0, 384, (1, 2, 3, 4)), (3, 0, 512, (1, 2, 3, 4))], [(0, -1), (1, -1), (2, -1), (3, -1), (4, -1), (5, -1), (6, -1), (7, -1), (8, -1), (9, -1), (-1, 0), (0, 0), (3, 0), (1, 0), (-2, 0), (-2, 1), (2, 0), (4, 0), (7, 0), (5, 0), (8, 0), (3, 1), (9, 0), (-1, 1), (6, 0), (2, 1), (0, 1), (1, 1), (4, 1), (0, 2), (5, 1), (1, 2), (-2, 2), (6, 1), (3, 2), (4, 2), (0, 3), (2, 2), (7, 1), (1, 3), (8, 1), (6, 2), (9, 1), (-1, 2), (4, 3), (-2, 3), (3, 3), (7, 2), (5, 2), (8, 2), (2, 3), (9, 2), (6, 3), (-1, 3), (5, 3), (7, 3), (8, 3), (9, 3), (-2, 4), (-1, 4)], (4, 0, 2, 1, 3))

SMALL_ROWS = 16
LATE_ARRAY = 4


def dot(left, right):
    return jnp.dot(left, right, preferred_element_type=F32)


def dot_rt(left, right):
    return lax.dot_general(left, right, (((1,), (1,)), ((), ())), preferred_element_type=F32)


PAIRS_OF_HEADS = HEADS // 2
LANES = 128
VMEM = pl.BlockSpec(memory_space=pltpu.VMEM)
BIG = pltpu.CompilerParams(vmem_limit_bytes=56 * 1024 * 1024)


def dot_exact(left, right):
    return jnp.dot(left, right, preferred_element_type=F32, precision=HIGHEST)


def dot_rt_exact(left, right):
    return lax.dot_general(
        left, right, (((1,), (1,)), ((), ())), preferred_element_type=F32, precision=HIGHEST
    )


def sigmoid(x):
    return 1.0 / (1.0 + jnp.exp(-x))


def column_index(shape):
    return lax.broadcasted_iota(jnp.int32, shape, len(shape) - 1)


def shifted_down(values, offset, position):
    return jnp.where(position >= offset, pltpu.roll(values, offset, 0), 0.0)


def conv_before(conv_in, taps, position):
    total = conv_in * taps[TAPS - 1 : TAPS]
    for offset in range(1, TAPS):
        total = total + shifted_down(conv_in, offset, position) * taps[
            TAPS - 1 - offset : TAPS - offset
        ]
    return total


def spans(count, parts):
    edges = [count * k // parts for k in range(parts + 1)]
    return list(zip(edges[:-1], edges[1:]))


def run_steps(steps):
    for _ in steps:
        pass


def step_sizes(inner_ref, heads_ref):
    raw = inner_ref[:, INNER + CONVCH :] + heads_ref[2:3, :HEADS]
    step = jnp.maximum(raw, 0.0) + jnp.log1p(jnp.exp(-jnp.abs(raw)))
    return raw, step, -jnp.exp(heads_ref[0:1, :HEADS])


def mixer_setup(inner_ref, taps_ref, heads_ref, position, inside, x_ref, qcol, qrow, dtpair):
    rows = inner_ref.shape[0]
    for start, end in spans(CONVCH // LANES, 2):

        @pl.loop(start, end)
        def _(k):
            at = pl.multiple_of(k * LANES, LANES)
            before = conv_before(
                inner_ref[:, pl.ds(pl.multiple_of(INNER + at, LANES), LANES)],
                taps_ref[:, pl.ds(at, LANES)],
                position,
            )
            x_ref[:, pl.ds(at, LANES)] = before * sigmoid(before)

        yield

    raw, step, rates = step_sizes(inner_ref, heads_ref)
    sums = dot_exact(inside, step * rates)
    wide = jnp.concatenate([sums, jnp.zeros((rows, LANES - HEADS), F32)], axis=1)
    qrow[...] = wide.T[: qrow.shape[0]]
    first = column_index((rows, LANES)) < HDIM
    yield
    for p in range(PAIRS_OF_HEADS):
        for source, target in ((sums, qcol), (step, dtpair)):
            both = [
                jnp.broadcast_to(source[:, h : h + 1], (rows, LANES)) for h in (2 * p, 2 * p + 1)
            ]
            target[p] = jnp.where(first, both[0], both[1])
        if p % 4 == 3:
            yield


def mixer_forward_kernel(
    inner_ref, taps_ref, heads_ref, skip_ref, gain_ref, position_ref, inside_ref,
    mixed_ref, turned_ref, y_ref, x_ref, qcol, qrow, dtpair, aff_ref,
):
    rows = inner_ref.shape[0]
    position = position_ref[...]
    inside = inside_ref[...]
    run_steps(
        mixer_setup(inner_ref, taps_ref, heads_ref, position, inside, x_ref, qcol, qrow, dtpair)
    )
    b_all = x_ref[:, INNER : INNER + STATE]
    c_all = x_ref[:, INNER + STATE :]
    aff_ref[...] = dot_rt_exact(c_all, b_all) * inside
    first = column_index((rows, LANES)) < HDIM

    def pair(p, total):
        at = pl.multiple_of(p * LANES, LANES)
        x = x_ref[:, pl.ds(at, LANES)]
        scaled = (x * dtpair[p]).astype(BF16)
        outs = []
        columns = qcol[p]
        for k in (0, 1):
            h = 2 * p + k
            gaps = columns[:, k * HDIM : k * HDIM + 1] - qrow[pl.ds(h, 1), :]
            prod = jnp.exp(jnp.minimum(gaps, 0.0)) * aff_ref[...]
            outs.append(dot(prod.astype(BF16), scaled))
        y = jnp.where(first, outs[0], outs[1]) + x * skip_ref[:, pl.ds(at, LANES)]
        y_ref[:, pl.ds(at, LANES)] = y
        z = inner_ref[:, pl.ds(at, LANES)]
        w = y * (z * sigmoid(z))
        return total + jnp.sum(w * w, axis=1, keepdims=True)

    total = lax.fori_loop(0, PAIRS_OF_HEADS, pair, jnp.zeros((rows, 1), F32))
    scale = lax.rsqrt(total / INNER + EPSILON)

    @pl.loop(0, PAIRS_OF_HEADS)
    def _(p):
        at = pl.multiple_of(p * LANES, LANES)
        z = inner_ref[:, pl.ds(at, LANES)]
        w = y_ref[:, pl.ds(at, LANES)] * (z * sigmoid(z))
        mixed = w * scale * gain_ref[:, pl.ds(at, LANES)]
        mixed_ref[:, pl.ds(at, LANES)] = mixed.astype(BF16)
        turned_ref[pl.ds(at, LANES), :] = mixed.T.astype(BF16)


def mixer_scratch(rows):
    return [
        pltpu.VMEM((rows, CONVCH), F32),
        pltpu.VMEM((PAIRS_OF_HEADS, rows, LANES), F32),
        pltpu.VMEM((HEADS, rows), F32),
        pltpu.VMEM((PAIRS_OF_HEADS, rows, LANES), F32),
        pltpu.VMEM((rows, rows), F32),
    ]


def mixer_forward(inner, taps, heads, skip, gain, position, inside):
    rows = inner.shape[0]
    shape = jax.ShapeDtypeStruct
    return pl.pallas_call(
        mixer_forward_kernel,
        out_shape=[
            shape((rows, INNER), BF16),
            shape((INNER, rows), BF16),
            shape((rows, INNER), F32),
        ],
        in_specs=[VMEM] * 7,
        out_specs=[VMEM] * 3,
        scratch_shapes=mixer_scratch(rows),
        compiler_params=BIG,
        name="mixer_forward",
    )(inner, taps, heads, skip, gain, position, inside)


def mixer_backward_steps(
    inner_ref, taps_ref, heads_ref, skip_ref, gain_ref, position_ref, inside_ref, y_ref, dmixed_ref,
    dinner_ref, dtaps_ref, dgain_ref, dskip_ref, dheads_ref,
    x_ref, qcol, qrow, dtpair, aff_ref, dx_ref, daff_ref, rowsum, stepgrad, colsum,
):
    rows = inner_ref.shape[0]
    position = position_ref[...]
    yield from mixer_setup(
        inner_ref, taps_ref, heads_ref, position, inside_ref[...], x_ref, qcol, qrow, dtpair
    )
    aff_ref[...] = (
        dot_rt_exact(x_ref[:, INNER : INNER + STATE], x_ref[:, INNER + STATE :]) * inside_ref[...].T
    )
    daff_ref[...] = jnp.zeros_like(daff_ref)
    stepgrad[...] = jnp.zeros_like(stepgrad)
    colsum[...] = jnp.zeros_like(colsum)
    lane = column_index((rows, LANES))
    first = lane < HDIM
    yield

    def sums(p, carry):
        squares, product = carry
        at = pl.multiple_of(p * LANES, LANES)
        z = inner_ref[:, pl.ds(at, LANES)]
        w = y_ref[:, pl.ds(at, LANES)] * (z * sigmoid(z))
        g = dmixed_ref[:, pl.ds(at, LANES)] * gain_ref[:, pl.ds(at, LANES)]
        return (
            squares + jnp.sum(w * w, axis=1, keepdims=True),
            product + jnp.sum(w * g, axis=1, keepdims=True),
        )

    zero = jnp.zeros((rows, 1), F32)
    squares, product = lax.fori_loop(0, PAIRS_OF_HEADS, sums, (zero, zero))
    scale = lax.rsqrt(squares / INNER + EPSILON)
    pull = scale * scale * scale * product / INNER
    yield

    def pair(p):
        at = pl.multiple_of(p * LANES, LANES)
        here = pl.ds(at, LANES)
        z = inner_ref[:, here]
        y = y_ref[:, here]
        sig = sigmoid(z)
        silu = z * sig
        w = y * silu
        g = dmixed_ref[:, here]
        dgain_ref[:, here] = jnp.sum(g * w * scale, axis=0, keepdims=True)
        dw = scale * (g * gain_ref[:, here]) - w * pull
        dinner_ref[:, here] = (dw * y * (sig * (1.0 + z * (1.0 - sig)))).astype(BF16)
        dy = dw * silu
        x = x_ref[:, here]
        dskip_ref[:, here] = jnp.sum(dy * x, axis=0, keepdims=True)
        steps = dtpair[p]
        scaled = x * steps
        low = dy.astype(BF16)
        outs = []
        columns = qcol[p]
        for k in (0, 1):
            h = 2 * p + k
            gaps = qrow[pl.ds(h, 1), :] - columns[:, k * HDIM : k * HDIM + 1]
            decay = jnp.exp(jnp.minimum(gaps, 0.0))
            prod = decay * aff_ref[...]
            own = first if k == 0 else jnp.logical_not(first)
            dprod = dot_rt(jnp.where(own, scaled, 0.0).astype(BF16), low)
            daff_ref[...] += dprod * decay
            both = dprod * prod
            rowsum[pl.ds(h, 1), :] = jnp.sum(both, axis=0, keepdims=True)
            away = jnp.sum(both, axis=1, keepdims=True)
            colsum[...] += jnp.where(lane == h, away, 0.0)
            outs.append(dot(prod.astype(BF16), low))
        dscaled = jnp.where(first, outs[0], outs[1])
        dx_ref[:, here] = dscaled * steps + dy * skip_ref[:, here]
        gain_step = dscaled * x
        left = jnp.sum(jnp.where(first, gain_step, 0.0), axis=1, keepdims=True)
        right = jnp.sum(jnp.where(first, 0.0, gain_step), axis=1, keepdims=True)
        stepgrad[...] += jnp.where(lane == 2 * p, left, 0.0) + jnp.where(
            lane == 2 * p + 1, right, 0.0
        )

    for start, end in spans(PAIRS_OF_HEADS, 6):
        pl.loop(start, end)(pair)
        yield

    daff = daff_ref[...] * inside_ref[...].T
    dx_ref[:, INNER : INNER + STATE] = dot_exact(daff, x_ref[:, INNER + STATE :])
    dx_ref[:, INNER + STATE :] = dot_exact(daff.T, x_ref[:, INNER : INNER + STATE])
    yield
    pad = jnp.zeros((LANES - HEADS, rows), F32)
    dsums = jnp.concatenate([rowsum[...], pad], axis=0).T - colsum[...]
    dlog = dot_exact(inside_ref[...].T, dsums)[:, :HEADS]
    raw, step, rates = step_sizes(inner_ref, heads_ref)
    dstep = stepgrad[:, :HEADS] + dlog * rates
    draw = dstep * sigmoid(raw)
    dinner_ref[:, INNER + CONVCH :] = draw.astype(BF16)
    dheads_ref[0:1, :HEADS] = jnp.sum(dlog * step, axis=0, keepdims=True) * rates
    dheads_ref[1:2, :HEADS] = jnp.sum(draw, axis=0, keepdims=True)
    yield

    def conv_back(k):
        here = pl.ds(pl.multiple_of(k * LANES, LANES), LANES)
        there = pl.ds(pl.multiple_of(INNER + k * LANES, LANES), LANES)
        conv_in = inner_ref[:, there]
        taps = taps_ref[:, here]
        before = conv_before(conv_in, taps, position)
        sig = sigmoid(before)
        grad = dx_ref[:, here] * (sig * (1.0 + before * (1.0 - sig)))
        back = grad * taps[TAPS - 1 : TAPS]
        dtaps_ref[TAPS - 1 : TAPS, here] = jnp.sum(grad * conv_in, axis=0, keepdims=True)
        for offset in range(1, TAPS):
            t = TAPS - 1 - offset
            valid = jnp.where(position >= offset, grad, 0.0)
            dtaps_ref[t : t + 1, here] = jnp.sum(
                valid * pltpu.roll(conv_in, offset, 0), axis=0, keepdims=True
            )
            back = back + pltpu.roll(valid, rows - offset, 0) * taps[t : t + 1]
        dinner_ref[:, there] = back.astype(BF16)

    for start, end in spans(CONVCH // LANES, 4):
        pl.loop(start, end)(conv_back)
        yield


def mixer_backward_scratch(rows):
    return mixer_scratch(rows) + [
        pltpu.VMEM((rows, CONVCH), F32),
        pltpu.VMEM((rows, rows), F32),
        pltpu.VMEM((HEADS, rows), F32),
        pltpu.VMEM((rows, LANES), F32),
        pltpu.VMEM((rows, LANES), F32),
    ]


def mixer_backward_shapes(inner, taps):
    shape = jax.ShapeDtypeStruct
    return [
        shape(inner.shape, BF16),
        shape(taps.shape, F32),
        shape((1, INNER), F32),
        shape((1, INNER), F32),
        shape((8, LANES), F32),
    ]


def rotate_rows(front, rear, cosine, sine):
    return front * cosine - rear * sine, rear * cosine + front * sine


def attention_setup(packed_ref, cosine_ref, sine_ref, query, key_rows):
    half = HD // 2
    for h in range(QH + KVH):
        at = h * HD
        turned = rotate_rows(
            packed_ref[at : at + half], packed_ref[at + half : at + HD],
            cosine_ref[...], sine_ref[...],
        )
        both = jnp.concatenate(turned, axis=0)
        if h < QH:
            query[at : at + HD] = both.astype(BF16)
        else:
            key_rows[at - QH * HD : at - (QH - 1) * HD] = both


def turned_probs(keys, query, outside):
    scores = dot(keys, query) * SCORE_SCALE + outside
    expo = jnp.exp(scores - jnp.max(scores, axis=0, keepdims=True))
    return expo / jnp.sum(expo, axis=0, keepdims=True)


def attention_forward_kernel(
    packed_ref, cosine_ref, sine_ref, outside_ref, context_ref, turned_ref, query, key_rows
):
    attention_setup(packed_ref, cosine_ref, sine_ref, query, key_rows)
    keys = key_rows[...].T.astype(BF16)
    values = packed_ref[(QH + KVH) * HD :].astype(BF16)
    for h in range(QH):
        kv = h * KVH // QH
        probs = turned_probs(
            keys[:, kv * HD : (kv + 1) * HD], query[h * HD : (h + 1) * HD], outside_ref[...]
        )
        turned = dot(values[kv * HD : (kv + 1) * HD], probs.astype(BF16))
        turned_ref[h * HD : (h + 1) * HD] = turned.astype(BF16)
    for k in range(QH * HD // LANES):
        here = slice(k * LANES, (k + 1) * LANES)
        context_ref[:, here] = turned_ref[here].astype(F32).T.astype(BF16)


def attention_forward(packed, cosine, sine, outside):
    rows = packed.shape[1]
    shape = jax.ShapeDtypeStruct
    return pl.pallas_call(
        attention_forward_kernel,
        out_shape=[shape((rows, QH * HD), BF16), shape((QH * HD, rows), BF16)],
        in_specs=[VMEM] * 4,
        out_specs=[VMEM] * 2,
        scratch_shapes=[pltpu.VMEM((QH * HD, rows), BF16), pltpu.VMEM((KVH * HD, rows), F32)],
        compiler_params=BIG,
        name="attention_forward",
    )(packed, cosine, sine, outside)


def attention_backward_steps(
    packed_ref, cosine_ref, sine_ref, outside_ref, dcontext_ref, dpacked_ref,
    query, key_rows, grad_rows,
):
    half = HD // 2
    attention_setup(packed_ref, cosine_ref, sine_ref, query, key_rows)
    low_rows = key_rows[...].astype(BF16)
    keys = key_rows[...].T.astype(BF16)
    values = packed_ref[(QH + KVH) * HD :].T.astype(BF16)
    for k in range(QH * HD // LANES):
        here = slice(k * LANES, (k + 1) * LANES)
        grad_rows[here] = dcontext_ref[:, here].astype(F32).T
    yield
    for kv in range(KVH):
        of_kv = slice(kv * HD, (kv + 1) * HD)
        dkey = jnp.zeros((HD, keys.shape[0]), F32)
        dvalue = jnp.zeros((HD, keys.shape[0]), F32)
        for h in range(kv * QH // KVH, (kv + 1) * QH // KVH):
            here = slice(h * HD, (h + 1) * HD)
            probs = turned_probs(keys[:, of_kv], query[here], outside_ref[...])
            grad = grad_rows[here].astype(BF16)
            dprobs = dot(values[:, of_kv], grad)
            dvalue = dvalue + dot_rt(grad, probs.astype(BF16))
            inner = jnp.sum(probs * dprobs, axis=0, keepdims=True)
            dscores = (probs * (dprobs - inner) * SCORE_SCALE).astype(BF16)
            dquery = dot(low_rows[of_kv], dscores)
            dkey = dkey + dot_rt(query[here], dscores)
            turned = rotate_rows(dquery[:half], dquery[half:], cosine_ref[...], -sine_ref[...])
            grad_rows[here] = jnp.concatenate(turned, axis=0)
            yield
        turned = rotate_rows(dkey[:half], dkey[half:], cosine_ref[...], -sine_ref[...])
        at = QH * HD + kv * HD
        grad_rows[at : at + HD] = jnp.concatenate(turned, axis=0)
        at = (QH + KVH) * HD + kv * HD
        grad_rows[at : at + HD] = dvalue
    for k in range((QH + 2 * KVH) * HD // LANES):
        here = slice(k * LANES, (k + 1) * LANES)
        dpacked_ref[:, here] = grad_rows[here].T.astype(BF16)
    yield


def attention_backward_scratch(rows):
    return [
        pltpu.VMEM((QH * HD, rows), BF16),
        pltpu.VMEM((KVH * HD, rows), F32),
        pltpu.VMEM(((QH + 2 * KVH) * HD, rows), F32),
    ]


def host_steps(ins, outs, scratch):
    yield from mixer_backward_steps(*ins[:9], *outs[:5], *scratch[:10])
    yield from attention_backward_steps(*ins[9:], outs[5], *scratch[10:])


def host_shapes(ins):
    rows, wide = ins[0].shape[0], ins[9].shape[0]
    return mixer_backward_shapes(ins[0], ins[1]) + [jax.ShapeDtypeStruct((rows, wide), BF16)]


def host_scratch(ins):
    rows = ins[0].shape[0]
    return mixer_backward_scratch(rows) + attention_backward_scratch(rows)


def host_plain(ins):
    shapes, scratch = host_shapes(ins), host_scratch(ins)

    def kernel(*refs):
        one, two = len(ins), len(ins) + len(shapes)
        run_steps(host_steps(refs[:one], refs[one:two], refs[two:]))

    return pl.pallas_call(
        kernel,
        out_shape=shapes,
        in_specs=[VMEM] * len(ins),
        out_specs=[VMEM] * len(shapes),
        scratch_shapes=scratch,
        compiler_params=BIG,
        name="mixer_attention_backward",
    )(*ins)


def flip(me, bit):
    step = 1 << bit
    return me + step * (1 - 2 * ((me // step) % 2))


def place(bits, free, mine, flipped=()):
    return tuple(
        slice(None) if b in free else 1 - mine[b] if b in flipped else mine[b]
        for b in reversed(range(bits))
    )


def greet(me, bits):
    barrier = pltpu.get_barrier_semaphore()
    for b in range(bits):
        pl.semaphore_signal(barrier, inc=1, device_id=(flip(me, b),), device_id_type=MESH)
    pl.semaphore_wait(barrier, bits)


def remote(me, src, dst, send, recv, bit):
    return pltpu.make_async_remote_copy(
        src_ref=src,
        dst_ref=dst,
        send_sem=send,
        recv_sem=recv,
        device_id=(flip(me, bit),),
        device_id_type=MESH,
    )


def gather_kernel(devices, chunks, events, layers, arrays, *refs):
    bits = devices.bit_length() - 1
    ins = refs[:arrays]
    outs = refs[arrays : arrays + layers * arrays]
    send_sem, recv_sem, csend_sem, crecv_sem, own_sem = refs[arrays + layers * arrays :]
    me = lax.axis_index("dp")
    mine = [(me // (1 << b)) % 2 for b in range(bits)]
    greet(me, bits)
    own, sends, cores, pending = [], [], [], {}
    for c, (l, a, order) in enumerate(chunks):
        here = outs[l * arrays + a].at[place(bits, (), mine)]
        src = ins[a].at[l]
        copy = remote(me, src, here, send_sem.at[c, 0], recv_sem.at[c, 0], order[0])
        copy.start()
        pending[c] = copy
        sends.append(copy)
        local = pltpu.make_async_copy(src, here, own_sem.at[c])
        local.start()
        own.append(local)
    for c, (l, a, order) in enumerate(chunks):
        here = outs[l * arrays + a].at[place(bits, (), mine)]
        copy = remote(me, ins[a].at[l], here, csend_sem.at[c, 0], crecv_sem.at[c, 0], 0)
        copy.start()
        sends.append(copy)
        cores.append(copy)
    for local in own:
        local.wait()
    for c, s in events:
        l, a, order = chunks[c]
        full = outs[l * arrays + a]
        pending[c].wait_recv()
        if s + 1 < bits - 1:
            view = full.at[place(bits, order[: s + 1], mine)]
            copy = remote(
                me, view, view, send_sem.at[c, s + 1], recv_sem.at[c, s + 1], order[s + 1]
            )
            copy.start()
            pending[c] = copy
            sends.append(copy)
        new = full.at[place(bits, order[:s], mine, (order[s],))]
        copy = remote(me, new, new, csend_sem.at[c, s + 1], crecv_sem.at[c, s + 1], 0)
        copy.start()
        sends.append(copy)
        cores.append(copy)
    for copy in sends:
        copy.wait_send()
    for copy in cores:
        copy.wait_recv()


def gather_all(shards, devices):
    bits = devices.bit_length() - 1
    layers = shards[0].shape[0]
    n = len(AG_CHUNKS)
    sent = {(layer, a) for layer, a, _ in AG_CHUNKS}
    outs = [
        jax.ShapeDtypeStruct(
            (2,) * bits + (s.shape[1:] if (layer, a) in sent else (8, 128)), s.dtype
        )
        for layer in range(layers)
        for a, s in enumerate(shards)
    ]
    res = pl.pallas_call(
        functools.partial(gather_kernel, devices, AG_CHUNKS, AG_EVENTS, layers, len(shards)),
        out_shape=outs,
        in_specs=[pl.BlockSpec(memory_space=pltpu.VMEM)] * len(shards),
        out_specs=[pl.BlockSpec(memory_space=pl.ANY)] * len(outs),
        scratch_shapes=[pltpu.SemaphoreType.DMA((n, bits - 1))] * 2
        + [pltpu.SemaphoreType.DMA((n, bits))] * 2
        + [pltpu.SemaphoreType.DMA((n,))],
        compiler_params=pltpu.CompilerParams(collective_id=0, has_side_effects=True),
        name="gather_all",
    )(*shards)
    full = [r.reshape((devices * r.shape[-2], r.shape[-1])) for r in res]
    return [full[l * len(shards) : (l + 1) * len(shards)] for l in range(layers)]


PAIRS = ((0, 0), (1, 2), (0, 1), (2, 2), (3, 3), (4, 4))


def take(refs, *sizes):
    groups, at = [], 0
    for size in sizes:
        groups.append(refs[at : at + size])
        at += size
    return groups + [refs[at:]]


def scatter_kernel(devices, plan, jobs, arrs, counts, *refs):
    chunks, events, row_bits = plan
    bits = devices.bit_length() - 1
    half = devices // 2
    nx, ny, nsmall, nrows, nhost, nhost_out = counts
    na, nc = len(arrs), len(chunks)
    xs, ys, small_in, rows_in, host_in, refs = take(refs, nx, ny, nsmall, nrows, nhost)
    outs, small_out, rows_out, host_out, refs = take(refs, na, nsmall, nrows, nhost_out)
    xr, yr, sums, parts, refs = take(refs, nx, ny, nc, nc * (bits - 1))
    small_mid, small_got, rows_got, refs = take(
        refs, nsmall * (bits - 1), nsmall * bits, nrows * bits
    )
    host_scratch_refs, sems = refs[:-10], refs[-10:]
    xs_s, xs_r, ys_s, ys_r, st_s, st_r, sm_s, sm_r, ro_s, ro_r = sems
    me = lax.axis_index("dp")
    mine = [(me // (1 << b)) % 2 for b in range(bits)]
    greet(me, bits)
    core = mine[0]
    swaps_x, swaps_y, got_x, got_y = {}, {}, set(), set()
    for a, _, _, _ in chunks:
        xi, yi = jobs[a]
        if xi not in swaps_x:
            swaps_x[xi] = remote(
                me, xs[xi].at[:, 1 - core], xr[xi], xs_s.at[xi], xs_r.at[xi], 0
            )
            swaps_x[xi].start()
        if yi not in swaps_y:
            swaps_y[yi] = remote(me, ys[yi], yr[yi], ys_s.at[yi], ys_r.at[yi], 0)
            swaps_y[yi].start()
    sends, pending = [], {}

    def small_send(s):
        src = small_in[0] if s == 0 else small_mid[s - 1]
        copy = remote(me, src, small_got[s], sm_s.at[s], sm_r.at[s], s)
        copy.start()
        pending["small"] = copy
        sends.append(copy)

    def small_receive(s):
        src = small_in[0] if s == 0 else small_mid[s - 1]
        pending["small"].wait_recv()
        total = src[...] + small_got[s][...]
        if s + 1 < bits:
            small_mid[s][...] = total
            small_send(s + 1)
        else:
            small_out[0][...] = total

    def rows_send(s):
        bit = row_bits[s]
        index = tuple(1 - mine[q] if q == bit else slice(None) for q in reversed(range(bits)))
        copy = remote(me, rows_out[0].at[index], rows_got[s], ro_s.at[s], ro_r.at[s], bit)
        copy.start()
        pending["rows"] = copy

    def rows_receive(s):
        pending["rows"].wait_send()
        pending["rows"].wait_recv()

        @pl.loop(0, 1 << (bits - 1))
        def _(j):
            here, there, pos = [], [], bits - 1
            for q in reversed(range(bits)):
                if q == row_bits[s]:
                    here.append(1 - mine[q])
                else:
                    pos -= 1
                    value = (j // (1 << pos)) % 2
                    here.append(value)
                    there.append(value)
            rows_out[0][tuple(here)] = rows_got[s][tuple(there)]

        if s + 1 < bits:
            rows_send(s + 1)

    def send(c, s):
        order = chunks[c][3]
        index = tuple(
            1 - mine[q] if q == order[s] else mine[q] if q in order[:s] else slice(None)
            for q in reversed(range(1, bits))
        )
        copy = remote(
            me,
            sums[c].at[index],
            parts[c * (bits - 1) + s],
            st_s.at[c, s],
            st_r.at[c, s],
            order[s],
        )
        copy.start()
        pending[c] = copy
        sends.append(copy)

    def compute(c):
        a, first, end, _ = chunks[c]
        xi, yi = jobs[a]
        rows = arrs[a][0]
        if xi not in got_x:
            swaps_x[xi].wait_recv()
            got_x.add(xi)
        if yi not in got_y:
            swaps_y[yi].wait_recv()
            got_y.add(yi)

        def tile(start, width, offset):
            left = xs[xi][:, core].reshape(half * rows, -1)
            other = xr[xi][...].reshape(half * rows, -1)
            value = dot(left, ys[yi][:, pl.ds(start, width)])
            value = value + dot(other, yr[yi][:, pl.ds(start, width)])
            sums[c][..., pl.ds(offset, width)] = value.astype(BF16).reshape(
                (2,) * (bits - 1) + (rows, width)
            )

        width, step = end - first, 256
        whole = width // step

        @pl.loop(0, whole)
        def _(i):
            tile(
                pl.multiple_of(first + i * step, 128), step, pl.multiple_of(i * step, 128)
            )

        if width % step:
            tile(first + whole * step, width % step, whole * step)
        send(c, 0)

    def receive(c, s):
        a, first, end, order = chunks[c]
        pending[c].wait_recv()
        fixed = order[: s + 1]
        free = [q for q in reversed(range(1, bits)) if q not in fixed]

        def add(j, last):
            here, there, pos = [], [], len(free)
            for q in reversed(range(1, bits)):
                if q in fixed:
                    here.append(mine[q])
                else:
                    pos -= 1
                    value = (j // (1 << pos)) % 2
                    here.append(value)
                    there.append(value)
            part = parts[c * (bits - 1) + s]
            total = part[tuple(there)].astype(F32) + sums[c][tuple(here)].astype(F32)
            if last:
                outs[a][:, first:end] = total
            else:
                sums[c][tuple(here)] = total.astype(BF16)

        if not free:
            add(0, True)
        else:

            @pl.loop(0, 1 << len(free))
            def _(j):
                add(j, False)

            send(c, s + 1)

    steps = host_steps(host_in, host_out, host_scratch_refs) if nhost else iter(())
    if nsmall:
        small_send(0)
    if nrows:
        fetch = pltpu.make_async_copy(rows_in[0], rows_out[0], ro_s.at[0])
        fetch.start()
        fetch.wait()
        rows_send(0)
    for c, s in events:
        if c == -1:
            small_receive(s)
        elif c == -2:
            rows_receive(s)
        elif c == -3:
            next(steps, None)
        elif s < 0:
            compute(c)
        else:
            receive(c, s)
    run_steps(steps)
    for copy in list(swaps_x.values()) + list(swaps_y.values()) + sends:
        copy.wait_send()


def scatter(plan, jobs, turned, grads, devices, number, small=None, rows=None, host=()):
    chunks = plan[0]
    bits = devices.bit_length() - 1
    nx, ny = len(turned), len(grads)
    half = devices // 2
    split = [x.reshape(half, 2, x.shape[0] // devices, x.shape[1]) for x in turned]
    arrs = [(turned[xi].shape[0] // devices, grads[yi].shape[1]) for xi, yi in jobs]
    smalls = [] if small is None else [small]
    moved = []
    if rows is not None:
        moved.append(rows.reshape((2,) * bits + (rows.shape[0] // devices, rows.shape[1])))
    shape = jax.ShapeDtypeStruct
    extra = host_shapes(host) if host else []
    outs = [shape(size, F32) for size in arrs] + [shape(x.shape, F32) for x in smalls]
    outs += [shape(x.shape, BF16) for x in moved] + extra
    scratch = [pltpu.VMEM((half, x.shape[0] // devices, x.shape[1]), BF16) for x in turned]
    scratch += [pltpu.VMEM(y.shape, BF16) for y in grads]
    for a, first, end, _ in chunks:
        scratch.append(pltpu.VMEM((2,) * (bits - 1) + (arrs[a][0], end - first), BF16))
    for a, first, end, _ in chunks:
        for s in range(bits - 1):
            scratch.append(pltpu.VMEM((2,) * (bits - 2 - s) + (arrs[a][0], end - first), BF16))
    for x in smalls:
        scratch += [pltpu.VMEM(x.shape, F32)] * (2 * bits - 1)
    for x in moved:
        scratch += [pltpu.VMEM(x.shape[1:], BF16)] * bits
    if host:
        scratch += host_scratch(host)
    dma = pltpu.SemaphoreType.DMA
    scratch += [dma((nx,))] * 2 + [dma((ny,))] * 2 + [dma((len(chunks), bits - 1))] * 2
    scratch += [dma((bits,))] * 4
    counts = (nx, ny, len(smalls), len(moved), len(host), len(extra))
    res = pl.pallas_call(
        functools.partial(scatter_kernel, devices, plan, jobs, arrs, counts),
        out_shape=outs,
        in_specs=[VMEM] * (nx + ny + len(smalls))
        + [pl.BlockSpec(memory_space=pl.ANY)] * len(moved)
        + [VMEM] * len(host),
        out_specs=[VMEM] * len(outs),
        scratch_shapes=scratch,
        compiler_params=pltpu.CompilerParams(
            collective_id=number, has_side_effects=True, vmem_limit_bytes=67043328
        ),
        name="scatter",
    )(*split, *grads, *smalls, *moved, *host)
    owned, small_total, back, own_work = take(res, len(arrs), len(smalls), len(moved))
    return owned, small_total, [x.reshape(rows.shape) for x in back], own_work


def scatter_plain(turned, grads, small):
    owned = [
        lax.psum_scatter(
            dot(turned[xi], grads[yi]).astype(BF16), "dp", scatter_dimension=0, tiled=True
        ).astype(F32)
        for xi, yi in PAIRS
    ]
    return owned + [lax.psum(small, "dp")]


def doc_layout(doc_lengths, rows_count):
    rows_index = jnp.arange(rows_count, dtype=jnp.int32)
    doc_ends = jnp.cumsum(doc_lengths, dtype=jnp.int32)
    later = (rows_index[:, None] >= doc_ends[None, :]).astype(jnp.int32)
    segment = jnp.sum(later, axis=1, dtype=jnp.int32)
    position = rows_index - jnp.sum(later * doc_lengths[None, :], axis=1, dtype=jnp.int32)
    return (segment, position)


def inverse_rms(values):
    return lax.rsqrt(jnp.mean(values * values, axis=-1, keepdims=True) + EPSILON)


def norm_backward(grad, values, scale, gain):
    normed = values * scale
    grad_gain = jnp.sum(grad * normed, axis=0)
    inner = grad * gain
    return scale * (inner - normed * jnp.mean(inner * normed, axis=-1, keepdims=True)), grad_gain


def layer_forward(hidden, weights, small, layout):
    w_in, w_mix, w_qkv, w_attn, w_gate_up, w_down = weights
    gains, taps, gain_inner, heads, skip = small
    position, inside, outside, cosine, sine = layout
    scale = inverse_rms(hidden)
    normed = (hidden * scale * gains[0]).astype(BF16)
    inner = dot(normed, w_in)
    packed = lax.dot_general(
        w_qkv, normed, (((0,), (1,)), ((), ())), preferred_element_type=F32
    )
    mixed, mixed_rows, y = mixer_forward(inner, taps, heads, skip, gain_inner, position, inside)
    context, context_rows = attention_forward(packed, cosine, sine, outside)
    middle = hidden + dot(mixed, w_mix) + dot(context, w_attn)
    scale_two = inverse_rms(middle)
    normed_two = (middle * scale_two * gains[1]).astype(BF16)
    both = dot(normed_two, w_gate_up)
    active = (jax.nn.silu(both[:, :FF]) * both[:, FF:]).astype(BF16)
    out = middle + dot(active, w_down)
    turned = [normed.T, mixed_rows, context_rows, normed_two.T, active.T]
    return out, (hidden, scale, inner, packed, y, middle, scale_two, both, turned)


def backward_start(grad, kept, weights, small, layout):
    w_in, w_mix, w_qkv, w_attn, w_gate_up, w_down = weights
    gains, taps, gain_inner, heads, skip = small
    position, inside, outside, cosine, sine = layout
    hidden, scale, inner, packed, y, middle, scale_two, both, turned = kept
    ddown = grad.astype(BF16)
    dactive = dot_rt(ddown, w_down)
    gate, up = both[:, :FF], both[:, FF:]
    sig = jax.nn.sigmoid(gate)
    dgate = dactive * up * (sig * (1.0 + gate * (1.0 - sig)))
    dboth = jnp.concatenate([dgate, dactive * (gate * sig)], axis=1).astype(BF16)
    dmiddle, dgain_two = norm_backward(dot_rt(dboth, w_gate_up), middle, scale_two, gains[1])
    dmiddle = grad + dmiddle
    dbranch = dmiddle.astype(BF16)
    dmixed = dot_rt(dbranch, w_mix)
    dcontext = dot_rt(dbranch, w_attn).astype(BF16)
    host = (inner, taps, heads, skip, gain_inner, position, inside, y, dmixed)
    host += (packed, cosine, sine, outside, dcontext)
    return dmiddle, dgain_two, dbranch, dboth, ddown, host


def backward_end(dmiddle, dgain_two, kept, weights, small, done):
    w_in, w_qkv = weights[0], weights[2]
    hidden, scale = kept[:2]
    dinner, dtaps, dgain_inner, dskip, dheads, dpacked = done
    dnormed = dot_rt(dinner, w_in) + dot_rt(dpacked, w_qkv)
    dhidden, dgain = norm_backward(dnormed, hidden, scale, small[0][0])
    flat = [dgain, dgain_two, dtaps.reshape(-1), dgain_inner[0], dheads[0, :HEADS]]
    flat += [jnp.sum(dskip.reshape(HEADS, HDIM), axis=1), dheads[1, :HEADS]]
    flat = jnp.concatenate(flat)
    lines = -(-flat.shape[0] // 1024) * 8
    small_sum = jnp.pad(flat, (0, lines * 128 - flat.shape[0])).reshape(lines, 128)
    return dmiddle + dhidden, small_sum


def shards(
    tokens,
    cotangent,
    destination,
    lengths,
    norm_gains,
    in_proj,
    conv_weight,
    ssm_gain,
    mixer_out,
    qkv_proj,
    attn_out,
    gate_up,
    down_proj,
    a_log,
    d_skip,
    dt_bias,
):
    devices = lax.axis_size("dp")
    me = lax.axis_index("dp")
    rows_here, width = tokens.shape
    share = rows_here // devices
    own_kernels = devices == 32
    index = jnp.arange(rows_here, dtype=jnp.int32)
    slabs = destination.reshape(devices, rows_here)

    own = lax.dynamic_slice_in_dim(slabs, me, 1, 0)[0] // rows_here
    same = (own[:, None] == own[None, :]) & (index[None, :] < index[:, None])
    slot = own * share + jnp.sum(same.astype(jnp.int32), axis=1)
    leave = (slot[None, :] == index[:, None]).astype(BF16)
    outgoing = [dot(leave, x).astype(BF16) for x in (tokens, cotangent)]

    def exchange(rows):
        split = rows.reshape(devices, share, width)
        moved = lax.all_to_all(split, "dp", split_axis=0, concat_axis=0, tiled=True)
        return moved.reshape(rows_here, width)

    arrived = [exchange(x) for x in outgoing]

    local = slabs - me * rows_here
    mask = ((local >= 0) & (local < rows_here)).astype(BF16)
    below = (index[:, None] < index[None, :]).astype(BF16)
    rank = dot(mask, below).astype(jnp.int32)
    order = rank + share * jnp.arange(devices, dtype=jnp.int32)[:, None]
    hits = local.reshape(-1)[None, :] == index[:, None]
    taken = jnp.sum(jnp.where(hits, order.reshape(-1)[None, :], 0), axis=1)
    enter = (taken[:, None] == index[None, :]).astype(BF16)
    hidden = dot(enter, arrived[0])
    upstream = dot(enter, arrived[1])

    segment, position = doc_layout(lengths[0], rows_here)
    inside = (segment[:, None] == segment[None, :]) & (index[:, None] >= index[None, :])
    inverse = ROPE_BASE ** (-(jnp.arange(HD // 2, dtype=F32) * 2.0 / HD))
    angles = position.astype(F32)[:, None] * inverse[None, :]
    outside = jnp.where(inside.T, 0.0, -1e30)
    layout = (position[:, None], inside.astype(F32), outside, jnp.cos(angles).T, jnp.sin(angles).T)

    matrices = (in_proj, mixer_out, qkv_proj, attn_out, gate_up, down_proj)
    gain_part, conv_part, inner_part = (x.shape[-1] for x in (norm_gains, conv_weight, ssm_gain))
    packed = jnp.concatenate(
        [norm_gains.reshape(LAYERS, -1), conv_weight.reshape(LAYERS, -1), ssm_gain], axis=1
    )
    used = packed.shape[1]
    if own_kernels:
        room = SMALL_ROWS * 128
        padded = jnp.pad(packed, ((0, 0), (0, room - used))).reshape(LAYERS, SMALL_ROWS, 128)
        gathered = gather_all(list(matrices) + [padded], devices)
        weights = [g[:-1] for g in gathered]
        late = LATE_ARRAY
        tied = matrices[late][1] + gathered[0][-1][:1, :1] * 0
        weights[1][late] = lax.all_gather(tied, "dp", axis=0, tiled=True)
        smalls = [g[-1].reshape(devices, room)[:, :used] for g in gathered]
    else:
        weights = [
            [lax.all_gather(x[layer], "dp", axis=0, tiled=True) for x in matrices]
            for layer in range(LAYERS)
        ]
        every = lax.all_gather(packed, "dp", axis=0)
        smalls = [every[:, layer] for layer in range(LAYERS)]

    def spread(piece, count):
        shaped = piece.reshape(devices, count, -1)
        return jnp.swapaxes(shaped, 0, 1).reshape(count, -1).astype(F32)

    def small_of(layer):
        both = smalls[layer]
        mid = 2 * gain_part
        heads = jnp.stack([a_log[layer], d_skip[layer], dt_bias[layer]])
        return (
            spread(both[:, :mid], 2),
            spread(both[:, mid : mid + TAPS * conv_part], TAPS),
            spread(both[:, mid + TAPS * conv_part :], 1),
            jnp.pad(heads, ((0, 5), (0, LANES - HEADS))),
            jnp.repeat(d_skip[layer], HDIM)[None],
        )

    params = [small_of(layer) for layer in range(LAYERS)]

    kept = [None] * LAYERS
    for layer in range(LAYERS):
        hidden, kept[layer] = layer_forward(hidden, weights[layer], params[layer], layout)

    def permute_back(choice, rows):
        return lax.dot_general(
            choice, rows.astype(BF16), (((0,), (0,)), ((), ())), preferred_element_type=F32
        )

    top, low = 1, 0
    start = backward_start(upstream, kept[top], weights[top], params[top], layout)
    dmiddle, dgain_two, dbranch, dboth, ddown, host = start
    if own_kernels:
        up_down, _, _, done = scatter(
            PLAN_A, ((0, 0), (1, 1)), kept[top][-1][3:], [dboth, ddown], devices, 1, host=host
        )
    else:
        done = host_plain(host)
    flowing, small_top = backward_end(
        dmiddle, dgain_two, kept[top], weights[top], params[top], done
    )
    turned_top = kept[top][-1]
    grads_top = [done[0], done[5], dbranch, dboth, ddown]

    start = backward_start(flowing, kept[low], weights[low], params[low], layout)
    dmiddle, dgain_two, dbranch, dboth, ddown, host = start
    leaving = permute_back(enter, hidden).astype(BF16)
    turned_low = kept[low][-1]
    if own_kernels:
        second, sum_top, home, done = scatter(
            PLAN_B,
            ((0, 0), (1, 2), (0, 1), (2, 2), (3, 3), (4, 4)),
            turned_top[:3] + turned_low[3:],
            grads_top[:3] + [dboth, ddown],
            devices,
            2,
            small=small_top,
            rows=leaving,
            host=host,
        )
    else:
        done = host_plain(host)
    flowing, small_low = backward_end(
        dmiddle, dgain_two, kept[low], weights[low], params[low], done
    )
    grads_low = [done[0], done[5], dbranch, dboth, ddown]
    leaving_grad = permute_back(enter, flowing).astype(BF16)
    if own_kernels:
        third, sum_low, home_grad, _ = scatter(
            PLAN_C,
            ((0, 0), (1, 2), (0, 1), (2, 2)),
            turned_low[:3],
            grads_low[:3],
            devices,
            3,
            small=small_low,
            rows=leaving_grad,
        )
        home, home_grad = home[0], home_grad[0]
        owned = [third + second[4:] + sum_low, second[:4] + up_down + sum_top]
    else:
        owned = [
            scatter_plain(turned_low, grads_low, small_low),
            scatter_plain(turned_top, grads_top, small_top),
        ]
        home, home_grad = exchange(leaving), exchange(leaving_grad)
    out_tokens = permute_back(leave, home).astype(BF16)
    in_grad = permute_back(leave, home_grad)

    big = [jnp.stack([owned[layer][k] for layer in range(LAYERS)]) for k in range(6)]
    totals = jnp.stack([owned[layer][6].reshape(-1) for layer in range(LAYERS)])
    model = gain_part * devices
    sizes = (2 * model, TAPS * CONVCH, INNER, HEADS, HEADS, HEADS)
    pieces, at = [], 0
    for size in sizes:
        pieces.append(totals[:, at : at + size])
        at += size

    def mine(piece, count, part):
        shaped = piece.reshape(LAYERS, count, devices * part)
        return lax.dynamic_slice_in_dim(shaped, me * part, part, 2)

    return (
        out_tokens,
        in_grad,
        mine(pieces[0], 2, gain_part),
        big[0],
        mine(pieces[1], TAPS, conv_part),
        mine(pieces[2], 1, inner_part)[:, 0],
        big[1],
        big[2],
        big[3],
        big[4],
        big[5],
        pieces[3],
        pieces[4],
        pieces[5],
    )


def solution(mesh):
    placed = (
        P("dp", None),
        P("dp", None),
        P(),
        P("dp", None),
        P(None, None, "dp"),
        P(None, "dp", None),
        P(None, None, "dp"),
        P(None, "dp"),
        P(None, "dp", None),
        P(None, "dp", None),
        P(None, "dp", None),
        P(None, "dp", None),
        P(None, "dp", None),
        P(),
        P(),
        P(),
    )
    return jax.shard_map(
        shards,
        mesh=mesh,
        in_specs=placed,
        out_specs=(
            P("dp", None),
            P("dp", None),
            P(None, None, "dp"),
            P(None, "dp", None),
            P(None, None, "dp"),
            P(None, "dp"),
            P(None, "dp", None),
            P(None, "dp", None),
            P(None, "dp", None),
            P(None, "dp", None),
            P(None, "dp", None),
            P(),
            P(),
            P(),
        ),
        check_vma=False,
    )
```

time: 937 us -> 675 us (0.72)
  matrix products: 183 us -> 78.8 us
  local copies, waits for them, and re-layouts: 81.7 us -> 26.8 us
  other arithmetic: 78.5 us -> 26.6 us
  Pallas kernels: 548 us -> 507 us
  starting transfers between devices: 20 us -> 6.45 us
  between operations: 3.34 us -> 16.1 us
    dot_general x30 -> x6, matrix products: 110 us -> 12.5 us  [the longest x4 9.32 us: permute_back(): lax.dot_general(choice, rows.astype(BF16), (((0,), (0,)), ((), ())), pref...]
    pallas_call x3 -> x8, Pallas kernels: 548 us -> 507 us  [the longest x3 280 us: scatter(): pl.pallas_call(functools.partial(scatter_kernel, devices, plan, jobs, arr...]
    reduce_sum x11 -> x2, other arithmetic: 33.9 us -> 0.23 us  [backward_end(): flat += [jnp.sum(dskip.reshape(HEADS, HDIM), axis=1), dheads[1, :HEADS]]]
    unnamed x422 -> x188, local copies, waits for them, and re-layouts: 21 us -> 5.87 us
    reshape x20 -> x6, local copies, waits for them, and re-layouts: 15.2 us -> 1.42 us  [the longest x2 1.25 us: backward_end(): jnp.pad(flat, (0, lines * 128 - flat.shape[0])).reshape(lines, 128)]
    all_to_all x4 -> x2, starting transfers between devices: 20 us -> 6.41 us  [exchange(): moved = lax.all_to_all(split, 'dp', split_axis=0, concat_axis=0, tiled=True)]
    mul x7 -> x0, other arithmetic: 11.3 us -> none  [the longest x2 4.94 us: mixer_core(): conv_out = jax.nn.silu(causal_conv(conv_in, kernel, position))]
    mul x11 -> x0, local copies, waits for them, and re-layouts: 10.4 us -> none  [the longest x2 6.13 us: mixer_core(): return scanned.reshape(rows_count, INNER) * jax.nn.silu(gate_z)]
  transfers between devices with their start and end apart: 4 -> 3, of which waited for: 2 -> 1; matrix products, arithmetic and copies ran while one was open for 13% -> 7% of each run, Pallas kernels for 26% -> 6%
where the time goes in v4:
time: 675 us; the launch traced here: 670 us
  Pallas kernels  507 us (75%)
  matrix products  78.8 us (12%)
  local copies, waits for them, and re-layouts  26.8 us (4%)
  other arithmetic  26.6 us (4%)
  between operations  16.1 us (2%)
  waiting for transfers between devices  8.18 us (1%)
    pallas_call x3, Pallas kernels, scatter(): pl.pallas_call(functools.partial(scatter_kernel, devices, plan, jobs, arr...  280 us
    pallas_call x1, Pallas kernels, gather_all(): pl.pallas_call(functools.partial(gather_kernel, devices, AG_CHUNKS, AG_EV...  187 us
    dot_general x14, matrix products, dot(): return jnp.dot(left, right, preferred_element_type=F32)  35.2 us
    dot_general x12, matrix products, dot_rt(): lax.dot_general(left, right, (((1,), (1,)), ((), ())), preferred_element_...  31.1 us
    pallas_call x2, Pallas kernels, mixer_forward(): pl.pallas_call(mixer_forward_kernel, out_shape=[shape((rows, INNER), BF16...  30.9 us
  transfers between devices with their start and end apart: 3, of which 1 were waited for; matrix products, arithmetic and copies ran while one was open for 7% of the time, Pallas kernels for 6%

profile of v4, /device:TPU:0, one launch (start us, length us, event | category | flops | bytes accessed | tf_op | source)
XLA Modules:
  0.0 670.3 jit_solution(10787227859165858404)
XLA Ops:
  10.2 186.8 %gather_all.1 = (bf16[2,2,2,2,2,32,3352]{6,5,4,3,2,1,0:T(8,128)(2,1)}, bf16[2,2,2,2,2,48,1024]{6,5,4,3,2,1,0:T(8,128)(2,1)}, bf16[2,2,2,2,2,32,768]{6,5,4,3,2,1,...) custom-call(bf16[2,32,3352]{2,1,0:T(8,128)(2,1)} %refs_0_.1, ...), custom_call_target="tpu_custom_call" | custom-call | tf_op jit(solution)/shard_map/gather_all/pallas_call | solution.py:579
  199.0 1.7 slice_add_fusion
  202.1 2.6 all-to-all-start
  217.8 8.2 %all-to-all-done = bf16[32,8,1024]{2,1,0:T(8,128)(2,1)S(1)} async-done(((bf16[32,8,1024]{2,1,0:T(8,128)(2,1)}), bf16[32,8,1024]{2,1,0:T(8,128)(2,1)S(1)}, u32[]{:S(2)}, u32[]{:S(2)}) %all-to-all-start) | async-done | bytes 524320 | tf_op jit(solution)/shard_map/all_to_all | solution.py:958
  225.9 3.8 all-to-all-start.1
  231.8 4.7 attention_forward.2
  236.5 7.0 %fusion.62.inner_ref.refs_12_ = f32[256,3352]{1,0:T(8,128)} fusion(bf16[1024,3352]{1,0:T(8,128)(2,1)} %bitcast.179, f32[256,1024]{1,0:T(8,128)S(1)} %get-tuple-element.163, f32[1024]{0:T(1024)S(1)} %mul.344, f32[256]{0:T(256)S(1)} %add_rsqrt_fusion.3), kind=kOutput, calls=%fused_computation.197 | convolution fusion | flops 1758199808 | bytes 11351040 | tf_op jit(solution)/shard_map/dot_general | solution.py:40
  243.5 15.3 %mixer_forward.2 = (bf16[256,1536]{1,0:T(8,128)(2,1)}, bf16[1536,256]{1,0:T(8,128)(2,1)}, f32[256,1536]{1,0:T(8,128)}) custom-call(f32[256,3352]{1,0:T(8,128)} %fusion.62.inner_ref.refs_12_, f32[4,1792]{1,0:T(4,128)} %reshape.396.taps_ref.refs_13_, f32[8,128]{1,0:T(8,128)} %select_maximum_fusion.2.heads_ref.refs_14_, ...), custom_call_target="tpu_custom_call" | custom-call | tf_op jit(solution)/shard_map/mixer_forward/pallas_call | solution.py:190
  258.9 2.2 convolution_add_fusion.5
  261.7 6.2 fusion.53
  270.6 1.6 fusion.65.packed_ref.refs_13_
  272.8 3.9 fusion.64.inner_ref.refs_4_
  276.9 4.7 attention_forward.3
  284.9 15.6 %mixer_forward.3 = (bf16[256,1536]{1,0:T(8,128)(2,1)}, bf16[1536,256]{1,0:T(8,128)(2,1)}, f32[256,1536]{1,0:T(8,128)}) custom-call(f32[256,3352]{1,0:T(8,128)} %fusion.64.inner_ref.refs_4_, f32[4,1792]{1,0:T(4,128)} %reshape.398.taps_ref.refs_5_, f32[8,128]{1,0:T(8,128)} %select_maximum_fusion.heads_ref.refs_6_, ...), custom_call_target="tpu_custom_call" | custom-call | tf_op jit(solution)/shard_map/mixer_forward/pallas_call | solution.py:190
  300.6 2.2 convolution_add_fusion.4
  303.4 2.5 fusion.61
  305.9 5.9 fusion.2
  311.9 3.0 multiply_convert_fusion.3
  314.9 3.1 multiply_reduce_fusion.4
  320.7 2.2 fusion.66.refs_12_
  326.8 69.0 %scatter.3 = (f32[32,4096]{1,0:T(8,128)}, f32[64,1024]{1,0:T(8,128)}, bf16[256,3352]{1,0:T(8,128)(2,1)}, f32[4,1792]{1,0:T(4,128)}, f32[1,1536]{1,0:T(1,128)}, /...) custom-call(bf16[16,2,32,256]{3,2,1,0:T(8,128)(2,1)} %bitcast.197, ...), custom_call_target="tpu_custom_call" | custom-call | tf_op jit(solution)/shard_map/scatter/pallas_call | solution.py:820
  395.9 5.8 fusion.67
  404.2 1.7 copy-done.5
  405.9 2.0 multiply_convert_fusion.1
  408.5 3.1 multiply_reduce_fusion.1
  414.4 2.2 fusion.68.refs_20_
  416.6 4.4 convolution_convert_fusion.2
  421.1 3.1 pad_maximum_fusion.1.refs_8_
  427.0 130.4 %scatter.4 = (f32[32,3352]{1,0:T(8,128)}, f32[48,1024]{1,0:T(8,128)}, f32[32,768]{1,0:T(8,128)}, f32[16,1024]{1,0:T(8,128)}, f32[32,4096]{1,0:T(8,128)}, /*index...) custom-call(bf16[16,2,32,256]{3,2,1,0:T(8,128)(2,1)} %bitcast.195, ...), custom_call_target="tpu_custom_call" | custom-call | tf_op jit(solution)/shard_map/scatter/pallas_call | solution.py:820
  557.4 5.8 fusion.69
  567.2 80.8 %scatter.5 = (f32[32,3352]{1,0:T(8,128)}, f32[48,1024]{1,0:T(8,128)}, f32[32,768]{1,0:T(8,128)}, f32[16,1024]{1,0:T(8,128)}, f32[88,128]{1,0:T(8,128)}, /*index=5*/bf16[2,2,2,2,2,8,1024]{6,5,4,3,2,1,0:T(8,128)(2,1)}) custom-call(bf16[16,2,32,256]{3,2,1,0:T(8,128)(2,1)} %bitcast.198, bf16[16,2,48,256]{3,2,1,0:T(8,128)(2,1)} %bitcast.202, ...), custom_call_target="tpu_custom_call" | custom-call | tf_op jit(solution)/shard_map/scatter/pallas_call | solution.py:820
  652.7 2.4 fusion.18
  (311 shorter events, 60.2 us)
Async XLA Ops:
  7.2 193.5 %copy-start.55 = (s32[8192]{0:T(1024)S(1)}, s32[8192]{0:T(1024)}, u32[]{:S(2)}) copy-start(s32[8192]{0:T(1024)} %param.18) | copy-start | bytes 98308
  7.2 193.8 %copy-start.34 = (bf16[256,1024]{1,0:T(8,128)(2,1)S(1)}, bf16[256,1024]{1,0:T(8,128)(2,1)}, u32[]{:S(2)}) copy-start(bf16[256,1024]{1,0:T(8,128)(2,1)} %param.16) | copy-start | bytes 1572868
  7.2 298.7 %all-gather.3.cloned.1.call-start = ((), (), s32[]{:S(2)}) async-start(), calls=%async_computation.2 | async-start | bytes 8650752 | tf_op jit(solution)/shard_map/all_gather | solution.py:994
  196.9 7.8 %copy-start.54 = (bf16[2,2,2,2,2,16,128]{6,5,4,3,2,1,0:T(8,128)(2,1)S(1)}, bf16[2,2,2,2,2,16,128]{6,5,4,3,2,1,0:T(8,128)(2,1)}, u32[]{:S(2)}) copy-start(bf16[2,2,2,2,2,16,128]{6,5,4,3,2,1,0:T(8,128)(2,1)} %get-tuple-element.65) | copy-start | bytes 393220
  197.0 7.9 %copy-start.53 = (bf16[2,2,2,2,2,16,128]{6,5,4,3,2,1,0:T(8,128)(2,1)S(1)}, bf16[2,2,2,2,2,16,128]{6,5,4,3,2,1,0:T(8,128)(2,1)}, u32[]{:S(2)}) copy-start(bf16[2,2,2,2,2,16,128]{6,5,4,3,2,1,0:T(8,128)(2,1)} %get-tuple-element.74) | copy-start | bytes 393220
  197.0 8.1 %copy-start.82 = (s32[1,4]{1,0:T(1,128)S(1)}, s32[1,4]{1,0:T(1,128)}, u32[]{:S(2)}) copy-start(s32[1,4]{1,0:T(1,128)} %param.19) | copy-start | bytes 52
  197.0 8.3 %copy-start.81 = (f32[2,24]{1,0:T(2,128)S(1)}, f32[2,24]{1,0:T(2,128)}, u32[]{:S(2)}) copy-start(f32[2,24]{1,0:T(2,128)} %param.31) | copy-start | bytes 580
  197.0 8.3 %copy-start.79 = (f32[2,24]{1,0:T(2,128)S(1)}, f32[2,24]{1,0:T(2,128)}, u32[]{:S(2)}) copy-start(f32[2,24]{1,0:T(2,128)} %param.30) | copy-start | bytes 580
  197.0 8.3 %copy-start.80 = (f32[2,24]{1,0:T(2,128)S(1)}, f32[2,24]{1,0:T(2,128)}, u32[]{:S(2)}) copy-start(f32[2,24]{1,0:T(2,128)} %param.29) | copy-start | bytes 580
  197.0 9.3 %copy-start.35 = (bf16[256,1024]{1,0:T(8,128)(2,1)S(1)}, bf16[256,1024]{1,0:T(8,128)(2,1)}, u32[]{:S(2)}) copy-start(bf16[256,1024]{1,0:T(8,128)(2,1)} %param.17) | copy-start | bytes 1572868
  201.0 6.7 copy-start.66
  202.1 23.8 %all-to-all-start = ((bf16[32,8,1024]{2,1,0:T(8,128)(2,1)}), bf16[32,8,1024]{2,1,0:T(8,128)(2,1)S(1)}, u32[]{:S(2)}, u32[]{:S(2)}) async-start(bf16[32,8,1024]{2,1,0:T(8,128)(2,1)} %fusion.7), calls=%async_computation | async-start | bytes 1048576 | tf_op jit(solution)/shard_map/all_to_all | solution.py:958
  209.3 67.4 %copy-start.41 = (f32[1024]{0:T(1024)}, f32[1024]{0:T(1024)S(1)}, u32[]{:S(2)}) copy-start(f32[1024]{0:T(1024)S(1)} %mul.344) | copy-start | bytes 12292
  210.1 20.1 %copy-start.16 = (bf16[2,2,2,2,2,32,768]{6,5,4,3,2,1,0:T(8,128)(2,1)S(1)}, bf16[2,2,2,2,2,32,768]{6,5,4,3,2,1,0:T(8,128)(2,1)}, u32[]{:S(2)}) copy-start(bf16[2,2,2,2,2,32,768]{6,5,4,3,2,1,0:T(8,128)(2,1)} %get-tuple-element.69) | copy-start | bytes 4718596
  211.7 49.9 %copy-start.51 = (f32[1024]{0:T(1024)}, f32[1024]{0:T(1024)S(1)}, u32[]{:S(2)}) copy-start(f32[1024]{0:T(1024)S(1)} %mul.356) | copy-start | bytes 12292
  211.8 61.0 %copy-start.43 = (f32[1024]{0:T(1024)}, f32[1024]{0:T(1024)S(1)}, u32[]{:S(2)}) copy-start(f32[1024]{0:T(1024)S(1)} %mul.365) | copy-start | bytes 12292
  217.8 85.6 %copy-start.68 = (s32[256]{0:T(256)}, s32[256]{0:T(256)S(1)}, u32[]{:S(2)}) copy-start(s32[256]{0:T(256)S(1)} %select_reduce_fusion) | copy-start | bytes 3076
  225.9 77.4 %all-to-all-start.1 = ((bf16[32,8,1024]{2,1,0:T(8,128)(2,1)}), bf16[32,8,1024]{2,1,0:T(8,128)(2,1)}, u32[]{:S(2)}, u32[]{:S(2)}) async-start(bf16[32,8,1024]{2,1,0:T(8,128)(2,1)} %fusion.8), calls=%async_computation.1 | async-start | bytes 1048576 | tf_op jit(solution)/shard_map/all_to_all | solution.py:958
  230.2 46.5 %copy-start = (f32[256,1024]{1,0:T(8,128)}, f32[256,1024]{1,0:T(8,128)S(1)}, u32[]{:S(2)}) copy-start(f32[256,1024]{1,0:T(8,128)S(1)} %get-tuple-element.163) | copy-start | bytes 3145732
  230.2 46.5 %copy-start.60 = (f32[256]{0:T(256)}, f32[256]{0:T(256)S(1)}, u32[]{:S(2)}) copy-start(f32[256]{0:T(256)S(1)} %add_rsqrt_fusion.3) | copy-start | bytes 3076
  243.5 15.3 %copy-start.6 = (bf16[2,2,2,2,2,48,1024]{6,5,4,3,2,1,0:T(8,128)(2,1)S(1)}, bf16[2,2,2,2,2,48,1024]{6,5,4,3,2,1,0:T(8,128)(2,1)}, u32[]{:S(2)}) copy-start(bf16[2,2,2,2,2,48,1024]{6,5,4,3,2,1,0:T(8,128)(2,1)} %get-tuple-element.68) | copy-start | bytes 9437188
  261.7 11.1 %slice-start.4 = ((s8[7077888]{0:T(1024)(128)(4,1)}), s8[4194304]{0:T(1024)(128)(4,1)S(1)}, s32[]{:S(2)}) async-start(s8[7077888]{0:T(1024)(128)(4,1)} %bitcast.182), calls=%async_computation.7 | async-start | bytes 8388608
  269.4 31.1 %copy-start.2 = (f32[256,1024]{1,0:T(8,128)}, f32[256,1024]{1,0:T(8,128)S(1)}, u32[]{:S(2)}) copy-start(f32[256,1024]{1,0:T(8,128)S(1)} %get-tuple-element.167) | copy-start | bytes 3145732
  284.9 15.6 %copy-start.8 = (bf16[2,2,2,2,2,48,1024]{6,5,4,3,2,1,0:T(8,128)(2,1)S(1)}, bf16[2,2,2,2,2,48,1024]{6,5,4,3,2,1,0:T(8,128)(2,1)}, u32[]{:S(2)}) copy-start(bf16[2,2,2,2,2,48,1024]{6,5,4,3,2,1,0:T(8,128)(2,1)} %get-tuple-element.80) | copy-start | bytes 9437188
  303.3 14.7 %copy-start.12 = (f32[256,1024]{1,0:T(8,128)}, f32[256,1024]{1,0:T(8,128)S(1)}, u32[]{:S(2)}) copy-start(f32[256,1024]{1,0:T(8,128)S(1)} %get-tuple-element.171) | copy-start | bytes 3145732
  305.9 9.0 %slice-start.2 = ((s8[8388608]{0:T(1024)(128)(4,1)}), s8[4194304]{0:T(1024)(128)(4,1)S(1)}, s32[]{:S(2)}) async-start(s8[8388608]{0:T(1024)(128)(4,1)} %bitcast.173), calls=%async_computation.5 | async-start | bytes 8388608
  648.0 7.1 %copy-start.36 = (bf16[2,2,2,2,2,8,1024]{6,5,4,3,2,1,0:T(8,128)(2,1)S(1)}, bf16[2,2,2,2,2,8,1024]{6,5,4,3,2,1,0:T(8,128)(2,1)}, u32[]{:S(2)}) copy-start(bf16[2,2,2,2,2,8,1024]{6,5,4,3,2,1,0:T(8,128)(2,1)} %get-tuple-element.92) | copy-start | bytes 1572868
  648.0 7.1 %copy-start.67 = (s32[1,256]{1,0:T(1,128)S(1)}, s32[1,256]{1,0:T(1,128)}, u32[]{:S(2)}) copy-start(s32[1,256]{1,0:T(1,128)} %copy-done.66) | copy-start | bytes 3076
  648.0 8.2 %copy-start.47 = (f32[64,1024]{1,0:T(8,128)S(1)}, f32[64,1024]{1,0:T(8,128)}, u32[]{:S(2)}) copy-start(f32[64,1024]{1,0:T(8,128)} %get-tuple-element.115) | copy-start | bytes 786436
  648.0 8.2 %copy-start.48 = (f32[64,1024]{1,0:T(8,128)S(1)}, f32[64,1024]{1,0:T(8,128)}, u32[]{:S(2)}) copy-start(f32[64,1024]{1,0:T(8,128)} %get-tuple-element.114) | copy-start | bytes 786436
  650.2 6.9 %copy-start.37 = (f32[32,4096]{1,0:T(8,128)S(1)}, f32[32,4096]{1,0:T(8,128)}, u32[]{:S(2)}) copy-start(f32[32,4096]{1,0:T(8,128)} %get-tuple-element.113) | copy-start | bytes 1572868
  650.2 6.9 %copy-start.38 = (f32[32,4096]{1,0:T(8,128)S(1)}, f32[32,4096]{1,0:T(8,128)}, u32[]{:S(2)}) copy-start(f32[32,4096]{1,0:T(8,128)} %get-tuple-element.112) | copy-start | bytes 1572868
  (63 other events, 223.7 us)
Sparse Core Ops, SparseCore 0:
  200.8 85.9 all-gather.2

commit v5 on v4

--- a/solution.py
+++ b/solution.py
@@ -28,9 +28,9 @@
 
 AG_CHUNKS = [(0, 6, (4, 3, 2, 1)), (1, 6, (4, 3, 2, 1)), (1, 0, (4, 3, 1, 2)), (1, 3, (4, 3, 2, 1)), (1, 2, (4, 3, 2, 1)), (0, 2, (4, 3, 2, 1)), (1, 5, (4, 3, 2, 1)), (0, 0, (4, 3, 1, 2)), (0, 3, (1, 4, 3, 2)), (0, 5, (4, 3, 2, 1)), (0, 4, (1, 2, 4, 3)), (0, 1, (1, 2, 4, 3)), (1, 1, (4, 3, 2, 1))]
 AG_EVENTS = [(0, 0), (1, 0), (8, 0), (10, 0), (11, 0), (2, 0), (3, 0), (4, 0), (5, 0), (0, 1), (1, 1), (6, 0), (10, 1), (11, 1), (0, 2), (1, 2), (0, 3), (1, 3), (7, 0), (2, 1), (3, 1), (4, 1), (9, 0), (5, 1), (3, 2), (12, 0), (6, 1), (4, 2), (8, 1), (5, 2), (2, 2), (6, 2), (3, 3), (4, 3), (5, 3), (7, 1), (9, 1), (10, 2), (12, 1), (2, 3), (8, 2), (6, 3), (11, 2), (9, 2), (12, 2), (7, 2), (8, 3), (9, 3), (10, 3), (12, 3), (7, 3), (11, 3)]
+PLAN_B = ([(3, 0, 1024, (2, 3, 1, 4)), (0, 0, 1664, (1, 3, 4, 2)), (0, 1664, 3352, (2, 1, 3, 4)), (4, 0, 1408, (2, 1, 3, 4)), (1, 0, 512, (2, 3, 1, 4)), (5, 512, 1024, (1, 3, 2, 4)), (2, 0, 768, (3, 2, 1, 4)), (4, 2688, 4096, (2, 1, 3, 4)), (4, 1408, 2688, (1, 3, 2, 4)), (5, 0, 512, (2, 1, 3, 4)), (1, 512, 1024, (2, 1, 3, 4))], [(0, -1), (1, -1), (2, -1), (3, -1), (4, -1), (5, -1), (6, -1), (7, -1), (8, -1), (9, -1), (10, -1), (-1, 0), (0, 0), (-2, 0), (-3, 0), (-3, 0), (-3, 0), (-3, 0), (-3, 0), (-3, 0), (-3, 0), (-3, 0), (6, 0), (1, 0), (0, 1), (-3, 0), (2, 0), (-3, 0), (-2, 1), (-3, 0), (-2, 2), (5, 0), (-3, 0), (-3, 0), (1, 1), (-3, 0), (-3, 0), (3, 0), (-3, 0), (-3, 0), (5, 1), (-3, 0), (-3, 0), (-3, 0), (8, 0), (-3, 0), (-1, 1), (-3, 0), (-3, 0), (0, 2), (4, 0), (-3, 0), (-3, 0), (-3, 0), (-3, 0), (-3, 0), (-3, 0), (-3, 0), (1, 2), (2, 1), (8, 1), (0, 3), (7, 0), (4, 1), (3, 1), (2, 2), (3, 2), (9, 0), (7, 1), (4, 2), (2, 3), (3, 3), (10, 0), (9, 1), (7, 2), (6, 1), (4, 3), (9, 2), (10, 1), (6, 2), (-2, 3), (7, 3), (5, 2), (-1, 2), (9, 3), (10, 2), (1, 3), (6, 3), (-2, 4), (8, 2), (-1, 3), (5, 3), (10, 3), (8, 3), (-1, 4)], (4, 3, 0, 2, 1))
+PLAN_C = ([(0, 0, 896, (1, 2, 3, 4)), (3, 0, 512, (2, 3, 1, 4)), (0, 1664, 2560, (1, 2, 3, 4)), (1, 512, 1024, (2, 3, 4, 1)), (1, 0, 512, (1, 2, 3, 4)), (0, 2560, 3352, (1, 2, 3, 4)), (0, 896, 1664, (2, 3, 1, 4)), (2, 0, 384, (1, 2, 3, 4)), (2, 384, 768, (3, 1, 2, 4)), (3, 512, 1024, (1, 2, 3, 4))], [(0, -1), (1, -1), (2, -1), (3, -1), (4, -1), (5, -1), (6, -1), (7, -1), (8, -1), (9, -1), (-1, 0), (1, 0), (0, 0), (-2, 0), (3, 0), (-2, 1), (8, 0), (1, 1), (2, 0), (3, 1), (6, 0), (0, 1), (-2, 2), (4, 0), (2, 1), (3, 2), (6, 1), (4, 1), (0, 2), (5, 0), (2, 2), (7, 0), (4, 2), (9, 0), (0, 3), (5, 1), (-1, 1), (7, 1), (8, 1), (2, 3), (1, 2), (9, 1), (4, 3), (-1, 2), (5, 2), (8, 2), (7, 2), (9, 2), (1, 3), (-2, 3), (-1, 3), (3, 3), (6, 2), (5, 3), (8, 3), (7, 3), (9, 3), (-1, 4), (-2, 4), (6, 3)], (4, 0, 3, 1, 2))
 PLAN_A = ([(1, 0, 256, (2, 1, 3, 4)), (1, 768, 1024, (3, 4, 1, 2)), (0, 0, 1024, (1, 2, 3, 4)), (0, 2048, 3072, (2, 3, 4, 1)), (0, 3072, 4096, (3, 4, 1, 2)), (0, 1024, 2048, (1, 2, 3, 4)), (1, 256, 512, (1, 2, 3, 4)), (1, 512, 768, (2, 1, 3, 4))], [(0, -1), (1, -1), (2, -1), (3, -1), (4, -1), (5, -1), (6, -1), (7, -1), (-3, 0), (0, 0), (1, 0), (-3, 0), (-3, 0), (-3, 0), (-3, 0), (-3, 0), (-3, 0), (-3, 0), (2, 0), (-3, 0), (1, 1), (3, 0), (4, 0), (-3, 0), (-3, 0), (7, 0), (-3, 0), (5, 0), (3, 1), (-3, 0), (2, 1), (-3, 0), (6, 0), (-3, 0), (-3, 0), (0, 1), (4, 1), (-3, 0), (5, 1), (1, 2), (-3, 0), (-3, 0), (7, 1), (6, 1), (2, 2), (-3, 0), (0, 2), (3, 2), (-3, 0), (1, 3), (-3, 0), (4, 2), (-3, 0), (-3, 0), (5, 2), (-3, 0), (-3, 0), (7, 2), (-3, 0), (-3, 0), (3, 3), (-3, 0), (6, 2), (2, 3), (-3, 0), (4, 3), (0, 3), (5, 3), (7, 3), (6, 3)], (1, 2, 3, 4, 0))
-PLAN_B = ([(1, 512, 1024, (1, 2, 3, 4)), (4, 2688, 4096, (2, 1, 3, 4)), (0, 0, 1664, (3, 4, 2, 1)), (2, 0, 768, (3, 4, 2, 1)), (3, 0, 1024, (2, 1, 3, 4)), (4, 1408, 2688, (1, 3, 4, 2)), (0, 1664, 3352, (2, 1, 3, 4)), (4, 0, 1408, (1, 2, 3, 4)), (5, 512, 1024, (1, 3, 4, 2)), (5, 0, 512, (2, 1, 3, 4)), (1, 0, 512, (2, 1, 3, 4))], [(0, -1), (1, -1), (2, -1), (3, -1), (4, -1), (5, -1), (6, -1), (7, -1), (8, -1), (9, -1), (10, -1), (-1, 0), (0, 0), (-2, 0), (-3, 0), (-2, 1), (-3, 0), (-3, 0), (-3, 0), (-3, 0), (1, 0), (-3, 0), (-3, 0), (-3, 0), (-3, 0), (5, 0), (4, 0), (2, 0), (-3, 0), (-3, 0), (-3, 0), (3, 0), (-3, 0), (-3, 0), (-3, 0), (-3, 0), (7, 0), (5, 1), (-3, 0), (-3, 0), (-3, 0), (6, 0), (-3, 0), (-3, 0), (-3, 0), (-3, 0), (-3, 0), (-3, 0), (-3, 0), (-3, 0), (-3, 0), (2, 1), (-3, 0), (-3, 0), (8, 0), (-1, 1), (9, 0), (3, 1), (1, 1), (4, 1), (8, 1), (10, 0), (5, 2), (0, 1), (1, 2), (4, 2), (6, 1), (-2, 2), (8, 2), (0, 2), (1, 3), (9, 1), (4, 3), (0, 3), (7, 1), (6, 2), (10, 1), (9, 2), (2, 2), (-1, 2), (-2, 3), (3, 2), (7, 2), (6, 3), (5, 3), (2, 3), (8, 3), (3, 3), (9, 3), (10, 2), (-1, 3), (7, 3), (10, 3), (-2, 4), (-1, 4)], (4, 0, 2, 1, 3))
-PLAN_C = ([(3, 512, 1024, (2, 1, 3, 4)), (1, 0, 512, (1, 2, 3, 4)), (0, 2560, 3352, (3, 4, 1, 2)), (2, 384, 768, (2, 3, 4, 1)), (0, 0, 896, (2, 1, 3, 4)), (0, 896, 1664, (3, 4, 2, 1)), (0, 1664, 2560, (2, 1, 3, 4)), (1, 512, 1024, (1, 2, 3, 4)), (2, 0, 384, (1, 2, 3, 4)), (3, 0, 512, (1, 2, 3, 4))], [(0, -1), (1, -1), (2, -1), (3, -1), (4, -1), (5, -1), (6, -1), (7, -1), (8, -1), (9, -1), (-1, 0), (0, 0), (3, 0), (1, 0), (-2, 0), (-2, 1), (2, 0), (4, 0), (7, 0), (5, 0), (8, 0), (3, 1), (9, 0), (-1, 1), (6, 0), (2, 1), (0, 1), (1, 1), (4, 1), (0, 2), (5, 1), (1, 2), (-2, 2), (6, 1), (3, 2), (4, 2), (0, 3), (2, 2), (7, 1), (1, 3), (8, 1), (6, 2), (9, 1), (-1, 2), (4, 3), (-2, 3), (3, 3), (7, 2), (5, 2), (8, 2), (2, 3), (9, 2), (6, 3), (-1, 3), (5, 3), (7, 3), (8, 3), (9, 3), (-2, 4), (-1, 4)], (4, 0, 2, 1, 3))
 
 SMALL_ROWS = 16
 LATE_ARRAY = 4
@@ -97,11 +97,13 @@
     return raw, step, -jnp.exp(heads_ref[0:1, :HEADS])
 
 
-def mixer_setup(inner_ref, taps_ref, heads_ref, position, inside, x_ref, qcol, qrow, dtpair):
+def mixer_setup(
+    inner_ref, taps_ref, heads_ref, position, inside, x_ref, qcol, qrow, dtpair, unroll=1
+):
     rows = inner_ref.shape[0]
     for start, end in spans(CONVCH // LANES, 2):
 
-        @pl.loop(start, end)
+        @pl.loop(start, end, unroll=unroll)
         def _(k):
             at = pl.multiple_of(k * LANES, LANES)
             before = conv_before(
@@ -137,7 +139,9 @@
     position = position_ref[...]
     inside = inside_ref[...]
     run_steps(
-        mixer_setup(inner_ref, taps_ref, heads_ref, position, inside, x_ref, qcol, qrow, dtpair)
+        mixer_setup(
+            inner_ref, taps_ref, heads_ref, position, inside, x_ref, qcol, qrow, dtpair, unroll=7
+        )
     )
     b_all = x_ref[:, INNER : INNER + STATE]
     c_all = x_ref[:, INNER + STATE :]
@@ -152,19 +156,23 @@
         columns = qcol[p]
         for k in (0, 1):
             h = 2 * p + k
-            gaps = columns[:, k * HDIM : k * HDIM + 1] - qrow[pl.ds(h, 1), :]
-            prod = jnp.exp(jnp.minimum(gaps, 0.0)) * aff_ref[...]
-            outs.append(dot(prod.astype(BF16), scaled))
+            column, row = columns[:, k * HDIM : k * HDIM + 1], qrow[pl.ds(h, 1), :]
+            halves = []
+            for low, high in ((0, rows // 2), (rows // 2, rows)):
+                gaps = column[low:high] - row[:, :high]
+                prod = jnp.exp(jnp.minimum(gaps, 0.0)) * aff_ref[low:high, :high]
+                halves.append(dot(prod.astype(BF16), scaled[:high]))
+            outs.append(jnp.concatenate(halves, axis=0))
         y = jnp.where(first, outs[0], outs[1]) + x * skip_ref[:, pl.ds(at, LANES)]
         y_ref[:, pl.ds(at, LANES)] = y
         z = inner_ref[:, pl.ds(at, LANES)]
         w = y * (z * sigmoid(z))
         return total + jnp.sum(w * w, axis=1, keepdims=True)
 
-    total = lax.fori_loop(0, PAIRS_OF_HEADS, pair, jnp.zeros((rows, 1), F32))
+    total = lax.fori_loop(0, PAIRS_OF_HEADS, pair, jnp.zeros((rows, 1), F32), unroll=2)
     scale = lax.rsqrt(total / INNER + EPSILON)
 
-    @pl.loop(0, PAIRS_OF_HEADS)
+    @pl.loop(0, PAIRS_OF_HEADS, unroll=2)
     def _(p):
         at = pl.multiple_of(p * LANES, LANES)
         z = inner_ref[:, pl.ds(at, LANES)]

time: 675 us -> 660 us (0.978)
  Pallas kernels: 507 us -> 493 us
    pallas_call x2, Pallas kernels: 30.9 us -> 23.2 us  [mixer_forward(): pl.pallas_call(mixer_forward_kernel, out_shape=[shape((rows, INNER), BF16...]
    pallas_call x3, Pallas kernels: 280 us -> 273 us  [scatter(): pl.pallas_call(functools.partial(scatter_kernel, devices, plan, jobs, arr...]
  transfers between devices with their start and end apart: 3 -> 3, of which waited for: 1 -> 1; matrix products, arithmetic and copies ran while one was open for 7% -> 7% of each run, Pallas kernels for 6% -> 5%
where the time goes in v5:
time: 660 us; the launch traced here: 655 us
  Pallas kernels  493 us (75%)
  matrix products  78.8 us (12%)
  local copies, waits for them, and re-layouts  26.8 us (4%)
  other arithmetic  26.6 us (4%)
  between operations  16.1 us (2%)
  waiting for transfers between devices  8.18 us (1%)
    pallas_call x3, Pallas kernels, scatter(): pl.pallas_call(functools.partial(scatter_kernel, devices, plan, jobs, arr...  273 us
    pallas_call x1, Pallas kernels, gather_all(): pl.pallas_call(functools.partial(gather_kernel, devices, AG_CHUNKS, AG_EV...  187 us
    dot_general x14, matrix products, dot(): return jnp.dot(left, right, preferred_element_type=F32)  35.2 us
    dot_general x12, matrix products, dot_rt(): lax.dot_general(left, right, (((1,), (1,)), ((), ())), preferred_element_...  31.1 us
    pallas_call x2, Pallas kernels, mixer_forward(): pl.pallas_call(mixer_forward_kernel, out_shape=[shape((rows, INNER), BF16...  23.2 us
  transfers between devices with their start and end apart: 3, of which 1 were waited for; matrix products, arithmetic and copies ran while one was open for 7% of the time, Pallas kernels for 5%

profile of v5, /device:TPU:0, one launch (start us, length us, event | category | flops | bytes accessed | tf_op | source)
XLA Modules:
  0.0 655.5 jit_solution(11788826086156929460)
XLA Ops:
  10.2 186.8 %gather_all.1 = (bf16[2,2,2,2,2,32,3352]{6,5,4,3,2,1,0:T(8,128)(2,1)}, bf16[2,2,2,2,2,48,1024]{6,5,4,3,2,1,0:T(8,128)(2,1)}, bf16[2,2,2,2,2,32,768]{6,5,4,3,2,1,...) custom-call(bf16[2,32,3352]{2,1,0:T(8,128)(2,1)} %refs_0_.1, ...), custom_call_target="tpu_custom_call" | custom-call | tf_op jit(solution)/shard_map/gather_all/pallas_call | solution.py:587
  199.0 1.7 slice_add_fusion
  202.1 2.6 all-to-all-start
  217.8 8.2 %all-to-all-done = bf16[32,8,1024]{2,1,0:T(8,128)(2,1)S(1)} async-done(((bf16[32,8,1024]{2,1,0:T(8,128)(2,1)}), bf16[32,8,1024]{2,1,0:T(8,128)(2,1)S(1)}, u32[]{:S(2)}, u32[]{:S(2)}) %all-to-all-start) | async-done | bytes 524320 | tf_op jit(solution)/shard_map/all_to_all | solution.py:966
  225.9 3.8 all-to-all-start.1
  231.8 4.7 attention_forward.2
  236.5 7.0 %fusion.62.inner_ref.refs_12_ = f32[256,3352]{1,0:T(8,128)} fusion(bf16[1024,3352]{1,0:T(8,128)(2,1)} %bitcast.179, f32[256,1024]{1,0:T(8,128)S(1)} %get-tuple-element.163, f32[1024]{0:T(1024)S(1)} %mul.344, f32[256]{0:T(256)S(1)} %add_rsqrt_fusion.3), kind=kOutput, calls=%fused_computation.197 | convolution fusion | flops 1758199808 | bytes 11351040 | tf_op jit(solution)/shard_map/dot_general | solution.py:40
  243.5 11.4 %mixer_forward.2 = (bf16[256,1536]{1,0:T(8,128)(2,1)}, bf16[1536,256]{1,0:T(8,128)(2,1)}, f32[256,1536]{1,0:T(8,128)}) custom-call(f32[256,3352]{1,0:T(8,128)} %fusion.62.inner_ref.refs_12_, f32[4,1792]{1,0:T(4,128)} %reshape.396.taps_ref.refs_13_, f32[8,128]{1,0:T(8,128)} %select_maximum_fusion.2.heads_ref.refs_14_, ...), custom_call_target="tpu_custom_call" | custom-call | tf_op jit(solution)/shard_map/mixer_forward/pallas_call | solution.py:198
  255.0 2.2 convolution_add_fusion.5
  257.8 6.2 fusion.53
  266.6 1.6 fusion.65.packed_ref.refs_13_
  268.9 3.9 fusion.64.inner_ref.refs_4_
  272.9 4.7 attention_forward.3
  281.0 11.8 %mixer_forward.3 = (bf16[256,1536]{1,0:T(8,128)(2,1)}, bf16[1536,256]{1,0:T(8,128)(2,1)}, f32[256,1536]{1,0:T(8,128)}) custom-call(f32[256,3352]{1,0:T(8,128)} %fusion.64.inner_ref.refs_4_, f32[4,1792]{1,0:T(4,128)} %reshape.398.taps_ref.refs_5_, f32[8,128]{1,0:T(8,128)} %select_maximum_fusion.heads_ref.refs_6_, ...), custom_call_target="tpu_custom_call" | custom-call | tf_op jit(solution)/shard_map/mixer_forward/pallas_call | solution.py:198
  292.8 2.2 convolution_add_fusion.4
  295.6 2.5 fusion.61
  298.1 5.9 fusion.2
  304.1 3.0 multiply_convert_fusion.3
  307.1 3.1 multiply_reduce_fusion.4
  313.0 2.2 fusion.66.refs_12_
  319.0 68.9 %scatter.3 = (f32[32,4096]{1,0:T(8,128)}, f32[64,1024]{1,0:T(8,128)}, bf16[256,3352]{1,0:T(8,128)(2,1)}, f32[4,1792]{1,0:T(4,128)}, f32[1,1536]{1,0:T(1,128)}, /...) custom-call(bf16[16,2,32,256]{3,2,1,0:T(8,128)(2,1)} %bitcast.197, ...), custom_call_target="tpu_custom_call" | custom-call | tf_op jit(solution)/shard_map/scatter/pallas_call | solution.py:828
  387.9 5.8 fusion.67
  396.3 1.7 copy-done.5
  398.0 2.0 multiply_convert_fusion.1
  400.6 3.1 multiply_reduce_fusion.1
  406.5 2.2 fusion.68.refs_20_
  408.7 4.4 convolution_convert_fusion.2
  413.1 3.1 pad_maximum_fusion.1.refs_8_
  419.0 129.2 %scatter.4 = (f32[32,3352]{1,0:T(8,128)}, f32[48,1024]{1,0:T(8,128)}, f32[32,768]{1,0:T(8,128)}, f32[16,1024]{1,0:T(8,128)}, f32[32,4096]{1,0:T(8,128)}, /*index...) custom-call(bf16[16,2,32,256]{3,2,1,0:T(8,128)(2,1)} %bitcast.195, ...), custom_call_target="tpu_custom_call" | custom-call | tf_op jit(solution)/shard_map/scatter/pallas_call | solution.py:828
  548.2 5.8 fusion.69
  558.1 75.1 %scatter.5 = (f32[32,3352]{1,0:T(8,128)}, f32[48,1024]{1,0:T(8,128)}, f32[32,768]{1,0:T(8,128)}, f32[16,1024]{1,0:T(8,128)}, f32[88,128]{1,0:T(8,128)}, /*index=5*/bf16[2,2,2,2,2,8,1024]{6,5,4,3,2,1,0:T(8,128)(2,1)}) custom-call(bf16[16,2,32,256]{3,2,1,0:T(8,128)(2,1)} %bitcast.198, bf16[16,2,48,256]{3,2,1,0:T(8,128)(2,1)} %bitcast.202, ...), custom_call_target="tpu_custom_call" | custom-call | tf_op jit(solution)/shard_map/scatter/pallas_call | solution.py:828
  637.9 2.4 fusion.18
  (311 shorter events, 60.3 us)
Async XLA Ops:
  7.2 193.5 %copy-start.55 = (s32[8192]{0:T(1024)S(1)}, s32[8192]{0:T(1024)}, u32[]{:S(2)}) copy-start(s32[8192]{0:T(1024)} %param.18) | copy-start | bytes 98308
  7.2 193.8 %copy-start.34 = (bf16[256,1024]{1,0:T(8,128)(2,1)S(1)}, bf16[256,1024]{1,0:T(8,128)(2,1)}, u32[]{:S(2)}) copy-start(bf16[256,1024]{1,0:T(8,128)(2,1)} %param.16) | copy-start | bytes 1572868
  7.2 290.9 %all-gather.3.cloned.1.call-start = ((), (), s32[]{:S(2)}) async-start(), calls=%async_computation.2 | async-start | bytes 8650752 | tf_op jit(solution)/shard_map/all_gather | solution.py:1002
  196.9 7.8 %copy-start.54 = (bf16[2,2,2,2,2,16,128]{6,5,4,3,2,1,0:T(8,128)(2,1)S(1)}, bf16[2,2,2,2,2,16,128]{6,5,4,3,2,1,0:T(8,128)(2,1)}, u32[]{:S(2)}) copy-start(bf16[2,2,2,2,2,16,128]{6,5,4,3,2,1,0:T(8,128)(2,1)} %get-tuple-element.65) | copy-start | bytes 393220
  197.0 7.9 %copy-start.53 = (bf16[2,2,2,2,2,16,128]{6,5,4,3,2,1,0:T(8,128)(2,1)S(1)}, bf16[2,2,2,2,2,16,128]{6,5,4,3,2,1,0:T(8,128)(2,1)}, u32[]{:S(2)}) copy-start(bf16[2,2,2,2,2,16,128]{6,5,4,3,2,1,0:T(8,128)(2,1)} %get-tuple-element.74) | copy-start | bytes 393220
  197.0 8.1 %copy-start.82 = (s32[1,4]{1,0:T(1,128)S(1)}, s32[1,4]{1,0:T(1,128)}, u32[]{:S(2)}) copy-start(s32[1,4]{1,0:T(1,128)} %param.19) | copy-start | bytes 52
  197.0 8.3 %copy-start.81 = (f32[2,24]{1,0:T(2,128)S(1)}, f32[2,24]{1,0:T(2,128)}, u32[]{:S(2)}) copy-start(f32[2,24]{1,0:T(2,128)} %param.31) | copy-start | bytes 580
  197.0 8.3 %copy-start.79 = (f32[2,24]{1,0:T(2,128)S(1)}, f32[2,24]{1,0:T(2,128)}, u32[]{:S(2)}) copy-start(f32[2,24]{1,0:T(2,128)} %param.30) | copy-start | bytes 580
  197.0 8.3 %copy-start.80 = (f32[2,24]{1,0:T(2,128)S(1)}, f32[2,24]{1,0:T(2,128)}, u32[]{:S(2)}) copy-start(f32[2,24]{1,0:T(2,128)} %param.29) | copy-start | bytes 580
  197.0 9.3 %copy-start.35 = (bf16[256,1024]{1,0:T(8,128)(2,1)S(1)}, bf16[256,1024]{1,0:T(8,128)(2,1)}, u32[]{:S(2)}) copy-start(bf16[256,1024]{1,0:T(8,128)(2,1)} %param.17) | copy-start | bytes 1572868
  201.0 6.7 %copy-start.66 = (s32[1,256]{1,0:T(1,128)}, s32[1,256]{1,0:T(1,128)S(1)}, u32[]{:S(2)}) copy-start(s32[1,256]{1,0:T(1,128)S(1)} %multiply_add_fusion.3) | copy-start | bytes 3076
  202.1 23.8 %all-to-all-start = ((bf16[32,8,1024]{2,1,0:T(8,128)(2,1)}), bf16[32,8,1024]{2,1,0:T(8,128)(2,1)S(1)}, u32[]{:S(2)}, u32[]{:S(2)}) async-start(bf16[32,8,1024]{2,1,0:T(8,128)(2,1)} %fusion.7), calls=%async_computation | async-start | bytes 1048576 | tf_op jit(solution)/shard_map/all_to_all | solution.py:966
  209.3 63.5 %copy-start.41 = (f32[1024]{0:T(1024)}, f32[1024]{0:T(1024)S(1)}, u32[]{:S(2)}) copy-start(f32[1024]{0:T(1024)S(1)} %mul.344) | copy-start | bytes 12292
  210.1 20.1 %copy-start.16 = (bf16[2,2,2,2,2,32,768]{6,5,4,3,2,1,0:T(8,128)(2,1)S(1)}, bf16[2,2,2,2,2,32,768]{6,5,4,3,2,1,0:T(8,128)(2,1)}, u32[]{:S(2)}) copy-start(bf16[2,2,2,2,2,32,768]{6,5,4,3,2,1,0:T(8,128)(2,1)} %get-tuple-element.69) | copy-start | bytes 4718596
  211.7 46.1 %copy-start.51 = (f32[1024]{0:T(1024)}, f32[1024]{0:T(1024)S(1)}, u32[]{:S(2)}) copy-start(f32[1024]{0:T(1024)S(1)} %mul.356) | copy-start | bytes 12292
  211.8 57.1 %copy-start.43 = (f32[1024]{0:T(1024)}, f32[1024]{0:T(1024)S(1)}, u32[]{:S(2)}) copy-start(f32[1024]{0:T(1024)S(1)} %mul.365) | copy-start | bytes 12292
  217.8 77.8 %copy-start.68 = (s32[256]{0:T(256)}, s32[256]{0:T(256)S(1)}, u32[]{:S(2)}) copy-start(s32[256]{0:T(256)S(1)} %select_reduce_fusion) | copy-start | bytes 3076
  225.9 69.6 %all-to-all-start.1 = ((bf16[32,8,1024]{2,1,0:T(8,128)(2,1)}), bf16[32,8,1024]{2,1,0:T(8,128)(2,1)}, u32[]{:S(2)}, u32[]{:S(2)}) async-start(bf16[32,8,1024]{2,1,0:T(8,128)(2,1)} %fusion.8), calls=%async_computation.1 | async-start | bytes 1048576 | tf_op jit(solution)/shard_map/all_to_all | solution.py:966
  230.2 42.6 %copy-start = (f32[256,1024]{1,0:T(8,128)}, f32[256,1024]{1,0:T(8,128)S(1)}, u32[]{:S(2)}) copy-start(f32[256,1024]{1,0:T(8,128)S(1)} %get-tuple-element.163) | copy-start | bytes 3145732
  230.2 42.6 %copy-start.60 = (f32[256]{0:T(256)}, f32[256]{0:T(256)S(1)}, u32[]{:S(2)}) copy-start(f32[256]{0:T(256)S(1)} %add_rsqrt_fusion.3) | copy-start | bytes 3076
  243.5 11.4 %copy-start.6 = (bf16[2,2,2,2,2,48,1024]{6,5,4,3,2,1,0:T(8,128)(2,1)S(1)}, bf16[2,2,2,2,2,48,1024]{6,5,4,3,2,1,0:T(8,128)(2,1)}, u32[]{:S(2)}) copy-start(bf16[2,2,2,2,2,48,1024]{6,5,4,3,2,1,0:T(8,128)(2,1)} %get-tuple-element.68) | copy-start | bytes 9437188
  257.8 11.1 %slice-start.4 = ((s8[7077888]{0:T(1024)(128)(4,1)}), s8[4194304]{0:T(1024)(128)(4,1)S(1)}, s32[]{:S(2)}) async-start(s8[7077888]{0:T(1024)(128)(4,1)} %bitcast.182), calls=%async_computation.7 | async-start | bytes 8388608
  265.5 27.3 %copy-start.2 = (f32[256,1024]{1,0:T(8,128)}, f32[256,1024]{1,0:T(8,128)S(1)}, u32[]{:S(2)}) copy-start(f32[256,1024]{1,0:T(8,128)S(1)} %get-tuple-element.167) | copy-start | bytes 3145732
  281.0 11.8 %copy-start.8 = (bf16[2,2,2,2,2,48,1024]{6,5,4,3,2,1,0:T(8,128)(2,1)S(1)}, bf16[2,2,2,2,2,48,1024]{6,5,4,3,2,1,0:T(8,128)(2,1)}, u32[]{:S(2)}) copy-start(bf16[2,2,2,2,2,48,1024]{6,5,4,3,2,1,0:T(8,128)(2,1)} %get-tuple-element.80) | copy-start | bytes 9437188
  295.5 14.7 %copy-start.12 = (f32[256,1024]{1,0:T(8,128)}, f32[256,1024]{1,0:T(8,128)S(1)}, u32[]{:S(2)}) copy-start(f32[256,1024]{1,0:T(8,128)S(1)} %get-tuple-element.171) | copy-start | bytes 3145732
  298.1 9.0 %slice-start.2 = ((s8[8388608]{0:T(1024)(128)(4,1)}), s8[4194304]{0:T(1024)(128)(4,1)S(1)}, s32[]{:S(2)}) async-start(s8[8388608]{0:T(1024)(128)(4,1)} %bitcast.173), calls=%async_computation.5 | async-start | bytes 8388608
  633.2 7.1 %copy-start.36 = (bf16[2,2,2,2,2,8,1024]{6,5,4,3,2,1,0:T(8,128)(2,1)S(1)}, bf16[2,2,2,2,2,8,1024]{6,5,4,3,2,1,0:T(8,128)(2,1)}, u32[]{:S(2)}) copy-start(bf16[2,2,2,2,2,8,1024]{6,5,4,3,2,1,0:T(8,128)(2,1)} %get-tuple-element.92) | copy-start | bytes 1572868
  633.2 7.1 %copy-start.67 = (s32[1,256]{1,0:T(1,128)S(1)}, s32[1,256]{1,0:T(1,128)}, u32[]{:S(2)}) copy-start(s32[1,256]{1,0:T(1,128)} %copy-done.66) | copy-start | bytes 3076
  633.2 8.2 %copy-start.47 = (f32[64,1024]{1,0:T(8,128)S(1)}, f32[64,1024]{1,0:T(8,128)}, u32[]{:S(2)}) copy-start(f32[64,1024]{1,0:T(8,128)} %get-tuple-element.115) | copy-start | bytes 786436
  633.2 8.2 %copy-start.48 = (f32[64,1024]{1,0:T(8,128)S(1)}, f32[64,1024]{1,0:T(8,128)}, u32[]{:S(2)}) copy-start(f32[64,1024]{1,0:T(8,128)} %get-tuple-element.114) | copy-start | bytes 786436
  635.4 6.9 %copy-start.37 = (f32[32,4096]{1,0:T(8,128)S(1)}, f32[32,4096]{1,0:T(8,128)}, u32[]{:S(2)}) copy-start(f32[32,4096]{1,0:T(8,128)} %get-tuple-element.113) | copy-start | bytes 1572868
  635.4 6.9 %copy-start.38 = (f32[32,4096]{1,0:T(8,128)S(1)}, f32[32,4096]{1,0:T(8,128)}, u32[]{:S(2)}) copy-start(f32[32,4096]{1,0:T(8,128)} %get-tuple-element.112) | copy-start | bytes 1572868
  (63 other events, 223.6 us)
Sparse Core Ops, SparseCore 0:
  200.8 85.7 all-gather.2

commit v6 on v5

--- a/solution.py
+++ b/solution.py
@@ -27,7 +27,8 @@
 MESH = pl.DeviceIdType.MESH
 
 AG_CHUNKS = [(0, 6, (4, 3, 2, 1)), (1, 6, (4, 3, 2, 1)), (1, 0, (4, 3, 1, 2)), (1, 3, (4, 3, 2, 1)), (1, 2, (4, 3, 2, 1)), (0, 2, (4, 3, 2, 1)), (1, 5, (4, 3, 2, 1)), (0, 0, (4, 3, 1, 2)), (0, 3, (1, 4, 3, 2)), (0, 5, (4, 3, 2, 1)), (0, 4, (1, 2, 4, 3)), (0, 1, (1, 2, 4, 3)), (1, 1, (4, 3, 2, 1))]
-AG_EVENTS = [(0, 0), (1, 0), (8, 0), (10, 0), (11, 0), (2, 0), (3, 0), (4, 0), (5, 0), (0, 1), (1, 1), (6, 0), (10, 1), (11, 1), (0, 2), (1, 2), (0, 3), (1, 3), (7, 0), (2, 1), (3, 1), (4, 1), (9, 0), (5, 1), (3, 2), (12, 0), (6, 1), (4, 2), (8, 1), (5, 2), (2, 2), (6, 2), (3, 3), (4, 3), (5, 3), (7, 1), (9, 1), (10, 2), (12, 1), (2, 3), (8, 2), (6, 3), (11, 2), (9, 2), (12, 2), (7, 2), (8, 3), (9, 3), (10, 3), (12, 3), (7, 3), (11, 3)]
+AG_EVENTS = [(0, 0), (1, 0), (8, 0), (-2, 0), (10, 0), (11, 0), (2, 0), (3, 0), (4, 0), (-2, 1), (5, 0), (6, 0), (10, 1), (0, 1), (1, 1), (11, 1), (7, 0), (-2, 2), (0, 2), (1, 2), (0, 3), (2, 1), (1, 3), (9, 0), (3, 1), (4, 1), (12, 0), (5, 1), (8, 1), (3, 2), (6, 1), (4, 2), (5, 2), (2, 2), (6, 2), (3, 3), (4, 3), (5, 3), (7, 1), (10, 2), (9, 1), (2, 3), (6, 3), (12, 1), (11, 2), (8, 2), (9, 2), (-2, 3), (-2, 4), (7, 2), (12, 2), (8, 3), (9, 3), (10, 3), (12, 3), (7, 3), (11, 3)]
+AG_ROW_BITS = (3, 1, 2, 4, 0)
 PLAN_B = ([(3, 0, 1024, (2, 3, 1, 4)), (0, 0, 1664, (1, 3, 4, 2)), (0, 1664, 3352, (2, 1, 3, 4)), (4, 0, 1408, (2, 1, 3, 4)), (1, 0, 512, (2, 3, 1, 4)), (5, 512, 1024, (1, 3, 2, 4)), (2, 0, 768, (3, 2, 1, 4)), (4, 2688, 4096, (2, 1, 3, 4)), (4, 1408, 2688, (1, 3, 2, 4)), (5, 0, 512, (2, 1, 3, 4)), (1, 512, 1024, (2, 1, 3, 4))], [(0, -1), (1, -1), (2, -1), (3, -1), (4, -1), (5, -1), (6, -1), (7, -1), (8, -1), (9, -1), (10, -1), (-1, 0), (0, 0), (-2, 0), (-3, 0), (-3, 0), (-3, 0), (-3, 0), (-3, 0), (-3, 0), (-3, 0), (-3, 0), (6, 0), (1, 0), (0, 1), (-3, 0), (2, 0), (-3, 0), (-2, 1), (-3, 0), (-2, 2), (5, 0), (-3, 0), (-3, 0), (1, 1), (-3, 0), (-3, 0), (3, 0), (-3, 0), (-3, 0), (5, 1), (-3, 0), (-3, 0), (-3, 0), (8, 0), (-3, 0), (-1, 1), (-3, 0), (-3, 0), (0, 2), (4, 0), (-3, 0), (-3, 0), (-3, 0), (-3, 0), (-3, 0), (-3, 0), (-3, 0), (1, 2), (2, 1), (8, 1), (0, 3), (7, 0), (4, 1), (3, 1), (2, 2), (3, 2), (9, 0), (7, 1), (4, 2), (2, 3), (3, 3), (10, 0), (9, 1), (7, 2), (6, 1), (4, 3), (9, 2), (10, 1), (6, 2), (-2, 3), (7, 3), (5, 2), (-1, 2), (9, 3), (10, 2), (1, 3), (6, 3), (-2, 4), (8, 2), (-1, 3), (5, 3), (10, 3), (8, 3), (-1, 4)], (4, 3, 0, 2, 1))
 PLAN_C = ([(0, 0, 896, (1, 2, 3, 4)), (3, 0, 512, (2, 3, 1, 4)), (0, 1664, 2560, (1, 2, 3, 4)), (1, 512, 1024, (2, 3, 4, 1)), (1, 0, 512, (1, 2, 3, 4)), (0, 2560, 3352, (1, 2, 3, 4)), (0, 896, 1664, (2, 3, 1, 4)), (2, 0, 384, (1, 2, 3, 4)), (2, 384, 768, (3, 1, 2, 4)), (3, 512, 1024, (1, 2, 3, 4))], [(0, -1), (1, -1), (2, -1), (3, -1), (4, -1), (5, -1), (6, -1), (7, -1), (8, -1), (9, -1), (-1, 0), (1, 0), (0, 0), (-2, 0), (3, 0), (-2, 1), (8, 0), (1, 1), (2, 0), (3, 1), (6, 0), (0, 1), (-2, 2), (4, 0), (2, 1), (3, 2), (6, 1), (4, 1), (0, 2), (5, 0), (2, 2), (7, 0), (4, 2), (9, 0), (0, 3), (5, 1), (-1, 1), (7, 1), (8, 1), (2, 3), (1, 2), (9, 1), (4, 3), (-1, 2), (5, 2), (8, 2), (7, 2), (9, 2), (1, 3), (-2, 3), (-1, 3), (3, 3), (6, 2), (5, 3), (8, 3), (7, 3), (9, 3), (-1, 4), (-2, 4), (6, 3)], (4, 0, 3, 1, 2))
 PLAN_A = ([(1, 0, 256, (2, 1, 3, 4)), (1, 768, 1024, (3, 4, 1, 2)), (0, 0, 1024, (1, 2, 3, 4)), (0, 2048, 3072, (2, 3, 4, 1)), (0, 3072, 4096, (3, 4, 1, 2)), (0, 1024, 2048, (1, 2, 3, 4)), (1, 256, 512, (1, 2, 3, 4)), (1, 512, 768, (2, 1, 3, 4))], [(0, -1), (1, -1), (2, -1), (3, -1), (4, -1), (5, -1), (6, -1), (7, -1), (-3, 0), (0, 0), (1, 0), (-3, 0), (-3, 0), (-3, 0), (-3, 0), (-3, 0), (-3, 0), (-3, 0), (2, 0), (-3, 0), (1, 1), (3, 0), (4, 0), (-3, 0), (-3, 0), (7, 0), (-3, 0), (5, 0), (3, 1), (-3, 0), (2, 1), (-3, 0), (6, 0), (-3, 0), (-3, 0), (0, 1), (4, 1), (-3, 0), (5, 1), (1, 2), (-3, 0), (-3, 0), (7, 1), (6, 1), (2, 2), (-3, 0), (0, 2), (3, 2), (-3, 0), (1, 3), (-3, 0), (4, 2), (-3, 0), (-3, 0), (5, 2), (-3, 0), (-3, 0), (7, 2), (-3, 0), (-3, 0), (3, 3), (-3, 0), (6, 2), (2, 3), (-3, 0), (4, 3), (0, 3), (5, 3), (7, 3), (6, 3)], (1, 2, 3, 4, 0))
@@ -522,14 +523,64 @@
     )
 
 
+def take(refs, *sizes):
+    groups, at = [], 0
+    for size in sizes:
+        groups.append(refs[at : at + size])
+        at += size
+    return groups + [refs[at:]]
+
+
+def row_exchange(me, mine, row_bits, rows, got, send_sem, recv_sem):
+    bits = len(row_bits)
+    flight = {}
+
+    def send(s):
+        bit = row_bits[s]
+        index = tuple(1 - mine[q] if q == bit else slice(None) for q in reversed(range(bits)))
+        copy = remote(me, rows.at[index], got[s], send_sem.at[s], recv_sem.at[s], bit)
+        copy.start()
+        flight[0] = copy
+
+    def receive(s):
+        flight[0].wait_send()
+        flight[0].wait_recv()
+
+        @pl.loop(0, 1 << (bits - 1))
+        def _(j):
+            here, there, pos = [], [], bits - 1
+            for q in reversed(range(bits)):
+                if q == row_bits[s]:
+                    here.append(1 - mine[q])
+                else:
+                    pos -= 1
+                    value = (j // (1 << pos)) % 2
+                    here.append(value)
+                    there.append(value)
+            rows[tuple(here)] = got[s][tuple(there)]
+
+        if s + 1 < bits:
+            send(s + 1)
+
+    return send, receive
+
+
 def gather_kernel(devices, chunks, events, layers, arrays, *refs):
     bits = devices.bit_length() - 1
-    ins = refs[:arrays]
-    outs = refs[arrays : arrays + layers * arrays]
-    send_sem, recv_sem, csend_sem, crecv_sem, own_sem = refs[arrays + layers * arrays :]
+    ins, rows_in, outs, rows_out, rows_got, sems = take(
+        refs, arrays, 1, layers * arrays, 1, bits
+    )
+    send_sem, recv_sem, csend_sem, crecv_sem, own_sem, ro_s, ro_r = sems
     me = lax.axis_index("dp")
     mine = [(me // (1 << b)) % 2 for b in range(bits)]
     greet(me, bits)
+    rows_send, rows_receive = row_exchange(
+        me, mine, AG_ROW_BITS, rows_out[0], rows_got, ro_s, ro_r
+    )
+    fetch = pltpu.make_async_copy(rows_in[0], rows_out[0], ro_s.at[0])
+    fetch.start()
+    fetch.wait()
+    rows_send(0)
     own, sends, cores, pending = [], [], [], {}
     for c, (l, a, order) in enumerate(chunks):
         here = outs[l * arrays + a].at[place(bits, (), mine)]
@@ -550,6 +601,9 @@
     for local in own:
         local.wait()
     for c, s in events:
+        if c == -2:
+            rows_receive(s)
+            continue
         l, a, order = chunks[c]
         full = outs[l * arrays + a]
         pending[c].wait_recv()
@@ -572,8 +626,9 @@
         copy.wait_recv()
 
 
-def gather_all(shards, devices):
+def gather_all(shards, rows, devices):
     bits = devices.bit_length() - 1
+    moved = rows.reshape((2,) * bits + (rows.shape[0] // devices, rows.shape[1]))
     layers = shards[0].shape[0]
     n = len(AG_CHUNKS)
     sent = {(layer, a) for layer, a, _ in AG_CHUNKS}
@@ -584,30 +639,27 @@
         for layer in range(layers)
         for a, s in enumerate(shards)
     ]
-    res = pl.pallas_call(
+    anywhere = pl.BlockSpec(memory_space=pl.ANY)
+    dma = pltpu.SemaphoreType.DMA
+    *res, arrived = pl.pallas_call(
         functools.partial(gather_kernel, devices, AG_CHUNKS, AG_EVENTS, layers, len(shards)),
-        out_shape=outs,
-        in_specs=[pl.BlockSpec(memory_space=pltpu.VMEM)] * len(shards),
-        out_specs=[pl.BlockSpec(memory_space=pl.ANY)] * len(outs),
-        scratch_shapes=[pltpu.SemaphoreType.DMA((n, bits - 1))] * 2
-        + [pltpu.SemaphoreType.DMA((n, bits))] * 2
-        + [pltpu.SemaphoreType.DMA((n,))],
+        out_shape=outs + [jax.ShapeDtypeStruct(moved.shape, BF16)],
+        in_specs=[VMEM] * len(shards) + [anywhere],
+        out_specs=[anywhere] * len(outs) + [VMEM],
+        scratch_shapes=[pltpu.VMEM(moved.shape[1:], BF16)] * bits
+        + [dma((n, bits - 1))] * 2
+        + [dma((n, bits))] * 2
+        + [dma((n,))]
+        + [dma((bits,))] * 2,
         compiler_params=pltpu.CompilerParams(collective_id=0, has_side_effects=True),
         name="gather_all",
-    )(*shards)
+    )(*shards, moved)
     full = [r.reshape((devices * r.shape[-2], r.shape[-1])) for r in res]
-    return [full[l * len(shards) : (l + 1) * len(shards)] for l in range(layers)]
+    weights = [full[l * len(shards) : (l + 1) * len(shards)] for l in range(layers)]
+    return weights, arrived.reshape(rows.shape)
 
 
 PAIRS = ((0, 0), (1, 2), (0, 1), (2, 2), (3, 3), (4, 4))
-
-
-def take(refs, *sizes):
-    groups, at = [], 0
-    for size in sizes:
-        groups.append(refs[at : at + size])
-        at += size
-    return groups + [refs[at:]]
 
 
 def scatter_kernel(devices, plan, jobs, arrs, counts, *refs):
@@ -658,32 +710,10 @@
         else:
             small_out[0][...] = total
 
-    def rows_send(s):
-        bit = row_bits[s]
-        index = tuple(1 - mine[q] if q == bit else slice(None) for q in reversed(range(bits)))
-        copy = remote(me, rows_out[0].at[index], rows_got[s], ro_s.at[s], ro_r.at[s], bit)
-        copy.start()
-        pending["rows"] = copy
-
-    def rows_receive(s):
-        pending["rows"].wait_send()
-        pending["rows"].wait_recv()
-
-        @pl.loop(0, 1 << (bits - 1))
-        def _(j):
-            here, there, pos = [], [], bits - 1
-            for q in reversed(range(bits)):
-                if q == row_bits[s]:
-                    here.append(1 - mine[q])
-                else:
-                    pos -= 1
-                    value = (j // (1 << pos)) % 2
-                    here.append(value)
-                    there.append(value)
-            rows_out[0][tuple(here)] = rows_got[s][tuple(there)]
-
-        if s + 1 < bits:
-            rows_send(s + 1)
+    if nrows:
+        rows_send, rows_receive = row_exchange(
+            me, mine, row_bits, rows_out[0], rows_got, ro_s, ro_r
+        )
 
     def send(c, s):
         order = chunks[c][3]
@@ -959,14 +989,40 @@
     same = (own[:, None] == own[None, :]) & (index[None, :] < index[:, None])
     slot = own * share + jnp.sum(same.astype(jnp.int32), axis=1)
     leave = (slot[None, :] == index[:, None]).astype(BF16)
-    outgoing = [dot(leave, x).astype(BF16) for x in (tokens, cotangent)]
 
     def exchange(rows):
         split = rows.reshape(devices, share, width)
         moved = lax.all_to_all(split, "dp", split_axis=0, concat_axis=0, tiled=True)
         return moved.reshape(rows_here, width)
 
-    arrived = [exchange(x) for x in outgoing]
+    outgoing = dot(leave, tokens).astype(BF16)
+    matrices = (in_proj, mixer_out, qkv_proj, attn_out, gate_up, down_proj)
+    gain_part, conv_part, inner_part = (x.shape[-1] for x in (norm_gains, conv_weight, ssm_gain))
+    packed = jnp.concatenate(
+        [norm_gains.reshape(LAYERS, -1), conv_weight.reshape(LAYERS, -1), ssm_gain], axis=1
+    )
+    used = packed.shape[1]
+    if own_kernels:
+        room = SMALL_ROWS * 128
+        padded = jnp.pad(packed, ((0, 0), (0, room - used))).reshape(LAYERS, SMALL_ROWS, 128)
+        gathered, arrived = gather_all(list(matrices) + [padded], outgoing, devices)
+        weights = [g[:-1] for g in gathered]
+        after = gathered[0][-1][:1, :1] * 0
+        weights[1][LATE_ARRAY] = lax.all_gather(
+            matrices[LATE_ARRAY][1] + after, "dp", axis=0, tiled=True
+        )
+        smalls = [g[-1].reshape(devices, room)[:, :used] for g in gathered]
+        late_cotangent = cotangent + after
+    else:
+        arrived = exchange(outgoing)
+        weights = [
+            [lax.all_gather(x[layer], "dp", axis=0, tiled=True) for x in matrices]
+            for layer in range(LAYERS)
+        ]
+        every = lax.all_gather(packed, "dp", axis=0)
+        smalls = [every[:, layer] for layer in range(LAYERS)]
+        late_cotangent = cotangent
+    arrived_cotangent = exchange(dot(leave, late_cotangent).astype(BF16))
 
     local = slabs - me * rows_here
     mask = ((local >= 0) & (local < rows_here)).astype(BF16)
@@ -976,8 +1032,8 @@
     hits = local.reshape(-1)[None, :] == index[:, None]
     taken = jnp.sum(jnp.where(hits, order.reshape(-1)[None, :], 0), axis=1)
     enter = (taken[:, None] == index[None, :]).astype(BF16)
-    hidden = dot(enter, arrived[0])
-    upstream = dot(enter, arrived[1])
+    hidden = dot(enter, arrived)
+    upstream = dot(enter, arrived_cotangent)
 
     segment, position = doc_layout(lengths[0], rows_here)
     inside = (segment[:, None] == segment[None, :]) & (index[:, None] >= index[None, :])
@@ -985,29 +1041,6 @@
     angles = position.astype(F32)[:, None] * inverse[None, :]
     outside = jnp.where(inside.T, 0.0, -1e30)
     layout = (position[:, None], inside.astype(F32), outside, jnp.cos(angles).T, jnp.sin(angles).T)
-
-    matrices = (in_proj, mixer_out, qkv_proj, attn_out, gate_up, down_proj)
-    gain_part, conv_part, inner_part = (x.shape[-1] for x in (norm_gains, conv_weight, ssm_gain))
-    packed = jnp.concatenate(
-        [norm_gains.reshape(LAYERS, -1), conv_weight.reshape(LAYERS, -1), ssm_gain], axis=1
-    )
-    used = packed.shape[1]
-    if own_kernels:
-        room = SMALL_ROWS * 128
-        padded = jnp.pad(packed, ((0, 0), (0, room - used))).reshape(LAYERS, SMALL_ROWS, 128)
-        gathered = gather_all(list(matrices) + [padded], devices)
-        weights = [g[:-1] for g in gathered]
-        late = LATE_ARRAY
-        tied = matrices[late][1] + gathered[0][-1][:1, :1] * 0
-        weights[1][late] = lax.all_gather(tied, "dp", axis=0, tiled=True)
-        smalls = [g[-1].reshape(devices, room)[:, :used] for g in gathered]
-    else:
-        weights = [
-            [lax.all_gather(x[layer], "dp", axis=0, tiled=True) for x in matrices]
-            for layer in range(LAYERS)
-        ]
-        every = lax.all_gather(packed, "dp", axis=0)
-        smalls = [every[:, layer] for layer in range(LAYERS)]
 
     def spread(piece, count):
         shaped = piece.reshape(devices, count, -1)

time: 660 us -> 655 us (level)
  waiting for transfers between devices: 8.18 us -> 0.02 us
    all_to_all x2 -> x1, waiting for transfers between devices: 8.17 us -> 0.01 us  [exchange(): moved = lax.all_to_all(split, 'dp', split_axis=0, concat_axis=0, tiled=True)]
  transfers between devices with their start and end apart: 3 -> 2, of which waited for: 1 -> 0; matrix products, arithmetic and copies ran while one was open for 7% -> 8% of each run, Pallas kernels for 5% -> 5%
where the time goes in v6:
time: 655 us; the launch traced here: 652 us
  Pallas kernels  493 us (75%)
  matrix products  83.1 us (13%)
  other arithmetic  28 us (4%)
  local copies, waits for them, and re-layouts  27.7 us (4%)
  between operations  16.1 us (2%)
    pallas_call x3, Pallas kernels, scatter(): pl.pallas_call(functools.partial(scatter_kernel, devices, plan, jobs, arr...  273 us
    pallas_call x1, Pallas kernels, gather_all(): pl.pallas_call(functools.partial(gather_kernel, devices, AG_CHUNKS, AG_EV...  188 us
    dot_general x14, matrix products, dot(): return jnp.dot(left, right, preferred_element_type=F32)  39.5 us
    dot_general x12, matrix products, dot_rt(): lax.dot_general(left, right, (((1,), (1,)), ((), ())), preferred_element_...  31.1 us
    pallas_call x2, Pallas kernels, mixer_forward(): pl.pallas_call(mixer_forward_kernel, out_shape=[shape((rows, INNER), BF16...  23.3 us
  transfers between devices with their start and end apart: 2, of which 0 were waited for; matrix products, arithmetic and copies ran while one was open for 8% of the time, Pallas kernels for 5%

profile of v6, /device:TPU:0, one launch (start us, length us, event | category | flops | bytes accessed | tf_op | source)
XLA Modules:
  0.0 651.8 jit_solution(11728531254900485026)
XLA Ops:
  11.2 2.1 convolution_convert_fusion.4
  13.4 187.7 %gather_all.1 = (bf16[2,2,2,2,2,32,3352]{6,5,4,3,2,1,0:T(8,128)(2,1)}, bf16[2,2,2,2,2,48,1024]{6,5,4,3,2,1,0:T(8,128)(2,1)}, bf16[2,2,2,2,2,32,768]{6,5,4,3,2,1,...) custom-call(bf16[2,32,3352]{2,1,0:T(8,128)(2,1)} %refs_0_.1, ...), custom_call_target="tpu_custom_call" | custom-call | tf_op jit(solution)/shard_map/gather_all/pallas_call | solution.py:644
  204.9 3.8 all-to-all-start
  218.4 1.6 fusion.63.packed_ref.refs_21_
  220.0 4.7 attention_forward.2
  226.8 7.0 %fusion.62.inner_ref.refs_12_ = f32[256,3352]{1,0:T(8,128)} fusion(bf16[1024,3352]{1,0:T(8,128)(2,1)} %bitcast.174, f32[256,1024]{1,0:T(8,128)S(1)} %get-tuple-element.165, f32[1024]{0:T(1024)S(1)} %mul.344, f32[256]{0:T(256)S(1)} %add_rsqrt_fusion.3), kind=kOutput, calls=%fused_computation.197 | convolution fusion | flops 1758199808 | bytes 11351040 | tf_op jit(solution)/shard_map/dot_general | solution.py:41
  233.8 11.6 %mixer_forward.2 = (bf16[256,1536]{1,0:T(8,128)(2,1)}, bf16[1536,256]{1,0:T(8,128)(2,1)}, f32[256,1536]{1,0:T(8,128)}) custom-call(f32[256,3352]{1,0:T(8,128)} %fusion.62.inner_ref.refs_12_, f32[4,1792]{1,0:T(4,128)} %reshape.396.taps_ref.refs_13_, f32[8,128]{1,0:T(8,128)} %select_maximum_fusion.2.heads_ref.refs_14_, ...), custom_call_target="tpu_custom_call" | custom-call | tf_op jit(solution)/shard_map/mixer_forward/pallas_call | solution.py:199
  245.5 2.2 convolution_add_fusion.5
  248.3 6.2 fusion.53
  257.1 1.6 fusion.65.packed_ref.refs_13_
  258.7 4.7 attention_forward.3
  264.7 2.8 fusion.117
  270.0 7.1 %fusion.64.inner_ref.refs_4_ = f32[256,3352]{1,0:T(8,128)} fusion(bf16[1024,3352]{1,0:T(8,128)(2,1)} %bitcast.176, f32[256,1024]{1,0:T(8,128)S(1)} %get-tuple-element.169, f32[1024]{0:T(1024)S(1)} %mul.365, f32[256]{0:T(256)S(1)} %add_rsqrt_fusion.1), kind=kOutput, calls=%fused_computation.199 | convolution fusion | flops 1758199808 | bytes 11351040 | tf_op jit(solution)/shard_map/dot_general | solution.py:41
  277.7 11.7 %mixer_forward.3 = (bf16[256,1536]{1,0:T(8,128)(2,1)}, bf16[1536,256]{1,0:T(8,128)(2,1)}, f32[256,1536]{1,0:T(8,128)}) custom-call(f32[256,3352]{1,0:T(8,128)} %fusion.64.inner_ref.refs_4_, f32[4,1792]{1,0:T(4,128)} %reshape.398.taps_ref.refs_5_, f32[8,128]{1,0:T(8,128)} %select_maximum_fusion.heads_ref.refs_6_, ...), custom_call_target="tpu_custom_call" | custom-call | tf_op jit(solution)/shard_map/mixer_forward/pallas_call | solution.py:199
  289.5 2.2 convolution_add_fusion.4
  292.3 2.5 fusion.61
  294.8 5.9 fusion.2
  300.8 3.0 multiply_convert_fusion.3
  303.8 3.1 multiply_reduce_fusion.4
  309.6 2.2 fusion.66.refs_12_
  315.7 69.1 %scatter.3 = (f32[32,4096]{1,0:T(8,128)}, f32[64,1024]{1,0:T(8,128)}, bf16[256,3352]{1,0:T(8,128)(2,1)}, f32[4,1792]{1,0:T(4,128)}, f32[1,1536]{1,0:T(1,128)}, /...) custom-call(bf16[16,2,32,256]{3,2,1,0:T(8,128)(2,1)} %bitcast.190, ...), custom_call_target="tpu_custom_call" | custom-call | tf_op jit(solution)/shard_map/scatter/pallas_call | solution.py:858
  384.8 5.8 fusion.67
  393.1 1.7 copy-done.5
  394.8 2.0 multiply_convert_fusion.1
  397.5 3.1 multiply_reduce_fusion.1
  403.4 2.2 fusion.68.refs_20_
  405.5 4.4 convolution_convert_fusion.2
  410.0 3.1 pad_maximum_fusion.1.refs_8_
  415.9 128.6 %scatter.4 = (f32[32,3352]{1,0:T(8,128)}, f32[48,1024]{1,0:T(8,128)}, f32[32,768]{1,0:T(8,128)}, f32[16,1024]{1,0:T(8,128)}, f32[32,4096]{1,0:T(8,128)}, /*index...) custom-call(bf16[16,2,32,256]{3,2,1,0:T(8,128)(2,1)} %bitcast.188, ...), custom_call_target="tpu_custom_call" | custom-call | tf_op jit(solution)/shard_map/scatter/pallas_call | solution.py:858
  544.5 5.8 fusion.69
  554.4 75.1 %scatter.5 = (f32[32,3352]{1,0:T(8,128)}, f32[48,1024]{1,0:T(8,128)}, f32[32,768]{1,0:T(8,128)}, f32[16,1024]{1,0:T(8,128)}, f32[88,128]{1,0:T(8,128)}, /*index=5*/bf16[2,2,2,2,2,8,1024]{6,5,4,3,2,1,0:T(8,128)(2,1)}) custom-call(bf16[16,2,32,256]{3,2,1,0:T(8,128)(2,1)} %bitcast.192, bf16[16,2,48,256]{3,2,1,0:T(8,128)(2,1)} %bitcast.196, ...), custom_call_target="tpu_custom_call" | custom-call | tf_op jit(solution)/shard_map/scatter/pallas_call | solution.py:858
  634.2 2.4 fusion.18
  (306 shorter events, 58.7 us)
Async XLA Ops:
  7.2 195.8 %copy-start.30 = (bf16[2,32,4096]{2,1,0:T(8,128)(2,1)S(1)}, bf16[2,32,4096]{2,1,0:T(8,128)(2,1)}, u32[]{:S(2)}) copy-start(bf16[2,32,4096]{2,1,0:T(8,128)(2,1)} %refs_4_.1) | copy-start | bytes 1572868
  7.2 196.6 %copy-start.36 = (bf16[256,1024]{1,0:T(8,128)(2,1)S(1)}, bf16[256,1024]{1,0:T(8,128)(2,1)}, u32[]{:S(2)}) copy-start(bf16[256,1024]{1,0:T(8,128)(2,1)} %param.17) | copy-start | bytes 1572868
  7.2 287.6 %all-gather.3.cloned.1.call-start = ((), (), s32[]{:S(2)}) async-start(), calls=%async_computation.1 | async-start | bytes 8650752 | tf_op jit(solution)/shard_map/all_gather | solution.py:1011
  8.3 196.5 %copy-start.67 = (s32[1,256]{1,0:T(1,128)}, s32[1,256]{1,0:T(1,128)S(1)}, u32[]{:S(2)}) copy-start(s32[1,256]{1,0:T(1,128)S(1)} %multiply_add_fusion.3) | copy-start | bytes 3076
  201.0 7.6 %copy-start.55 = (bf16[2,2,2,2,2,16,128]{6,5,4,3,2,1,0:T(8,128)(2,1)S(1)}, bf16[2,2,2,2,2,16,128]{6,5,4,3,2,1,0:T(8,128)(2,1)}, u32[]{:S(2)}) copy-start(bf16[2,2,2,2,2,16,128]{6,5,4,3,2,1,0:T(8,128)(2,1)} %get-tuple-element.67) | copy-start | bytes 393220
  201.0 7.8 %copy-start.54 = (bf16[2,2,2,2,2,16,128]{6,5,4,3,2,1,0:T(8,128)(2,1)S(1)}, bf16[2,2,2,2,2,16,128]{6,5,4,3,2,1,0:T(8,128)(2,1)}, u32[]{:S(2)}) copy-start(bf16[2,2,2,2,2,16,128]{6,5,4,3,2,1,0:T(8,128)(2,1)} %get-tuple-element.76) | copy-start | bytes 393220
  201.0 8.4 %copy-start.83 = (s32[1,4]{1,0:T(1,128)S(1)}, s32[1,4]{1,0:T(1,128)}, u32[]{:S(2)}) copy-start(s32[1,4]{1,0:T(1,128)} %param.19) | copy-start | bytes 52
  203.0 8.3 %copy-start.80 = (f32[2,24]{1,0:T(2,128)S(1)}, f32[2,24]{1,0:T(2,128)}, u32[]{:S(2)}) copy-start(f32[2,24]{1,0:T(2,128)} %param.30) | copy-start | bytes 580
  203.0 8.3 %copy-start.81 = (f32[2,24]{1,0:T(2,128)S(1)}, f32[2,24]{1,0:T(2,128)}, u32[]{:S(2)}) copy-start(f32[2,24]{1,0:T(2,128)} %param.29) | copy-start | bytes 580
  203.7 11.1 %copy-start.56 = (s32[8192]{0:T(1024)S(1)}, s32[8192]{0:T(1024)}, u32[]{:S(2)}) copy-start(s32[8192]{0:T(1024)} %param.18) | copy-start | bytes 98308
  203.8 12.4 %copy-start.37 = (bf16[2,2,2,2,2,8,1024]{6,5,4,3,2,1,0:T(8,128)(2,1)S(1)}, bf16[2,2,2,2,2,8,1024]{6,5,4,3,2,1,0:T(8,128)(2,1)}, u32[]{:S(2)}) copy-start(bf16[2,2,2,2,2,8,1024]{6,5,4,3,2,1,0:T(8,128)(2,1)} %get-tuple-element.66) | copy-start | bytes 1572868
  204.9 87.4 %all-to-all-start = ((bf16[32,8,1024]{2,1,0:T(8,128)(2,1)}), bf16[32,8,1024]{2,1,0:T(8,128)(2,1)}, u32[]{:S(2)}, u32[]{:S(2)}) async-start(bf16[32,8,1024]{2,1,0:T(8,128)(2,1)} %fusion.7), calls=%async_computation | async-start | bytes 1048576 | tf_op jit(solution)/shard_map/all_to_all | solution.py:995
  208.7 9.8 %copy-start.16 = (bf16[2,2,2,2,2,32,768]{6,5,4,3,2,1,0:T(8,128)(2,1)S(1)}, bf16[2,2,2,2,2,32,768]{6,5,4,3,2,1,0:T(8,128)(2,1)}, u32[]{:S(2)}) copy-start(bf16[2,2,2,2,2,32,768]{6,5,4,3,2,1,0:T(8,128)(2,1)} %get-tuple-element.71) | copy-start | bytes 4718596
  209.2 59.6 %copy-start.42 = (f32[1024]{0:T(1024)}, f32[1024]{0:T(1024)S(1)}, u32[]{:S(2)}) copy-start(f32[1024]{0:T(1024)S(1)} %mul.344) | copy-start | bytes 12292
  212.3 35.9 %copy-start.52 = (f32[1024]{0:T(1024)}, f32[1024]{0:T(1024)S(1)}, u32[]{:S(2)}) copy-start(f32[1024]{0:T(1024)S(1)} %mul.356) | copy-start | bytes 12292
  212.4 57.6 %copy-start.44 = (f32[1024]{0:T(1024)}, f32[1024]{0:T(1024)S(1)}, u32[]{:S(2)}) copy-start(f32[1024]{0:T(1024)S(1)} %mul.365) | copy-start | bytes 12292
  216.2 76.1 %copy-start.69 = (s32[256]{0:T(256)}, s32[256]{0:T(256)S(1)}, u32[]{:S(2)}) copy-start(s32[256]{0:T(256)S(1)} %select_reduce_fusion) | copy-start | bytes 3076
  216.6 52.2 %copy-start = (f32[256,1024]{1,0:T(8,128)}, f32[256,1024]{1,0:T(8,128)S(1)}, u32[]{:S(2)}) copy-start(f32[256,1024]{1,0:T(8,128)S(1)} %get-tuple-element.165) | copy-start | bytes 3145732
  216.7 52.2 %copy-start.61 = (f32[256]{0:T(256)}, f32[256]{0:T(256)S(1)}, u32[]{:S(2)}) copy-start(f32[256]{0:T(256)S(1)} %add_rsqrt_fusion.3) | copy-start | bytes 3076
  218.4 6.3 copy-start.82
  233.8 11.6 %copy-start.6 = (bf16[2,2,2,2,2,48,1024]{6,5,4,3,2,1,0:T(8,128)(2,1)S(1)}, bf16[2,2,2,2,2,48,1024]{6,5,4,3,2,1,0:T(8,128)(2,1)}, u32[]{:S(2)}) copy-start(bf16[2,2,2,2,2,48,1024]{6,5,4,3,2,1,0:T(8,128)(2,1)} %get-tuple-element.70) | copy-start | bytes 9437188
  256.5 32.9 %copy-start.2 = (f32[256,1024]{1,0:T(8,128)}, f32[256,1024]{1,0:T(8,128)S(1)}, u32[]{:S(2)}) copy-start(f32[256,1024]{1,0:T(8,128)S(1)} %get-tuple-element.169) | copy-start | bytes 3145732
  256.5 13.5 %copy-start.63 = (f32[256]{0:T(256)}, f32[256]{0:T(256)S(1)}, u32[]{:S(2)}) copy-start(f32[256]{0:T(256)S(1)} %add_rsqrt_fusion.1) | copy-start | bytes 3076
  277.1 12.3 %copy-start.8 = (bf16[2,2,2,2,2,48,1024]{6,5,4,3,2,1,0:T(8,128)(2,1)S(1)}, bf16[2,2,2,2,2,48,1024]{6,5,4,3,2,1,0:T(8,128)(2,1)}, u32[]{:S(2)}) copy-start(bf16[2,2,2,2,2,48,1024]{6,5,4,3,2,1,0:T(8,128)(2,1)} %get-tuple-element.82) | copy-start | bytes 9437188
  292.2 14.7 %copy-start.12 = (f32[256,1024]{1,0:T(8,128)}, f32[256,1024]{1,0:T(8,128)S(1)}, u32[]{:S(2)}) copy-start(f32[256,1024]{1,0:T(8,128)S(1)} %get-tuple-element.173) | copy-start | bytes 3145732
  294.8 9.0 %slice-start.2 = ((s8[8388608]{0:T(1024)(128)(4,1)}), s8[4194304]{0:T(1024)(128)(4,1)S(1)}, s32[]{:S(2)}) async-start(s8[8388608]{0:T(1024)(128)(4,1)} %bitcast.168), calls=%async_computation.4 | async-start | bytes 8388608
  629.5 7.1 %copy-start.35 = (bf16[2,2,2,2,2,8,1024]{6,5,4,3,2,1,0:T(8,128)(2,1)S(1)}, bf16[2,2,2,2,2,8,1024]{6,5,4,3,2,1,0:T(8,128)(2,1)}, u32[]{:S(2)}) copy-start(bf16[2,2,2,2,2,8,1024]{6,5,4,3,2,1,0:T(8,128)(2,1)} %get-tuple-element.94) | copy-start | bytes 1572868
  629.5 7.1 %copy-start.68 = (s32[1,256]{1,0:T(1,128)S(1)}, s32[1,256]{1,0:T(1,128)}, u32[]{:S(2)}) copy-start(s32[1,256]{1,0:T(1,128)} %copy-done.67) | copy-start | bytes 3076
  629.5 8.3 %copy-start.48 = (f32[64,1024]{1,0:T(8,128)S(1)}, f32[64,1024]{1,0:T(8,128)}, u32[]{:S(2)}) copy-start(f32[64,1024]{1,0:T(8,128)} %get-tuple-element.117) | copy-start | bytes 786436
  629.5 8.3 %copy-start.49 = (f32[64,1024]{1,0:T(8,128)S(1)}, f32[64,1024]{1,0:T(8,128)}, u32[]{:S(2)}) copy-start(f32[64,1024]{1,0:T(8,128)} %get-tuple-element.116) | copy-start | bytes 786436
  631.7 6.9 %copy-start.38 = (f32[32,4096]{1,0:T(8,128)S(1)}, f32[32,4096]{1,0:T(8,128)}, u32[]{:S(2)}) copy-start(f32[32,4096]{1,0:T(8,128)} %get-tuple-element.115) | copy-start | bytes 1572868
  631.7 6.9 %copy-start.39 = (f32[32,4096]{1,0:T(8,128)S(1)}, f32[32,4096]{1,0:T(8,128)}, u32[]{:S(2)}) copy-start(f32[32,4096]{1,0:T(8,128)} %get-tuple-element.114) | copy-start | bytes 1572868
  (61 other events, 213.1 us)
Sparse Core Ops, SparseCore 0:
  203.9 79.0 all-gather.2
